TPU v7x, 128 devices: a whole 4x4x4 slice. The times are simulated.
128 devices in a mesh: row: 8 (over z, core), col: 16 (over y, x).
Axes of the slice: x: 4, y: 4, z: 4, core: 2. Of those that a mesh axis runs over, the one named last changes fastest.
Arguments:
- load_amp: float32 [4096, 8192], P('row', 'col'), may hold values from 0.05 to 1
- load_mask: int32 [4096, 8192], P('row', 'col'), may hold values 0 or 1
- leak: float32 [4096, 8192], P('row', 'col'), may hold values from 0.001 to 0.05
- coarse_leak: float32 [1024, 2048], P('row', 'col'), may hold values from 0.01 to 0.5
- coarse_init: float32 [1024, 2048], P('row', 'col'), may hold values from 0 to 1
- via_fine: int32 [8, 32768], P('row', 'col'), may hold values from 0 to 262143
- via_coarse: int32 [8, 32768], P('row', 'col'), may hold values from 0 to 262143, as said below
- via_count: int32 [8, 256], P('row', 'col'), may hold values from 0 to 128, as said below
Outputs:
- fine_drop: float32 [4096, 8192], P('row', 'col')
- coarse_drop: float32 [1024, 2048], P('row', 'col')
Inputs may be any that keep to these rules, and one draw needn't show every extreme that they name: `via_coarse`: slot s of a tile names a coarse node whose stored column lies in s // 128 * 128 to s // 128 * 128 + 127. `via_count`: slots of an owner past its count are padding and carry arbitrary indices. In each tile row some owner gets 128 live slots from every tile of that row.
All inputs are finite; a program needn't handle non-finite values. No bound on the sum of `load_mask` on one device may be relied on, other than what follows from the above.
Results may differ from a plain program's by a relative error of at most 0.00022.
Values sent between devices are 32-bit elements; how exact they have to be, the bound alone decides.
No kernel may reach another device: no remote copies, remote signals or barrier semaphores. Data moves between devices by JAX's collectives and lax.ppermute only.
A program may use at most 64 MiB of HBM per device.

v0:
```python
import functools

import jax
import jax.numpy as jnp
from jax import lax
from jax.sharding import Mesh
from jax.sharding import PartitionSpec as P

GROUP = 16
ITERS = 4
CSWEEP = 2
ROW_COL = ("row_0", "row_1", "col_0", "col_1")
ROW = ("row_0", "row_1")
COL = ("col_0", "col_1")


via_conductance = 2.0
coarse_conductance = 4.0
relaxation = 0.8


def padded_2(shard, sides, width):
    edges = {}
    for axis, dim in sides:
        size, length = (lax.axis_size(axis), shard.shape[dim])
        up = [(i, (i + 1) % size) for i in range(size - 1)]
        last = lax.slice_in_dim(shard, length - width, length, axis=dim)
        leading = lax.slice_in_dim(shard, 0, width, axis=dim)
        edges[dim] = (
            lax.ppermute(last, axis, up),
            lax.ppermute(leading, axis, [(b, a) for a, b in up]),
        )
    done = []
    for _, dim in sides:
        low, high = edges[dim]
        around = [(width, width) if d in done else (0, 0) for d in range(shard.ndim)]
        shard = jnp.concatenate([jnp.pad(low, around), shard, jnp.pad(high, around)], axis=dim)
        done.append(dim)
    return shard


def extended(block, sides, width, periodic):
    for axis, dim in sides:
        count = lax.axis_size(axis)
        forward = [(i, i + 1) for i in range(count - 1)]
        if periodic:
            forward.append((count - 1, 0))
        backward = [(target, source) for source, target in forward]
        low = lax.ppermute(
            lax.slice_in_dim(block, block.shape[dim] - width, None, axis=dim), axis, forward
        )
        high = lax.ppermute(lax.slice_in_dim(block, 0, width, axis=dim), axis, backward)
        block = jnp.concatenate([low, block, high], axis=dim)
    return block


def one_axis_at_a_time(shard, axes):
    return functools.reduce(lax.psum, axes, shard)


def fine_apply(field, diagonal):
    padded = padded_2(field, ((ROW, 0), (COL, 1)), 1)
    beside = padded[2:, 1:-1] + padded[:-2, 1:-1] + padded[1:-1, 2:] + padded[1:-1, :-2]
    return diagonal * field - beside


def coarse_apply(volt, diagonal):
    block_rows, block_cols = volt.shape
    groups = block_cols // GROUP
    stacked = extended(volt, ((ROW, 0),), 1, False)
    up_down = stacked[2:] + stacked[:-2]
    grouped = volt.reshape(block_rows, groups, GROUP)
    seam = jnp.stack([grouped[:, :, 0], grouped[:, :, GROUP - 1]], axis=0)
    edges = extended(seam, ((COL, 0),), 1, True)
    from_left = edges[0]
    from_right = edges[3]
    place = lax.axis_index(COL)
    width = lax.axis_size(COL)
    zero_col = jnp.zeros((block_rows, 1), jnp.float32)
    left_turned = jnp.concatenate([zero_col, from_left[:, :-1]], axis=1)
    from_left = jnp.where(place == 0, left_turned, from_left)
    right_turned = jnp.concatenate([from_right[:, 1:], zero_col], axis=1)
    from_right = jnp.where(place == width - 1, right_turned, from_right)
    left_full = jnp.concatenate([from_left[:, :, None], grouped[:, :, :-1]], axis=2).reshape(
        block_rows, block_cols
    )
    right_full = jnp.concatenate([grouped[:, :, 1:], from_right[:, :, None]], axis=2).reshape(
        block_rows, block_cols
    )
    return diagonal * volt - coarse_conductance * (up_down + left_full + right_full)


def paired_sum(first, second):
    return (
        one_axis_at_a_time(jnp.sum(first), ROW_COL),
        one_axis_at_a_time(jnp.sum(second), ROW_COL),
    )


def per_device(
    load_amp, load_mask, leak, coarse_leak, coarse_init, via_fine, via_coarse, via_count
):
    tile_rows, tile_cols = leak.shape
    block_rows, block_cols = coarse_leak.shape
    owners = lax.axis_size(COL)
    slot_count = via_fine.shape[1]
    per_owner = slot_count // owners
    row_width = block_cols * owners
    slot_all = jnp.arange(slot_count, dtype=jnp.int32)
    position = slot_all % per_owner
    live = position < jnp.repeat(via_count[0], per_owner)
    weight = jnp.where(live, via_conductance, 0.0).astype(jnp.float32)
    fine_index = via_fine[0]
    coarse_index = via_coarse[0]
    via_diag = jnp.zeros(tile_rows * tile_cols, jnp.float32).at[fine_index].add(weight)
    fine_diag = 4.0 + leak + via_diag.reshape(tile_rows, tile_cols)
    local_index = coarse_index // row_width * block_cols + coarse_index % row_width % block_cols
    request = jnp.where(live, local_index, -1).reshape(owners, per_owner)
    held = lax.all_to_all(request, COL, split_axis=0, concat_axis=0, tiled=True)
    held_valid = (held >= 0).reshape(-1)
    held_flat = jnp.where(held_valid, held.reshape(-1), 0)
    held_weight = jnp.where(held_valid, via_conductance, 0.0).astype(jnp.float32)
    coarse_count = (
        jnp.zeros(block_rows * block_cols, jnp.float32)
        .at[held_flat]
        .add(held_weight)
        .reshape(block_rows, block_cols)
    )
    coarse_diag = 4.0 * coarse_conductance + coarse_leak + coarse_count
    load = load_amp * load_mask.astype(jnp.float32)
    volt = coarse_init
    solution = jnp.zeros((tile_rows, tile_cols), jnp.float32)
    looked = jnp.where(held_valid, volt.reshape(-1)[held_flat], 0.0).reshape(owners, per_owner)
    at_via = lax.all_to_all(looked, COL, split_axis=0, concat_axis=0, tiled=True).reshape(-1)
    injected = jnp.zeros(tile_rows * tile_cols, jnp.float32).at[fine_index].add(weight * at_via)
    rhs = load + injected.reshape(tile_rows, tile_cols)
    residual = rhs - fine_apply(solution, fine_diag)
    precond = residual / fine_diag
    image = fine_apply(precond, fine_diag)
    product, curvature = paired_sum(residual * precond, image * precond)
    alpha = product / curvature
    direction = precond
    along = image
    for iteration in range(ITERS):
        solution = solution + alpha * direction
        residual = residual - alpha * along
        if iteration + 1 < ITERS:
            precond = residual / fine_diag
            image = fine_apply(precond, fine_diag)
            renewed, curvature = paired_sum(residual * precond, image * precond)
            ratio = renewed / product
            alpha = renewed / (curvature - ratio * renewed / alpha)
            direction = precond + ratio * direction
            along = image + ratio * along
            product = renewed
    at_fine = weight * solution.reshape(-1)[fine_index]
    arrived = lax.all_to_all(
        at_fine.reshape(owners, per_owner), COL, split_axis=0, concat_axis=0, tiled=True
    )
    sources = (
        jnp.zeros(block_rows * block_cols, jnp.float32)
        .at[held_flat]
        .add(arrived.reshape(-1))
        .reshape(block_rows, block_cols)
    )
    for sweep_turn in range(CSWEEP):
        volt = volt + relaxation * (sources - coarse_apply(volt, coarse_diag)) / coarse_diag
    return (solution, volt)


def solution(mesh):
    split = Mesh(mesh.devices.reshape(4, 2, 4, 4), ("row_0", "row_1", "col_0", "col_1"))
    in_specs = (
        P(ROW, COL),
        P(ROW, COL),
        P(ROW, COL),
        P(ROW, COL),
        P(ROW, COL),
        P(ROW, COL),
        P(ROW, COL),
        P(ROW, COL),
    )
    out_specs = (P(ROW, COL), P(ROW, COL))
    return jax.shard_map(
        per_device, mesh=split, in_specs=in_specs, out_specs=out_specs, check_vma=False
    )
```

profile of v0, /device:TPU:1, one launch (start us, length us, event | category | flops | bytes accessed | tf_op | source)
XLA Modules:
  0.0 359.7 jit_solution(15064754172412893006)
XLA Ops:
  14.8 8.6 %all-to-all-start = ((s32[16,1,128]{2,1,0:T(1,128)}), s32[16,1,128]{2,1,0:T(1,128)S(1)}, u32[]{:S(2)}, u32[]{:S(2)}) async-start(s32[16,1,128]{2,1,0:T(1,128)} %compare_select_fusion.13), calls=%async_computation | async-start | bytes 16384 | tf_op jit(solution)/shard_map/all_to_all | solution.py:119
  30.4 11.8 %gather_fusion = f32[2048]{0:T(1024)S(1)} fusion(f32[16384]{0:T(1024)S(1)} %bitcast.77, s32[2048]{0:T(1024)S(1)} %broadcast_clamp_fusion.1), kind=kCustom, calls=%fused_computation | custom fusion | bytes 24576 | tf_op jit(solution)/shard_map/gather | solution.py:133
  52.7 11.5 %scatter_custom_fusion = f32[262144]{0:T(1024)S(1)} fusion(s32[2048]{0:T(1024)S(1)} %bitcast.92, f32[2048]{0:T(1024)S(1)} %get-tuple-element.87, f32[]{:T(128)} %constant.72.clone.1), kind=kCustom, calls=%fused_computation.96 | custom fusion | flops 2048 | bytes 1048580 | tf_op jit(solution)/shard_map/scatter-add | solution.py:135
  64.4 11.5 %scatter_custom_fusion.1 = f32[262144]{0:T(1024)S(1)} fusion(s32[2048]{0:T(1024)S(1)} %bitcast.93, f32[2048]{0:T(1024)S(1)} %get-tuple-element.86, f32[]{:T(128)} %constant.72.clone.1), kind=kCustom, calls=%fused_computation.94 | custom fusion | flops 2048 | bytes 1048580 | tf_op jit(solution)/shard_map/scatter-add | solution.py:115
  96.0 9.3 %all-reduce.27 = (f32[]{:T(128)}, f32[]{:T(128)}) all-reduce(f32[]{:T(128)} %get-tuple-element.11, f32[]{:T(128)} %get-tuple-element.10), channel_id=1, replica_groups=mesh['row_0'=4,'row_1'=2,'col_0'=4,'col_1'=4] {'row_0'}, use_global_device_ids=true, to_apply=%region_3.4 | all-reduce | flops 2 | bytes 16 | tf_op jit(solution)/shard_map/psum | solution.py:58
  105.3 6.7 %all-reduce.31 = (f32[]{:T(128)}, f32[]{:T(128)}) all-reduce(f32[]{:T(128)} %get-tuple-element.34, f32[]{:T(128)} %get-tuple-element.35), channel_id=1, replica_groups=mesh['row_0'=4,'row_1'=2,'col_0'=4,'col_1'=4] {'row_1'}, use_global_device_ids=true, to_apply=%region_4.5 | all-reduce | flops 2 | bytes 16 | tf_op jit(solution)/shard_map/psum | solution.py:58
  111.9 8.6 %all-reduce.23 = (f32[]{:T(128)}, f32[]{:T(128)}) all-reduce(f32[]{:T(128)} %get-tuple-element.42, f32[]{:T(128)} %get-tuple-element.43), channel_id=1, replica_groups=mesh['row_0'=4,'row_1'=2,'col_0'=4,'col_1'=4] {'col_0'}, use_global_device_ids=true, to_apply=%region_5.6 | all-reduce | flops 2 | bytes 16 | tf_op jit(solution)/shard_map/psum | solution.py:58
  120.5 8.0 %all-reduce.19 = (f32[]{:T(128)}, f32[]{:T(128)}) all-reduce(f32[]{:T(128)} %get-tuple-element.26, f32[]{:T(128)} %get-tuple-element.27), channel_id=1, replica_groups=mesh['row_0'=4,'row_1'=2,'col_0'=4,'col_1'=4] {'col_1'}, use_global_device_ids=true, to_apply=%region_6.7 | all-reduce | flops 2 | bytes 16 | tf_op jit(solution)/shard_map/psum | solution.py:58
  140.1 6.8 %collective-permute-start.8 = (f32[1,512]{1,0:T(1,128)}, f32[1,512]{1,0:T(1,128)}, u32[]{:S(2)}, u32[]{:S(2)}) collective-permute-start(f32[1,512]{1,0:T(1,128)} %get-tuple-element.67), channel_id=1, source_target_pairs={{16,0},{32,16},{48,32},{64,48},{80,64},{96,80},{112,96},{17,1},{33... | collective-permute-start | bytes 6152 | tf_op jit(solution)/shard_map/ppermute | solution.py:31
  156.0 6.6 %all-reduce.26 = (f32[]{:T(128)}, f32[]{:T(128)}) all-reduce(f32[]{:T(128)} %get-tuple-element.9, f32[]{:T(128)} %get-tuple-element.8), channel_id=1, replica_groups=mesh['row_0'=4,'row_1'=2,'col_0'=4,'col_1'=4] {'row_0'}, use_global_device_ids=true, to_apply=%region_13.14 | all-reduce | flops 2 | bytes 16 | tf_op jit(solution)/shard_map/psum | solution.py:58
  162.6 6.7 %all-reduce.30 = (f32[]{:T(128)}, f32[]{:T(128)}) all-reduce(f32[]{:T(128)} %get-tuple-element.32, f32[]{:T(128)} %get-tuple-element.33), channel_id=1, replica_groups=mesh['row_0'=4,'row_1'=2,'col_0'=4,'col_1'=4] {'row_1'}, use_global_device_ids=true, to_apply=%region_14.15 | all-reduce | flops 2 | bytes 16 | tf_op jit(solution)/shard_map/psum | solution.py:58
  169.4 7.1 %all-reduce.22 = (f32[]{:T(128)}, f32[]{:T(128)}) all-reduce(f32[]{:T(128)} %get-tuple-element.40, f32[]{:T(128)} %get-tuple-element.41), channel_id=1, replica_groups=mesh['row_0'=4,'row_1'=2,'col_0'=4,'col_1'=4] {'col_0'}, use_global_device_ids=true, to_apply=%region_15.16 | all-reduce | flops 2 | bytes 16 | tf_op jit(solution)/shard_map/psum | solution.py:58
  176.4 10.2 %all-reduce.18 = (f32[]{:T(128)}, f32[]{:T(128)}) all-reduce(f32[]{:T(128)} %get-tuple-element.24, f32[]{:T(128)} %get-tuple-element.25), channel_id=1, replica_groups=mesh['row_0'=4,'row_1'=2,'col_0'=4,'col_1'=4] {'col_1'}, use_global_device_ids=true, to_apply=%region_16.17 | all-reduce | flops 2 | bytes 16 | tf_op jit(solution)/shard_map/psum | solution.py:58
  198.4 6.8 %collective-permute-start.12 = (f32[1,512]{1,0:T(1,128)S(1)}, f32[1,512]{1,0:T(1,128)S(1)}, u32[]{:S(2)}, u32[]{:S(2)}) collective-permute-start(f32[1,512]{1,0:T(1,128)S(1)} %get-tuple-element.63), channel_id=1, source_target_pairs={{16,0},{32,16},{48,32},{64,48},{80,64},{96,80},{112,96},{17,1},{33... | collective-permute-start | bytes 6152 | tf_op jit(solution)/shard_map/ppermute | solution.py:31
  213.9 7.2 %all-reduce.25 = (f32[]{:T(128)}, f32[]{:T(128)}) all-reduce(f32[]{:T(128)} %get-tuple-element.7, f32[]{:T(128)} %get-tuple-element.6), channel_id=1, replica_groups=mesh['row_0'=4,'row_1'=2,'col_0'=4,'col_1'=4] {'row_0'}, use_global_device_ids=true, to_apply=%region_23.24 | all-reduce | flops 2 | bytes 16 | tf_op jit(solution)/shard_map/psum | solution.py:58
  227.1 6.8 %all-reduce.21 = (f32[]{:T(128)}, f32[]{:T(128)}) all-reduce(f32[]{:T(128)} %get-tuple-element.38, f32[]{:T(128)} %get-tuple-element.39), channel_id=1, replica_groups=mesh['row_0'=4,'row_1'=2,'col_0'=4,'col_1'=4] {'col_0'}, use_global_device_ids=true, to_apply=%region_25.26 | all-reduce | flops 2 | bytes 16 | tf_op jit(solution)/shard_map/psum | solution.py:58
  233.9 8.4 %all-reduce.17 = (f32[]{:T(128)}, f32[]{:T(128)}) all-reduce(f32[]{:T(128)} %get-tuple-element.22, f32[]{:T(128)} %get-tuple-element.23), channel_id=1, replica_groups=mesh['row_0'=4,'row_1'=2,'col_0'=4,'col_1'=4] {'col_1'}, use_global_device_ids=true, to_apply=%region_26.27 | all-reduce | flops 2 | bytes 16 | tf_op jit(solution)/shard_map/psum | solution.py:58
  253.9 6.3 %collective-permute-start.16 = (f32[1,512]{1,0:T(1,128)S(1)}, f32[1,512]{1,0:T(1,128)S(1)}, u32[]{:S(2)}, u32[]{:S(2)}) collective-permute-start(f32[1,512]{1,0:T(1,128)S(1)} %get-tuple-element.59), channel_id=1, source_target_pairs={{16,0},{32,16},{48,32},{64,48},{80,64},{96,80},{112,96},{17,1},{33... | collective-permute-start | bytes 6152 | tf_op jit(solution)/shard_map/ppermute | solution.py:31
  265.5 7.3 %all-reduce.24 = (f32[]{:T(128)}, f32[]{:T(128)}) all-reduce(f32[]{:T(128)} %get-tuple-element.5, f32[]{:T(128)} %get-tuple-element.4), channel_id=1, replica_groups=mesh['row_0'=4,'row_1'=2,'col_0'=4,'col_1'=4] {'row_0'}, use_global_device_ids=true, to_apply=%region_33.34 | all-reduce | flops 2 | bytes 16 | tf_op jit(solution)/shard_map/psum | solution.py:58
  278.1 8.4 %all-reduce.20 = (f32[]{:T(128)}, f32[]{:T(128)}) all-reduce(f32[]{:T(128)} %get-tuple-element.36, f32[]{:T(128)} %get-tuple-element.37), channel_id=1, replica_groups=mesh['row_0'=4,'row_1'=2,'col_0'=4,'col_1'=4] {'col_0'}, use_global_device_ids=true, to_apply=%region_35.36 | all-reduce | flops 2 | bytes 16 | tf_op jit(solution)/shard_map/psum | solution.py:58
  286.5 8.8 %all-reduce.16 = (f32[]{:T(128)}, f32[]{:T(128)}) all-reduce(f32[]{:T(128)} %get-tuple-element.20, f32[]{:T(128)} %get-tuple-element.21), channel_id=1, replica_groups=mesh['row_0'=4,'row_1'=2,'col_0'=4,'col_1'=4] {'col_1'}, use_global_device_ids=true, to_apply=%region_36.37 | all-reduce | flops 2 | bytes 16 | tf_op jit(solution)/shard_map/psum | solution.py:58
  301.9 11.8 %gather_fusion.1 = f32[2048]{0:T(1024)S(1)} fusion(f32[262144]{0:T(1024)S(1)} %bitcast.78, s32[2048]{0:T(1024)S(1)} %copy-done.12), kind=kCustom, calls=%fused_computation.1 | custom fusion | bytes 24576 | tf_op jit(solution)/shard_map/gather | solution.py:156
  318.1 13.5 %scatter_custom_fusion.3 = f32[16384]{0:T(1024)S(1)} fusion(s32[2048]{0:T(1024)S(1)} %bitcast.90, f32[2048]{0:T(1024)} %bitcast.105, f32[]{:T(128)} %constant.72.clone.1), kind=kCustom, calls=%fused_computation.132 | custom fusion | flops 2048 | bytes 66048 | tf_op jit(solution)/shard_map/scatter-add | solution.py:126
  331.7 13.4 %scatter_custom_fusion.2 = f32[16384]{0:T(1024)S(1)} fusion(s32[2048]{0:T(1024)S(1)} %bitcast.91, f32[2048]{0:T(1024)S(1)} %bitcast.104, f32[]{:T(128)} %constant.72.clone.1), kind=kCustom, calls=%fused_computation.134 | custom fusion | flops 2048 | bytes 65540 | tf_op jit(solution)/shard_map/scatter-add | solution.py:163
  (152 shorter events, 133.6 us)
Async XLA Ops:
  0.7 76.3 %collective-permute-start.2 = (f32[512,1]{1,0:T(8,128)S(1)}, f32[512,1]{1,0:T(8,128)S(1)}, u32[]{:S(2)}, u32[]{:S(2)}) collective-permute-start(f32[512,1]{1,0:T(8,128)S(1)} %broadcast.399), channel_id=1, source_target_pairs={{1,0},{2,1},{3,2},{4,3},{5,4},{6,5},{7,6},{8,7},{9,8},{10,9},{11,1... | collective-permute-start | bytes 6152 | tf_op jit(solution)/shard_map/ppermute | solution.py:31
  2.0 75.1 %collective-permute-start.3 = (f32[512,1]{1,0:T(8,128)S(1)}, f32[512,1]{1,0:T(8,128)S(1)}, u32[]{:S(2)}, u32[]{:S(2)}) collective-permute-start(f32[512,1]{1,0:T(8,128)S(1)} %broadcast.399), channel_id=1, source_target_pairs={{0,1},{1,2},{2,3},{3,4},{4,5},{5,6},{6,7},{7,8},{8,9},{9,10},{10,1... | collective-permute-start | bytes 6152 | tf_op jit(solution)/shard_map/ppermute | solution.py:30
  6.6 70.5 %collective-permute-start = (f32[1,512]{1,0:T(1,128)S(1)}, f32[1,512]{1,0:T(1,128)S(1)}, u32[]{:S(2)}, u32[]{:S(2)}) collective-permute-start(f32[1,512]{1,0:T(1,128)S(1)} %broadcast.398), channel_id=1, source_target_pairs={{16,0},{32,16},{48,32},{64,48},{80,64},{96,80},{112,96},{17,1},{33... | collective-permute-start | bytes 6152 | tf_op jit(solution)/shard_map/ppermute | solution.py:31
  9.8 67.2 %collective-permute-start.1 = (f32[1,512]{1,0:T(1,128)S(1)}, f32[1,512]{1,0:T(1,128)S(1)}, u32[]{:S(2)}, u32[]{:S(2)}) collective-permute-start(f32[1,512]{1,0:T(1,128)S(1)} %broadcast.398), channel_id=1, source_target_pairs={{0,16},{16,32},{32,48},{48,64},{64,80},{80,96},{96,112},{1,17},{17... | collective-permute-start | bytes 6152 | tf_op jit(solution)/shard_map/ppermute | solution.py:30
  14.8 15.5 %all-to-all-start = ((s32[16,1,128]{2,1,0:T(1,128)}), s32[16,1,128]{2,1,0:T(1,128)S(1)}, u32[]{:S(2)}, u32[]{:S(2)}) async-start(s32[16,1,128]{2,1,0:T(1,128)} %compare_select_fusion.13), calls=%async_computation | async-start | bytes 16384 | tf_op jit(solution)/shard_map/all_to_all | solution.py:119
  24.9 124.5 %collective-permute-start.23 = (f32[1,128,8]{1,2,0:T(8,128)}, f32[1,128,8]{1,2,0:T(8,128)}, u32[]{:S(2)}, u32[]{:S(2)}) collective-permute-start(f32[1,128,8]{1,2,0:T(8,128)} %bitcast.20), channel_id=1, source_target_pairs={{1,0},{2,1},{3,2},{4,3},{5,4},{6,5},{7,6},{8,7},{9,8},{10,9},{11,1... | collective-permute-start | bytes 12296 | tf_op jit(solution)/shard_map/ppermute | solution.py:52
  42.8 9.8 %all-to-all-start.1 = ((f32[16,1,128]{2,1,0:T(1,128)}), f32[16,1,128]{2,1,0:T(1,128)S(1)}, u32[]{:S(2)}, u32[]{:S(2)}) async-start(f32[16,1,128]{2,1,0:T(1,128)} %get-tuple-element.85), calls=%async_computation.1 | async-start | bytes 16384 | tf_op jit(solution)/shard_map/all_to_all | solution.py:134
  81.7 12.8 %collective-permute-start.6 = (f32[512,1]{1,0:T(8,128)S(1)}, f32[512,1]{1,0:T(8,128)S(1)}, u32[]{:S(2)}, u32[]{:S(2)}) collective-permute-start(f32[512,1]{1,0:T(8,128)S(1)} %get-tuple-element.68), channel_id=1, source_target_pairs={{1,0},{2,1},{3,2},{4,3},{5,4},{6,5},{7,6},{8,7},{9,8},{10,9},{11,1... | collective-permute-start | bytes 6152 | tf_op jit(solution)/shard_map/ppermute | solution.py:31
  83.0 11.5 %collective-permute-start.7 = (f32[512,1]{1,0:T(8,128)S(1)}, f32[512,1]{1,0:T(8,128)S(1)}, u32[]{:S(2)}, u32[]{:S(2)}) collective-permute-start(f32[512,1]{1,0:T(8,128)S(1)} %get-tuple-element.69), channel_id=1, source_target_pairs={{0,1},{1,2},{2,3},{3,4},{4,5},{5,6},{6,7},{7,8},{8,9},{9,10},{10,1... | collective-permute-start | bytes 6152 | tf_op jit(solution)/shard_map/ppermute | solution.py:30
  134.1 16.0 %collective-permute-start.10 = (f32[512,1]{1,0:T(8,128)}, f32[512,1]{1,0:T(8,128)S(1)}, u32[]{:S(2)}, u32[]{:S(2)}) collective-permute-start(f32[512,1]{1,0:T(8,128)} %get-tuple-element.64), channel_id=1, source_target_pairs={{1,0},{2,1},{3,2},{4,3},{5,4},{6,5},{7,6},{8,7},{9,8},{10,9},{11,1... | collective-permute-start | bytes 6152 | tf_op jit(solution)/shard_map/ppermute | solution.py:31
  135.4 14.8 %collective-permute-start.11 = (f32[512,1]{1,0:T(8,128)}, f32[512,1]{1,0:T(8,128)}, u32[]{:S(2)}, u32[]{:S(2)}) collective-permute-start(f32[512,1]{1,0:T(8,128)} %get-tuple-element.65), channel_id=1, source_target_pairs={{0,1},{1,2},{2,3},{3,4},{4,5},{5,6},{6,7},{7,8},{8,9},{9,10},{10,1... | collective-permute-start | bytes 6152 | tf_op jit(solution)/shard_map/ppermute | solution.py:30
  140.1 10.1 %collective-permute-start.8 = (f32[1,512]{1,0:T(1,128)}, f32[1,512]{1,0:T(1,128)}, u32[]{:S(2)}, u32[]{:S(2)}) collective-permute-start(f32[1,512]{1,0:T(1,128)} %get-tuple-element.67), channel_id=1, source_target_pairs={{16,0},{32,16},{48,32},{64,48},{80,64},{96,80},{112,96},{17,1},{33... | collective-permute-start | bytes 6152 | tf_op jit(solution)/shard_map/ppermute | solution.py:31
  149.4 110.8 %collective-permute-start.22 = (f32[1,128,8]{1,2,0:T(8,128)}, f32[1,128,8]{1,2,0:T(8,128)S(1)}, u32[]{:S(2)}, u32[]{:S(2)}) collective-permute-start(f32[1,128,8]{1,2,0:T(8,128)} %bitcast.16), channel_id=1, source_target_pairs={{0,1},{1,2},{2,3},{3,4},{4,5},{5,6},{6,7},{7,8},{8,9},{9,10},{10,1... | collective-permute-start | bytes 12296 | tf_op jit(solution)/shard_map/ppermute | solution.py:49
  193.0 16.4 %collective-permute-start.14 = (f32[512,1]{1,0:T(8,128)S(1)}, f32[512,1]{1,0:T(8,128)S(1)}, u32[]{:S(2)}, u32[]{:S(2)}) collective-permute-start(f32[512,1]{1,0:T(8,128)S(1)} %get-tuple-element.60), channel_id=1, source_target_pairs={{1,0},{2,1},{3,2},{4,3},{5,4},{6,5},{7,6},{8,7},{9,8},{10,9},{11,1... | collective-permute-start | bytes 6152 | tf_op jit(solution)/shard_map/ppermute | solution.py:31
  194.3 17.2 %collective-permute-start.15 = (f32[512,1]{1,0:T(8,128)S(1)}, f32[512,1]{1,0:T(8,128)S(1)}, u32[]{:S(2)}, u32[]{:S(2)}) collective-permute-start(f32[512,1]{1,0:T(8,128)S(1)} %get-tuple-element.61), channel_id=1, source_target_pairs={{0,1},{1,2},{2,3},{3,4},{4,5},{5,6},{6,7},{7,8},{8,9},{9,10},{10,1... | collective-permute-start | bytes 6152 | tf_op jit(solution)/shard_map/ppermute | solution.py:30
  198.4 13.2 %collective-permute-start.12 = (f32[1,512]{1,0:T(1,128)S(1)}, f32[1,512]{1,0:T(1,128)S(1)}, u32[]{:S(2)}, u32[]{:S(2)}) collective-permute-start(f32[1,512]{1,0:T(1,128)S(1)} %get-tuple-element.63), channel_id=1, source_target_pairs={{16,0},{32,16},{48,32},{64,48},{80,64},{96,80},{112,96},{17,1},{33... | collective-permute-start | bytes 6152 | tf_op jit(solution)/shard_map/ppermute | solution.py:31
  209.5 135.6 %collective-permute-start.20 = (f32[1,128]{1,0:T(1,128)S(1)}, f32[1,128]{1,0:T(1,128)S(1)}, u32[]{:S(2)}, u32[]{:S(2)}) collective-permute-start(f32[1,128]{1,0:T(1,128)S(1)} %copy-done.18), channel_id=1, source_target_pairs={{16,0},{32,16},{48,32},{64,48},{80,64},{96,80},{112,96},{17,1},{33... | collective-permute-start | bytes 1544 | tf_op jit(solution)/shard_map/ppermute | solution.py:52
  248.6 13.6 %collective-permute-start.18 = (f32[512,1]{1,0:T(8,128)S(1)}, f32[512,1]{1,0:T(8,128)S(1)}, u32[]{:S(2)}, u32[]{:S(2)}) collective-permute-start(f32[512,1]{1,0:T(8,128)S(1)} %get-tuple-element.56), channel_id=1, source_target_pairs={{1,0},{2,1},{3,2},{4,3},{5,4},{6,5},{7,6},{8,7},{9,8},{10,9},{11,1... | collective-permute-start | bytes 6152 | tf_op jit(solution)/shard_map/ppermute | solution.py:31
  249.9 14.2 %collective-permute-start.19 = (f32[512,1]{1,0:T(8,128)S(1)}, f32[512,1]{1,0:T(8,128)S(1)}, u32[]{:S(2)}, u32[]{:S(2)}) collective-permute-start(f32[512,1]{1,0:T(8,128)S(1)} %get-tuple-element.57), channel_id=1, source_target_pairs={{0,1},{1,2},{2,3},{3,4},{4,5},{5,6},{6,7},{7,8},{8,9},{9,10},{10,1... | collective-permute-start | bytes 6152 | tf_op jit(solution)/shard_map/ppermute | solution.py:30
  253.9 10.2 %collective-permute-start.16 = (f32[1,512]{1,0:T(1,128)S(1)}, f32[1,512]{1,0:T(1,128)S(1)}, u32[]{:S(2)}, u32[]{:S(2)}) collective-permute-start(f32[1,512]{1,0:T(1,128)S(1)} %get-tuple-element.59), channel_id=1, source_target_pairs={{16,0},{32,16},{48,32},{64,48},{80,64},{96,80},{112,96},{17,1},{33... | collective-permute-start | bytes 6152 | tf_op jit(solution)/shard_map/ppermute | solution.py:31
  262.2 82.9 %collective-permute-start.21 = (f32[1,128]{1,0:T(1,128)S(1)}, f32[1,128]{1,0:T(1,128)S(1)}, u32[]{:S(2)}, u32[]{:S(2)}) collective-permute-start(f32[1,128]{1,0:T(1,128)S(1)} %copy-done.17), channel_id=1, source_target_pairs={{0,16},{16,32},{32,48},{48,64},{64,80},{80,96},{96,112},{1,17},{17... | collective-permute-start | bytes 1544 | tf_op jit(solution)/shard_map/ppermute | solution.py:49
  314.4 17.2 %all-to-all-start.2 = ((f32[16,1,128]{2,1,0:T(1,128)}), f32[16,1,128]{2,1,0:T(1,128)S(1)}, u32[]{:S(2)}, u32[]{:S(2)}) async-start(f32[16,1,128]{2,1,0:T(1,128)} %fusion.61), calls=%async_computation.2 | async-start | bytes 16384 | tf_op jit(solution)/shard_map/all_to_all | solution.py:157
  345.2 13.1 %collective-permute-start.26 = (f32[1,128,8]{1,2,0:T(8,128)S(1)}, f32[1,128,8]{1,2,0:T(8,128)S(1)}, u32[]{:S(2)}, u32[]{:S(2)}) collective-permute-start(f32[1,128,8]{1,2,0:T(8,128)S(1)} %bitcast.109), channel_id=1, source_target_pairs={{0,1},{1,2},{2,3},{3,4},{4,5},{5,6},{6,7},{7,8},{8,9},{9,10},{10,1... | collective-permute-start | bytes 12296 | tf_op jit(solution)/shard_map/ppermute | solution.py:49
  345.5 12.8 %collective-permute-start.27 = (f32[1,128,8]{1,2,0:T(8,128)S(1)}, f32[1,128,8]{1,2,0:T(8,128)S(1)}, u32[]{:S(2)}, u32[]{:S(2)}) collective-permute-start(f32[1,128,8]{1,2,0:T(8,128)S(1)} %bitcast.110), channel_id=1, source_target_pairs={{1,0},{2,1},{3,2},{4,3},{5,4},{6,5},{7,6},{8,7},{9,8},{10,9},{11,1... | collective-permute-start | bytes 12296 | tf_op jit(solution)/shard_map/ppermute | solution.py:52
  (26 other events, 305.1 us)
where the time goes:
time: 362 us; the launch traced here: 360 us
  blocking collectives  121 us (33%)
  starting transfers between devices  106 us (29%)
  other arithmetic  78.6 us (22%)
  local copies, waits for them, and re-layouts  33.3 us (9%)
  between operations  14 us (4%)
  waiting for transfers between devices  6.41 us (2%)
    psum x16, blocking collectives, one_axis_at_a_time(): return functools.reduce(lax.psum, axes, shard)  121 us
    ppermute x10, starting transfers between devices, padded_2(): lax.ppermute(last, axis, up)  35.7 us
    ppermute x10, starting transfers between devices, padded_2(): lax.ppermute(leading, axis, [(b, a) for a, b in up])  33.1 us
    ppermute x4, starting transfers between devices, extended(): lax.ppermute(lax.slice_in_dim(block, 0, width, axis=dim), axis, backward)  17.1 us
    scatter-add x1, other arithmetic, per_device(): coarse_count = jnp.zeros(block_rows * block_cols, jnp.float32).at[held_fl...  13.5 us
    scatter-add x1, other arithmetic, per_device(): sources = jnp.zeros(block_rows * block_cols, jnp.float32).at[held_flat].a...  13.4 us
    gather x1, local copies, waits for them, and re-layouts, per_device(): volt.reshape(-1)[held_flat]  11.8 us
    gather x1, local copies, waits for them, and re-layouts, per_device(): at_fine = weight * solution.reshape(-1)[fine_index]  11.8 us
  transfers between devices with their start and end apart: 31, of which 4 were waited for; matrix products, arithmetic and copies ran while one was open for 30% of the time, Pallas kernels for 0%

commit v1 on v0

v1 whole, which is shorter than its diff:
```python
import jax
import jax.numpy as jnp
from jax import lax
from jax.experimental import pallas as pl
from jax.experimental.pallas import tpu as pltpu
from jax.sharding import PartitionSpec as P

F32 = jnp.float32
BF16 = jnp.bfloat16
HI = lax.Precision.HIGHEST
ROW, COL = "row", "col"

GROUP = 16
via_conductance = 2.0
coarse_conductance = 4.0
relaxation = 0.8

T = 512
CB = 128
NO = 16
L = 128
OFF = 16
EXT = OFF + T + 16
W = T + L

Q0, Q1, Q2 = 1.08976773, 1.76773384, 1.28562461


def iota(shape, dim):
    return lax.broadcasted_iota(jnp.int32, shape, dim)


def nt(a, b, precision=None):
    return lax.dot_general(
        a, b, (((1,), (1,)), ((), ())), precision=precision, preferred_element_type=F32
    )


def tn(a, b, precision=None):
    return lax.dot_general(
        a, b, (((0,), (0,)), ((), ())), precision=precision, preferred_element_type=F32
    )


def onehot(idx, n):
    return jnp.where(iota((n, idx.shape[1]), 0) == idx, 1.0, 0.0).astype(BF16)


def hi_lo(x):
    hi = x.astype(BF16).astype(F32)
    return hi, x - hi


def lanes(o):
    return slice(o * L, (o + 1) * L)


def diag_kernel(vf, wt, amp, mask, leak, load, invd, strips, a_s, b_s):
    for o in range(NO):
        f = vf[o : o + 1, :]
        a_s[:, lanes(o)] = onehot(f // T, T)
        b_s[:, lanes(o)] = jnp.where(iota((T, L), 0) == f % T, wt[o : o + 1, :], 0.0).astype(BF16)
    ld = amp[...] * mask[...].astype(F32)
    load[...] = ld
    inv = 1.0 / (4.0 + leak[...] + nt(a_s[...], b_s[...]))
    invd[...] = inv
    j, lane = iota((8, L), 0), iota((8, L), 1)
    first = jnp.where((j < 4) & (lane == j), 1.0, 0.0)
    last = jnp.where((j >= 4) & (lane == 120 + j), 1.0, 0.0)
    strips[0:8, :] = nt(first, ld[:, :L], HI) + nt(last, ld[:, T - L :], HI)
    strips[8:16, :] = nt(first, inv[:, :L], HI) + nt(last, inv[:, T - L :], HI)


def owner_onehots(held, r_s, c_s):
    for o in range(NO):
        h = held[o : o + 1, :]
        r_s[:, lanes(o)] = onehot(h >> 7, CB)
        c_s[:, lanes(o)] = onehot(h & (CB - 1), CB)


def lookup_kernel(held, volt, cleak, looked, cdiag, r_s, c_s):
    owner_onehots(held, r_s, c_s)
    vt = volt[...].T
    v1, rest = hi_lo(vt)
    v2, v3 = hi_lo(rest)
    for o in range(NO):
        pick = r_s[:, lanes(o)]
        rows = jnp.zeros((CB, L), F32)
        for v in (v3, v2, v1):
            rows = rows + jnp.dot(v.astype(BF16), pick, preferred_element_type=F32)
        sel = c_s[:, lanes(o)].astype(F32)
        looked[o : o + 1, :] = jnp.sum(rows * sel, axis=0, keepdims=True)
    count = nt(r_s[...], c_s[...])
    cdiag[...] = 4.0 * coarse_conductance + cleak[...] + via_conductance * count


def strips_kernel(vf, val, strips, volt, send_l, send_r, a_out):
    injl = []
    j = iota((8, L), 0)
    colid = jnp.where(j < 4, j, T - 8 + j)
    hs, ls = [], []
    for o in range(NO):
        f = vf[o : o + 1, :]
        a_out[:, lanes(o)] = onehot(f // T, T)
        hi, lo = hi_lo(val[o : o + 1, :])
        on = colid == f % T
        hs.append(jnp.where(on, hi, 0.0))
        ls.append(jnp.where(on, lo, 0.0))
    lhs = jnp.concatenate(
        [jnp.concatenate(hs, axis=1), jnp.concatenate(ls, axis=1)], axis=0
    ).astype(BF16)
    inj = nt(lhs, a_out[...])
    inv = strips[8:16, :]
    z = (strips[0:8, :] + inj[0:8] + inj[8:16]) * inv
    low = iota((8, T), 0) < 4
    send_l[:, :T] = jnp.where(low, z, pltpu.roll(inv, 4, 0))
    send_r[:, :T] = jnp.where(low, pltpu.roll(z, 4, 0), inv)
    g, lane = iota((8, CB), 0), iota((8, CB), 1)
    send_l[:, T:] = nt(jnp.where(lane == g * GROUP, 1.0, 0.0), volt[...], HI)
    send_r[:, T:] = nt(jnp.where(lane == g * GROUP + GROUP - 1, 1.0, 0.0), volt[...], HI)


def rhs_kernel(vf, val, load, invd, a, z, b_s):
    for o in range(NO):
        f = vf[o : o + 1, :]
        hi, lo = hi_lo(val[o : o + 1, :])
        on = iota((T, L), 0) == f % T
        b_s[:, lanes(o)] = jnp.where(on, hi, 0.0).astype(BF16)
        b_s[:, lanes(NO + o)] = jnp.where(on, lo, 0.0).astype(BF16)
    inj = nt(a[...], b_s[:, : NO * L]) + nt(a[...], b_s[:, NO * L :])
    z[...] = (load[...] + inj) * invd[...]


def edge_kernel(flags, z, invd, got_l, got_r, volt, zcol, icol, send_u, send_d):
    left = jnp.where(flags[1] > 0, 1.0, 0.0)
    right = jnp.where(flags[1] < NO - 1, 1.0, 0.0)
    j, lane = iota((8, L), 0), iota((8, L), 1)
    gl, gr = got_l[:, :T], got_r[:, :T]
    zc = tn(gr, jnp.where((j < 4) & (lane == j), right, 0.0), HI) + tn(
        gl, jnp.where((j < 4) & (lane == 124 + j), left, 0.0), HI
    )
    ic = tn(gr, jnp.where((j >= 4) & (lane == j - 4), right, 0.0), HI) + tn(
        gl, jnp.where((j >= 4) & (lane == 120 + j), left, 0.0), HI
    )
    zcol[...] = zc
    icol[...] = ic
    low = iota((8, W), 0) < 4
    zt = jnp.concatenate([z[0:8, :], zc[0:8]], axis=1)
    it = jnp.concatenate([invd[0:8, :], ic[0:8]], axis=1)
    zb = jnp.concatenate([z[T - 8 :, :], zc[T - 8 :]], axis=1)
    ib = jnp.concatenate([invd[T - 8 :, :], ic[T - 8 :]], axis=1)
    send_u[:, :W] = jnp.where(low, zt, pltpu.roll(it, 4, 0))
    send_d[:, :W] = jnp.where(low, pltpu.roll(zb, 4, 0), ib)
    send_u[:, W:] = volt[0:8, :]
    send_d[:, W:] = volt[CB - 8 :, :]


def neighbours(ref, start, rows):
    block = ref[pl.ds(start - 8, rows + 16), :]
    mid = block[8 : rows + 8]
    near = block[7 : rows + 7] + block[9 : rows + 9]
    return mid, near + pltpu.roll(mid, 1, 1) + pltpu.roll(mid, W - 1, 1)


def basis_kernel(flags, z, invd, zcol, icol, got_u, got_d, w_o, n1_o, n2_o, part, ie, ze, we, n1e, n2e):
    up = jnp.where(flags[0] > 0, 1.0, 0.0)
    down = jnp.where(flags[0] < 7, 1.0, 0.0)
    low = iota((8, W), 0) < 4
    top, bot = got_u[:, :W], got_d[:, :W]
    zero = jnp.zeros((8, W), F32)
    for e, own, col, t, b in (
        (ze, z, zcol, pltpu.roll(top, 4, 0), bot),
        (ie, invd, icol, top, pltpu.roll(bot, 4, 0)),
    ):
        e[0:8, :] = zero
        e[8:16, :] = jnp.where(low, 0.0, t) * up
        e[OFF : OFF + T, :T] = own[...]
        e[OFF : OFF + T, T:] = col[...]
        e[OFF + T : OFF + T + 8, :] = jnp.where(low, b, 0.0) * down
        e[OFF + T + 8 :, :] = zero
    for e in (we, n1e):
        e[0:8, :] = zero
        e[EXT - 8 :, :] = zero
    rows = 24

    def apply_to(src, dst, minus):
        def step(i, carry):
            start = pl.multiple_of(8 + i * rows, 8)
            mid, near = neighbours(src, start, rows)
            near = near * ie[pl.ds(start, rows), :]
            dst[pl.ds(start, rows), :] = mid - near if minus else near
            return carry

        lax.fori_loop(0, (EXT - 16) // rows, step, 0)

    apply_to(ze, we, True)
    apply_to(we, n1e, False)
    apply_to(n1e, n2e, False)

    def fold(p):
        return (p[:, 0:128] + p[:, 128:256]) + (p[:, 256:384] + p[:, 384:512])

    def gram(i, acc):
        start = pl.multiple_of(OFF + i * 8, 8)
        out = pl.multiple_of(i * 8, 8)
        n2w, near = neighbours(n2e, start, 8)
        inv = ie[pl.ds(start, 8), :T]
        n3 = near[:, :T] * inv
        n2 = n2w[:, :T]
        zz = ze[pl.ds(start, 8), :T]
        w = we[pl.ds(start, 8), :T]
        n1 = n1e[pl.ds(start, 8), :T]
        w_o[pl.ds(out, 8), :] = w
        n1_o[pl.ds(out, 8), :] = n1
        n2_o[pl.ds(out, 8), :] = n2
        d = 1.0 / inv
        bw, bn1, bn2 = w - n1, n1 - n2, n2 - n3
        e = (zz - Q0 * w - Q1 * n1 - Q2 * n2, w, n1, n2 - 0.25 * w)
        be = (w - Q0 * bw - Q1 * bn1 - Q2 * bn2, bw, bn1, bn2 - 0.25 * bw)
        new = []
        k = 0
        for p in range(4):
            de = d * e[p]
            for q in range(p, 4):
                new.append(acc[k] + fold(de * be[q]))
                k += 1
            new.append(acc[k] + fold(de * zz))
            k += 1
        return tuple(new)

    acc = lax.fori_loop(0, T // 8, gram, tuple(jnp.zeros((8, L), F32) for _ in range(14)))
    rows14 = jnp.concatenate(
        [jnp.sum(a, axis=0, keepdims=True) for a in acc] + [jnp.zeros((L - 14, L), F32)], axis=0
    )
    sums = nt(jnp.ones((8, L), F32), rows14, HI)
    part[...] = jnp.broadcast_to(sums[0:1, :], (L, L))


def solve_kernel(parts, z, w, n1, n2, vf, wt, x_o, cur, hi_s, lo_s):
    tot = jnp.sum(parts[...], axis=0, keepdims=True)
    lane = iota((1, L), 1)

    def pick(k):
        return jnp.sum(jnp.where(lane == k, tot, 0.0), axis=1, keepdims=True)

    h, b = {}, []
    k = 0
    for p in range(4):
        for q in range(p, 4):
            h[p, q] = pick(k)
            k += 1
        b.append(pick(k))
        k += 1
    floor = [3e-7 * h[p, p] for p in range(4)]
    inv = []
    for p in range(4):
        inv.append(jnp.where(h[p, p] > floor[p], 1.0 / h[p, p], 0.0))
        for q in range(p + 1, 4):
            f = h[p, q] * inv[p]
            for r in range(q, 4):
                h[q, r] = h[q, r] - f * h[p, r]
            b[q] = b[q] - f * b[p]
    c = [None] * 4
    for p in (3, 2, 1, 0):
        s = b[p]
        for q in range(p + 1, 4):
            s = s - h[p, q] * c[q]
        c[p] = s * inv[p]
    d1 = c[1] - Q0 * c[0] - 0.25 * c[3]
    d2 = c[2] - Q1 * c[0]
    d3 = c[3] - Q2 * c[0]
    x = c[0] * z[...] + d1 * w[...] + d2 * n1[...] + d3 * n2[...]
    x_o[...] = x
    hi, lo = hi_lo(x)
    hi_s[...] = hi.astype(BF16)
    lo_s[...] = lo.astype(BF16)
    for o in range(NO):
        f = vf[o : o + 1, :]
        sel = onehot(f % T, T)
        y = jnp.dot(hi_s[...], sel, preferred_element_type=F32) + jnp.dot(
            lo_s[...], sel, preferred_element_type=F32
        )
        y = jnp.where(iota((T, L), 0) == f // T, y, 0.0)
        cur[o : o + 1, :] = jnp.sum(y, axis=0, keepdims=True) * wt[o : o + 1, :]


def coarse_neighbours(flags, u, above, below, from_l, from_r):
    up = jnp.where(flags[0] > 0, 1.0, 0.0)
    down = jnp.where(flags[0] < 7, 1.0, 0.0)
    r, lane = iota((CB, CB), 0), iota((CB, CB), 1)
    g, gl = iota((8, CB), 0), iota((8, CB), 1)
    turned_l = jnp.where(g == 0, 0.0, pltpu.roll(from_l, 1, 0))
    turned_r = jnp.where(g == 7, 0.0, pltpu.roll(from_r, 7, 0))
    from_l = jnp.where(flags[1] == 0, turned_l, from_l)
    from_r = jnp.where(flags[1] == NO - 1, turned_r, from_r)
    seam_l = tn(from_l, jnp.where(gl == g * GROUP, 1.0, 0.0), HI)
    seam_r = tn(from_r, jnp.where(gl == g * GROUP + GROUP - 1, 1.0, 0.0), HI)
    beside = jnp.where(r == 0, above * up, pltpu.roll(u, 1, 0))
    beside += jnp.where(r == CB - 1, below * down, pltpu.roll(u, CB - 1, 0))
    beside += jnp.where(lane % GROUP == 0, seam_l, pltpu.roll(u, 1, 1))
    beside += jnp.where(lane % GROUP == GROUP - 1, seam_r, pltpu.roll(u, CB - 1, 1))
    return beside


def sweep(u, src, diag, beside):
    return u + relaxation * (src - (diag * u - coarse_conductance * beside)) / diag


def sweep1_kernel(flags, held, arrived, volt, cdiag, got_l, got_r, got_u, got_d, u_o, src_o, sl, sr, su, sd, r_s, c_s):
    for o in range(NO):
        h = held[o : o + 1, :]
        r_s[:, lanes(o)] = onehot(h >> 7, CB)
        on = iota((CB, L), 0) == (h & (CB - 1))
        v = arrived[o : o + 1, :]
        hi, lo = hi_lo(v)
        c_s[:, lanes(o)] = jnp.where(on, hi, 0.0).astype(BF16)
        c_s[:, lanes(NO + o)] = jnp.where(on, lo, 0.0).astype(BF16)
    src = nt(r_s[...], c_s[:, : NO * L]) + nt(r_s[...], c_s[:, NO * L :])
    u = volt[...]
    beside = coarse_neighbours(
        flags, u, got_u[7:8, W:], got_d[0:1, W:], got_l[:, T:], got_r[:, T:]
    )
    u = sweep(u, src, cdiag[...], beside)
    u_o[...] = u
    src_o[...] = src
    g, lane = iota((8, CB), 0), iota((8, CB), 1)
    sl[...] = nt(jnp.where(lane == g * GROUP, 1.0, 0.0), u, HI)
    sr[...] = nt(jnp.where(lane == g * GROUP + GROUP - 1, 1.0, 0.0), u, HI)
    su[...] = u[0:8, :]
    sd[...] = u[CB - 8 :, :]


def sweep2_kernel(flags, u, src, cdiag, got_l, got_r, got_u, got_d, u_o):
    beside = coarse_neighbours(flags, u[...], got_u[7:8, :], got_d[0:1, :], got_l[...], got_r[...])
    u_o[...] = sweep(u[...], src[...], cdiag[...], beside)


VM = pl.BlockSpec(memory_space=pltpu.VMEM)
SM = pl.BlockSpec(memory_space=pltpu.SMEM)


def call(body, outs, n_in, scratch=(), flags=False, flops=0):
    specs = ([SM] if flags else []) + [VM] * (n_in - (1 if flags else 0))
    shapes = [jax.ShapeDtypeStruct(s, d) for s, d in outs]
    return pl.pallas_call(
        body,
        out_shape=shapes,
        in_specs=specs,
        out_specs=[VM] * len(outs),
        scratch_shapes=[pltpu.VMEM(s, d) for s, d in scratch],
        cost_estimate=pl.CostEstimate(flops=flops, bytes_accessed=0, transcendentals=0),
    )


def ring(axis):
    n = lax.axis_size(axis)
    up = [(i, (i + 1) % n) for i in range(n)]
    return up, [(b, a) for a, b in up]


def swap(axis, to_low, to_high):
    up, down = ring(axis)
    return lax.ppermute(to_high, axis, up), lax.ppermute(to_low, axis, down)


def spread(x):
    return lax.all_to_all(x, COL, split_axis=0, concat_axis=0, tiled=True)


def per_device(load_amp, load_mask, leak, coarse_leak, coarse_init, via_fine, via_coarse, via_count):
    flags = jnp.where(
        jnp.arange(2, dtype=jnp.int32) == 0, lax.axis_index(ROW), lax.axis_index(COL)
    ).astype(jnp.int32)
    live = jnp.arange(L, dtype=jnp.int32)[None, :] < via_count.reshape(NO, 1)
    weight = jnp.where(live, via_conductance, 0.0).astype(F32)
    fine = via_fine.reshape(NO, L)
    coarse = via_coarse.reshape(NO, L)
    width = CB * NO
    request = jnp.where(live, coarse // width * CB + coarse % width % CB, -1)
    held = spread(request)

    tile, block, slots = ((T, T), F32), ((CB, CB), F32), ((NO, L), F32)
    load, invd, strips = call(
        diag_kernel, [tile, tile, ((16, T), F32)], 5,
        [((T, NO * L), BF16), ((T, NO * L), BF16)], flops=20_000_000_000,
    )(fine, weight, load_amp, load_mask, leak)

    looked, cdiag = call(
        lookup_kernel, [slots, block], 3, [((CB, NO * L), BF16), ((CB, NO * L), BF16)],
    )(held, coarse_init, coarse_leak)
    val = spread(looked) * weight

    side = ((8, W), F32)
    send_l, send_r, a = call(strips_kernel, [side, side, ((T, NO * L), BF16)], 4)(
        fine, val, strips, coarse_init
    )
    got_l, got_r = swap(COL, send_l, send_r)
    z = call(rhs_kernel, [tile], 5, [((T, 2 * NO * L), BF16)], flops=20_000_000_000)(
        fine, val, load, invd, a
    )[0]
    strip, rim = ((T, L), F32), ((8, W + CB), F32)
    zcol, icol, send_u, send_d = call(edge_kernel, [strip, strip, rim, rim], 6, flags=True)(
        flags, z, invd, got_l, got_r, coarse_init
    )
    got_u, got_d = swap(ROW, send_u, send_d)
    ext = ((EXT, W), F32)
    w, n1, n2, part = call(
        basis_kernel, [tile, tile, tile, ((L, L), F32)], 7, [ext] * 5, flags=True,
    )(flags, z, invd, zcol, icol, got_u, got_d)
    parts = lax.all_to_all(part, (ROW, COL), split_axis=0, concat_axis=0, tiled=True)
    fine_drop, current = call(
        solve_kernel, [tile, slots], 7, [((T, T), BF16), ((T, T), BF16)],
    )(parts, z, w, n1, n2, fine, weight)
    arrived = spread(current)
    seam, edge = ((8, CB), F32), ((8, CB), F32)
    u, src, sl, sr, su, sd = call(
        sweep1_kernel, [block, block, seam, seam, edge, edge], 9,
        [((CB, NO * L), BF16), ((CB, 2 * NO * L), BF16)], flags=True,
    )(flags, held, arrived, coarse_init, cdiag, got_l, got_r, got_u, got_d)
    hl, hr = swap(COL, sl, sr)
    hu, hd = swap(ROW, su, sd)
    coarse_drop = call(sweep2_kernel, [block], 8, flags=True)(
        flags, u, src, cdiag, hl, hr, hu, hd
    )[0]
    return fine_drop, coarse_drop


def solution(mesh):
    spec = P(ROW, COL)
    return jax.shard_map(
        per_device, mesh=mesh, in_specs=(spec,) * 8, out_specs=(spec, spec), check_vma=False
    )
```

time: 362 us -> 130 us (0.36)
  blocking collectives: 121 us -> 25.1 us
  starting transfers between devices: 106 us -> 28.9 us
  other arithmetic: 78.6 us -> 3.31 us
  Pallas kernels: 0 us -> 49.7 us
  local copies, waits for them, and re-layouts: 33.3 us -> 2.98 us
  between operations: 14 us -> 0.7 us
  waiting for transfers between devices: 6.41 us -> 19 us
    psum x16 -> x0, blocking collectives: 121 us -> none  [one_axis_at_a_time(): return functools.reduce(lax.psum, axes, shard)]
    ppermute x28 -> x8, starting transfers between devices: 90.5 us -> 17.9 us  [swap(): return (lax.ppermute(to_high, axis, up), lax.ppermute(to_low, axis, down))]
    scatter-add x4 -> x0, other arithmetic: 49.9 us -> none  [the longest x1 13.5 us: per_device(): coarse_count = jnp.zeros(block_rows * block_cols, jnp.float32).at[held_fl...]
    pallas_call x0 -> x9, Pallas kernels: none -> 49.7 us  [the longest x1 16.7 us: per_device(): call(basis_kernel, [tile, tile, tile, ((L, L), F32)], 7, [ext] * 5, flags...]
    all_to_all x0 -> x2, blocking collectives: none -> 25.1 us  [the longest x1 14.7 us: per_device(): lax.all_to_all(part, (ROW, COL), split_axis=0, concat_axis=0, tiled=True)]
    gather x2 -> x0, local copies, waits for them, and re-layouts: 23.6 us -> none  [the longest x1 11.8 us: per_device(): volt.reshape(-1)[held_flat]]
    reduce_sum x4 -> x0, other arithmetic: 10.8 us -> none  [paired_sum(): jnp.sum(second)]
    div x4 -> x0, other arithmetic: 10.2 us -> none  [per_device(): precond = residual / fine_diag]
  transfers between devices with their start and end apart: 31 -> 10, of which waited for: 4 -> 6; matrix products, arithmetic and copies ran while one was open for 30% -> 0% of each run, Pallas kernels for 0% -> 5%
where the time goes in v1:
time: 130 us
  Pallas kernels  49.7 us (38%)
  starting transfers between devices  28.9 us (22%)
  blocking collectives  25.1 us (19%)
  waiting for transfers between devices  19 us (15%)
  other arithmetic  3.31 us (3%)
  local copies, waits for them, and re-layouts  2.98 us (2%)
    ppermute x8, starting transfers between devices, swap(): return (lax.ppermute(to_high, axis, up), lax.ppermute(to_low, axis, down))  17.9 us
    pallas_call x1, Pallas kernels, per_device(): call(basis_kernel, [tile, tile, tile, ((L, L), F32)], 7, [ext] * 5, flags...  16.7 us
    all_to_all x1, blocking collectives, per_device(): lax.all_to_all(part, (ROW, COL), split_axis=0, concat_axis=0, tiled=True)  14.7 us
    all_to_all x2, waiting for transfers between devices, spread(): return lax.all_to_all(x, COL, split_axis=0, concat_axis=0, tiled=True)  12.1 us
    all_to_all x2, starting transfers between devices, spread(): return lax.all_to_all(x, COL, split_axis=0, concat_axis=0, tiled=True)  11 us
    all_to_all x1, blocking collectives, spread(): return lax.all_to_all(x, COL, split_axis=0, concat_axis=0, tiled=True)  10.4 us
    pallas_call x1, Pallas kernels, per_device(): call(solve_kernel, [tile, slots], 7, [((T, T), BF16), ((T, T), BF16)])  7.65 us
    ppermute x8, waiting for transfers between devices, swap(): return (lax.ppermute(to_high, axis, up), lax.ppermute(to_low, axis, down))  6.97 us
  transfers between devices with their start and end apart: 10, of which 6 were waited for; matrix products, arithmetic and copies ran while one was open for 0% of the time, Pallas kernels for 5%

profile of v1, /device:TPU:1, one launch (start us, length us, event | category | flops | bytes accessed | tf_op | source)
XLA Modules:
  0.0 129.8 jit_solution(17224804238562936925)
XLA Ops:
  0.6 1.4 %compare_select_fusion.2 = s32[16,1,128]{2,1,0:T(1,128)} fusion(s32[1,2048]{1,0:T(1,128)} %param.14, s32[16]{0:T(128)} %bitcast.40), kind=kLoop, calls=%fused_computation.5 | loop fusion | flops 69632 | bytes 16448 | tf_op jit(solution)/shard_map/jit(_where)/select_n | solution.py:379
  2.0 7.6 %all-to-all-start = ((s32[16,1,128]{2,1,0:T(1,128)}), s32[16,1,128]{2,1,0:T(1,128)S(1)}, u32[]{:S(2)}, u32[]{:S(2)}) async-start(s32[16,1,128]{2,1,0:T(1,128)} %compare_select_fusion.2), calls=%async_computation | async-start | bytes 16384 | tf_op jit(solution)/shard_map/all_to_all | solution.py:367
  9.6 6.4 %all-to-all-done = s32[16,1,128]{2,1,0:T(1,128)S(1)} async-done(((s32[16,1,128]{2,1,0:T(1,128)}), s32[16,1,128]{2,1,0:T(1,128)S(1)}, u32[]{:S(2)}, u32[]{:S(2)}) %all-to-all-start) | async-done | bytes 8224 | tf_op jit(solution)/shard_map/all_to_all | solution.py:367
  16.6 2.4 %shard_map.95 = (f32[16,128]{1,0:T(8,128)}, f32[128,128]{1,0:T(8,128)}) custom-call(s32[16,128]{1,0:T(8,128)} %bitcast.29, f32[128,128]{1,0:T(8,128)} %volt.7, f32[128,128]{1,0:T(8,128)} %cleak.1), custom_call_target="tpu_custom_call" | custom-call | tf_op jit(solution)/shard_map/pallas_call | solution.py:388
  18.9 3.5 %all-to-all-start.1 = ((f32[16,1,128]{2,1,0:T(1,128)}), f32[16,1,128]{2,1,0:T(1,128)S(1)}, u32[]{:S(2)}, u32[]{:S(2)}) async-start(f32[16,1,128]{2,1,0:T(1,128)} %bitcast.38), calls=%async_computation.1 | async-start | bytes 16384 | tf_op jit(solution)/shard_map/all_to_all | solution.py:367
  23.0 5.7 %all-to-all-done.1 = f32[16,1,128]{2,1,0:T(1,128)S(1)} async-done(((f32[16,1,128]{2,1,0:T(1,128)}), f32[16,1,128]{2,1,0:T(1,128)S(1)}, u32[]{:S(2)}, u32[]{:S(2)}) %all-to-all-start.1) | async-done | bytes 8224 | tf_op jit(solution)/shard_map/all_to_all | solution.py:367
  28.7 1.3 %fusion.2 = (f32[16,128]{1,0:T(8,128)}, f32[16,128]{1,0:T(8,128)}) fusion(s32[16]{0:T(128)} %bitcast.41, f32[16,128]{1,0:T(8,128)S(1)} %bitcast.36), kind=kLoop, calls=%fused_computation.13 | loop fusion | flops 6144 | bytes 24640 | tf_op jit(solution)/shard_map/jit(_where)/select_n | solution.py:375
  30.0 5.4 %shard_map.96 = (f32[512,512]{1,0:T(8,128)}, f32[512,512]{1,0:T(8,128)}, f32[16,512]{1,0:T(8,128)}) custom-call(s32[16,128]{1,0:T(8,128)} %bitcast.32, f32[16,128]{1,0:T(8,128)} %get-tuple-element.50.wt, f32[512,512]{1,0:T(8,128)} %amp.1, s32[512,512]{1,0:T(8,128)} %mask.1, f32[512,512]{1,0:T(8,128)} %leak.1), custom_call_target="tpu_custom_call" | custom-call | flops 20000000000 | tf_op jit(solution)/shard_map/pallas_call | solution.py:383
  35.4 3.4 %shard_map.97 = (f32[8,640]{1,0:T(8,128)}, f32[8,640]{1,0:T(8,128)}, bf16[512,2048]{1,0:T(8,128)(2,1)}) custom-call(s32[16,128]{1,0:T(8,128)} %bitcast.33, f32[16,128]{1,0:T(8,128)} %get-tuple-element.51.val, f32[16,512]{1,0:T(8,128)} %get-tuple-element.29.strips, f32[128,128]{1,0:T(8,128)} %volt.7), custom_call_target="tpu_custom_call" | custom-call | tf_op jit(solution)/shard_map/pallas_call | solution.py:394
  39.1 4.5 %collective-permute-start.1 = (f32[8,640]{1,0:T(8,128)}, f32[8,640]{1,0:T(8,128)S(1)}, u32[]{:S(2)}, u32[]{:S(2)}) collective-permute-start(f32[8,640]{1,0:T(8,128)} %get-tuple-element.32), channel_id=1, source_target_pairs={{1,0},{2,1},{3,2},{4,3},{5,4},{6,5},{7,6},{8,7},{9,8},{10,9},{11,1... | collective-permute-start | bytes 61448 | tf_op jit(solution)/shard_map/ppermute | solution.py:363
  43.6 6.0 %shard_map.98.z = f32[512,512]{1,0:T(8,128)} custom-call(s32[16,128]{1,0:T(8,128)} %bitcast.34, f32[16,128]{1,0:T(8,128)} %get-tuple-element.51.val, f32[512,512]{1,0:T(8,128)} %get-tuple-element.27.load, f32[512,512]{1,0:T(8,128)} %get-tuple-element.28.invd, bf16[512,2048]{1,0:T(8,128)(2,1)} %get-tuple-element.30.a), custom_call_target="tpu_custom_call" | custom-call | flops 20000000000 | tf_op jit(solution)/shard_map/pallas_call | solution.py:398
  50.8 3.4 %shard_map.99 = (f32[512,128]{1,0:T(8,128)}, f32[512,128]{1,0:T(8,128)}, f32[8,768]{1,0:T(8,128)}, f32[8,768]{1,0:T(8,128)}) custom-call(s32[2]{0:T(128)} %compare_select_fusion.6.flags, f32[512,512]{1,0:T(8,128)} %shard_map.98.z, f32[512,512]{1,0:T(8,128)} %get-tuple-element.28.invd, f32[8,640]{1,0:T(8,128)} %copy-done.2, f32[8,640]{1,0:T(8,128)} %copy-done.3, ...), custom_call_target="tpu_custom_call" | custom-call | tf_op jit(solution)/shard_map/pallas_call | solution.py:402
  54.2 5.3 %collective-permute-start.2 = (f32[8,768]{1,0:T(8,128)}, f32[8,768]{1,0:T(8,128)S(1)}, u32[]{:S(2)}, u32[]{:S(2)}) collective-permute-start(f32[8,768]{1,0:T(8,128)} %get-tuple-element.35), channel_id=1, source_target_pairs={{0,16},{16,32},{32,48},{48,64},{64,80},{80,96},{96,112},{112,0},{1... | collective-permute-start | bytes 73736 | tf_op jit(solution)/shard_map/ppermute | solution.py:363
  59.5 1.2 collective-permute-done.2.got_u
  60.7 2.3 %collective-permute-done.3.got_d = f32[8,768]{1,0:T(8,128)S(1)} collective-permute-done((f32[8,768]{1,0:T(8,128)}, f32[8,768]{1,0:T(8,128)S(1)}, u32[]{:S(2)}, u32[]{:S(2)}) %collective-permute-start.3) | collective-permute-done | bytes 24608 | tf_op jit(solution)/shard_map/ppermute | solution.py:363
  63.6 16.7 %shard_map.100 = (f32[512,512]{1,0:T(8,128)}, f32[512,512]{1,0:T(8,128)}, f32[512,512]{1,0:T(8,128)}, f32[128,128]{1,0:T(8,128)}) custom-call(s32[2]{0:T(128)} %compare_select_fusion.6.flags, f32[512,512]{1,0:T(8,128)} %shard_map.98.z, f32[512,512]{1,0:T(8,128)} %get-tuple-element.28.invd, f32[512,128]{1,0:T(8,128)} %get-tuple-element.33.zcol, ...), custom_call_target="tpu_custom_call" | custom-call | tf_op jit(solution)/shard_map/pallas_call | solution.py:407
  80.3 14.7 %all_to_all.42 = f32[128,1,128]{2,1,0:T(1,128)} all-to-all(f32[128,1,128]{2,1,0:T(1,128)} %bitcast.31), channel_id=1, replica_groups=mesh['row'=8,'col'=16] {'row','col'}, dimensions={0} | all-to-all | bytes 131072 | tf_op jit(solution)/shard_map/all_to_all | solution.py:410
  95.0 7.6 %shard_map.101 = (f32[512,512]{1,0:T(8,128)}, f32[16,128]{1,0:T(8,128)}) custom-call(f32[128,128]{1,0:T(8,128)} %bitcast.28, f32[512,512]{1,0:T(8,128)} %shard_map.98.z, f32[512,512]{1,0:T(8,128)} %get-tuple-element.38.w, f32[512,512]{1,0:T(8,128)} %get-tuple-element.39.n1, f32[512,512]{1,0:T(8,128)} %get-tuple-element.40.n2, s32[16,128]{1,0:T(8,128)} %bitcast.35, ...), custom_call_target="tpu_custom_call" | custom-call | tf_op jit(solution)/shard_map/pallas_call | solution.py:411
  102.7 10.4 %all_to_all.43 = f32[16,1,128]{2,1,0:T(1,128)} all-to-all(f32[16,1,128]{2,1,0:T(1,128)} %bitcast.39), channel_id=1, replica_groups=mesh['row'=8,'col'=16] {'col'}, dimensions={0} | all-to-all | bytes 16384 | tf_op jit(solution)/shard_map/all_to_all | solution.py:367
  113.1 2.9 %shard_map.102 = (f32[128,128]{1,0:T(8,128)}, f32[128,128]{1,0:T(8,128)}, f32[8,128]{1,0:T(8,128)}, f32[8,128]{1,0:T(8,128)}, f32[8,128]{1,0:T(8,128)}, /*index=5*/f32[8,128]{1,0:T(8,128)}) custom-call(s32[2]{0:T(128)} %compare_select_fusion.6.flags, s32[16,128]{1,0:T(8,128)} %bitcast.30, f32[16,128]{1,0:T(8,128)} %bitcast.37, f32[128,128]{1,0:T(8,128)} %volt.7, ...), custom_call_target="tpu_custom_call" | custom-call | tf_op jit(solution)/shard_map/pallas_call | solution.py:416
  116.2 4.6 %collective-permute-start.5 = (f32[8,128]{1,0:T(8,128)}, f32[8,128]{1,0:T(8,128)S(1)}, u32[]{:S(2)}, u32[]{:S(2)}) collective-permute-start(f32[8,128]{1,0:T(8,128)} %get-tuple-element.47), channel_id=1, source_target_pairs={{1,0},{2,1},{3,2},{4,3},{5,4},{6,5},{7,6},{8,7},{9,8},{10,9},{11,1... | collective-permute-start | bytes 12296 | tf_op jit(solution)/shard_map/ppermute | solution.py:363
  120.8 3.0 %collective-permute-start.6 = (f32[8,128]{1,0:T(8,128)}, f32[8,128]{1,0:T(8,128)S(1)}, u32[]{:S(2)}, u32[]{:S(2)}) collective-permute-start(f32[8,128]{1,0:T(8,128)} %get-tuple-element.48), channel_id=1, source_target_pairs={{0,16},{16,32},{32,48},{48,64},{64,80},{80,96},{96,112},{112,0},{1... | collective-permute-start | bytes 12296 | tf_op jit(solution)/shard_map/ppermute | solution.py:363
  124.7 2.6 %collective-permute-done.7.got_d = f32[8,128]{1,0:T(8,128)S(1)} collective-permute-done((f32[8,128]{1,0:T(8,128)}, f32[8,128]{1,0:T(8,128)S(1)}, u32[]{:S(2)}, u32[]{:S(2)}) %collective-permute-start.7) | collective-permute-done | bytes 4128 | tf_op jit(solution)/shard_map/ppermute | solution.py:363
  127.9 1.9 %shard_map.103 = f32[128,128]{1,0:T(8,128)} custom-call(s32[2]{0:T(128)} %compare_select_fusion.6.flags, f32[128,128]{1,0:T(8,128)} %get-tuple-element.44.u, f32[128,128]{1,0:T(8,128)} %get-tuple-element.45.src, f32[128,128]{1,0:T(8,128)} %get-tuple-element.43.cdiag, f32[8,128]{1,0:T(8,128)} %copy-done.5, f32[8,128]{1,0:T(8,128)} %copy-done.6, ...), custom_call_target="tpu_custom_call" | custom-call | tf_op jit(solution)/shard_map/pallas_call | solution.py:422
  (28 shorter events, 4.9 us)
Async XLA Ops:
  2.0 13.9 %all-to-all-start = ((s32[16,1,128]{2,1,0:T(1,128)}), s32[16,1,128]{2,1,0:T(1,128)S(1)}, u32[]{:S(2)}, u32[]{:S(2)}) async-start(s32[16,1,128]{2,1,0:T(1,128)} %compare_select_fusion.2), calls=%async_computation | async-start | bytes 16384 | tf_op jit(solution)/shard_map/all_to_all | solution.py:367
  16.0 0.6 copy-start.4
  18.9 9.8 %all-to-all-start.1 = ((f32[16,1,128]{2,1,0:T(1,128)}), f32[16,1,128]{2,1,0:T(1,128)S(1)}, u32[]{:S(2)}, u32[]{:S(2)}) async-start(f32[16,1,128]{2,1,0:T(1,128)} %bitcast.38), calls=%async_computation.1 | async-start | bytes 16384 | tf_op jit(solution)/shard_map/all_to_all | solution.py:367
  38.8 10.8 %collective-permute-start = (f32[8,640]{1,0:T(8,128)}, f32[8,640]{1,0:T(8,128)S(1)}, u32[]{:S(2)}, u32[]{:S(2)}) collective-permute-start(f32[8,640]{1,0:T(8,128)} %get-tuple-element.31), channel_id=1, source_target_pairs={{0,1},{1,2},{2,3},{3,4},{4,5},{5,6},{6,7},{7,8},{8,9},{9,10},{10,1... | collective-permute-start | bytes 61448 | tf_op jit(solution)/shard_map/ppermute | solution.py:363
  39.1 10.5 %collective-permute-start.1 = (f32[8,640]{1,0:T(8,128)}, f32[8,640]{1,0:T(8,128)S(1)}, u32[]{:S(2)}, u32[]{:S(2)}) collective-permute-start(f32[8,640]{1,0:T(8,128)} %get-tuple-element.32), channel_id=1, source_target_pairs={{1,0},{2,1},{3,2},{4,3},{5,4},{6,5},{7,6},{8,7},{9,8},{10,9},{11,1... | collective-permute-start | bytes 61448 | tf_op jit(solution)/shard_map/ppermute | solution.py:363
  49.6 0.6 copy-start.2
  50.2 0.6 copy-start.3
  54.2 6.5 %collective-permute-start.2 = (f32[8,768]{1,0:T(8,128)}, f32[8,768]{1,0:T(8,128)S(1)}, u32[]{:S(2)}, u32[]{:S(2)}) collective-permute-start(f32[8,768]{1,0:T(8,128)} %get-tuple-element.35), channel_id=1, source_target_pairs={{0,16},{16,32},{32,48},{48,64},{64,80},{80,96},{96,112},{112,0},{1... | collective-permute-start | bytes 73736 | tf_op jit(solution)/shard_map/ppermute | solution.py:363
  59.5 3.5 %collective-permute-start.3 = (f32[8,768]{1,0:T(8,128)}, f32[8,768]{1,0:T(8,128)S(1)}, u32[]{:S(2)}, u32[]{:S(2)}) collective-permute-start(f32[8,768]{1,0:T(8,128)} %get-tuple-element.36), channel_id=1, source_target_pairs={{16,0},{32,16},{48,32},{64,48},{80,64},{96,80},{112,96},{0,112},{1... | collective-permute-start | bytes 73736 | tf_op jit(solution)/shard_map/ppermute | solution.py:363
  60.7 2.3 %copy-start = (f32[8,768]{1,0:T(8,128)}, f32[8,768]{1,0:T(8,128)S(1)}, u32[]{:S(2)}) copy-start(f32[8,768]{1,0:T(8,128)S(1)} %collective-permute-done.2.got_u) | copy-start | bytes 73732
  63.0 0.6 copy-start.1
  116.0 7.7 %collective-permute-start.4 = (f32[8,128]{1,0:T(8,128)}, f32[8,128]{1,0:T(8,128)S(1)}, u32[]{:S(2)}, u32[]{:S(2)}) collective-permute-start(f32[8,128]{1,0:T(8,128)} %get-tuple-element.46), channel_id=1, source_target_pairs={{0,1},{1,2},{2,3},{3,4},{4,5},{5,6},{6,7},{7,8},{8,9},{9,10},{10,1... | collective-permute-start | bytes 12296 | tf_op jit(solution)/shard_map/ppermute | solution.py:363
  116.2 7.6 %collective-permute-start.5 = (f32[8,128]{1,0:T(8,128)}, f32[8,128]{1,0:T(8,128)S(1)}, u32[]{:S(2)}, u32[]{:S(2)}) collective-permute-start(f32[8,128]{1,0:T(8,128)} %get-tuple-element.47), channel_id=1, source_target_pairs={{1,0},{2,1},{3,2},{4,3},{5,4},{6,5},{7,6},{8,7},{9,8},{10,9},{11,1... | collective-permute-start | bytes 12296 | tf_op jit(solution)/shard_map/ppermute | solution.py:363
  120.8 3.9 %collective-permute-start.6 = (f32[8,128]{1,0:T(8,128)}, f32[8,128]{1,0:T(8,128)S(1)}, u32[]{:S(2)}, u32[]{:S(2)}) collective-permute-start(f32[8,128]{1,0:T(8,128)} %get-tuple-element.48), channel_id=1, source_target_pairs={{0,16},{16,32},{32,48},{48,64},{64,80},{80,96},{96,112},{112,0},{1... | collective-permute-start | bytes 12296 | tf_op jit(solution)/shard_map/ppermute | solution.py:363
  123.8 3.5 %collective-permute-start.7 = (f32[8,128]{1,0:T(8,128)}, f32[8,128]{1,0:T(8,128)S(1)}, u32[]{:S(2)}, u32[]{:S(2)}) collective-permute-start(f32[8,128]{1,0:T(8,128)} %get-tuple-element.49), channel_id=1, source_target_pairs={{16,0},{32,16},{48,32},{64,48},{80,64},{96,80},{112,96},{0,112},{1... | collective-permute-start | bytes 12296 | tf_op jit(solution)/shard_map/ppermute | solution.py:363
  123.8 3.5 %copy-start.5 = (f32[8,128]{1,0:T(8,128)}, f32[8,128]{1,0:T(8,128)S(1)}, u32[]{:S(2)}) copy-start(f32[8,128]{1,0:T(8,128)S(1)} %collective-permute-done.4.got_l) | copy-start | bytes 12292
  123.8 3.5 %copy-start.6 = (f32[8,128]{1,0:T(8,128)}, f32[8,128]{1,0:T(8,128)S(1)}, u32[]{:S(2)}) copy-start(f32[8,128]{1,0:T(8,128)S(1)} %collective-permute-done.5.got_r) | copy-start | bytes 12292
  124.7 2.6 %copy-start.7 = (f32[8,128]{1,0:T(8,128)}, f32[8,128]{1,0:T(8,128)S(1)}, u32[]{:S(2)}) copy-start(f32[8,128]{1,0:T(8,128)S(1)} %collective-permute-done.6.got_u) | copy-start | bytes 12292
  127.3 0.6 copy-start.8

commit v2 on v1

v2 whole, which is shorter than its diff:
```python
import jax
import jax.numpy as jnp
from jax import lax
from jax.experimental import pallas as pl
from jax.experimental.pallas import tpu as pltpu
from jax.sharding import PartitionSpec as P


F32 = jnp.float32
BF16 = jnp.bfloat16
HI = lax.Precision.HIGHEST
ROW, COL = "row", "col"

GROUP = 16
via_conductance = 2.0
coarse_conductance = 4.0
relaxation = 0.8

T = 512
CB = 128
NO = 16
L = 128
OFF = 16
EXT = OFF + T + 16
W = T + L

Q0, Q1, Q2 = 1.08976773, 1.76773384, 1.28562461


def iota(shape, dim):
    return lax.broadcasted_iota(jnp.int32, shape, dim)


def nt(a, b, precision=None):
    return lax.dot_general(
        a, b, (((1,), (1,)), ((), ())), precision=precision, preferred_element_type=F32
    )


def tn(a, b, precision=None):
    return lax.dot_general(
        a, b, (((0,), (0,)), ((), ())), precision=precision, preferred_element_type=F32
    )


def onehot(idx, n):
    return jnp.where(iota((n, idx.shape[1]), 0) == idx, 1.0, 0.0).astype(BF16)


def hi_lo(x):
    hi = x.astype(BF16).astype(F32)
    return hi, x - hi


def lanes(o):
    return slice(o * L, (o + 1) * L)


def diag_kernel(vf, wt, amp, mask, leak, zl, invd, strips, rims, a_s, b_s):
    for o in range(NO):
        f = vf[o : o + 1, :]
        a_s[:, lanes(o)] = onehot(f // T, T)
        b_s[:, lanes(o)] = jnp.where(iota((T, L), 0) == f % T, wt[o : o + 1, :], 0.0).astype(BF16)
    inv = 1.0 / (4.0 + leak[...] + nt(a_s[...], b_s[...]))
    z = amp[...] * mask[...].astype(F32) * inv
    zl[...] = z
    invd[...] = inv
    j, lane = iota((8, L), 0), iota((8, L), 1)
    first = jnp.where((j < 4) & (lane == j), 1.0, 0.0)
    last = jnp.where((j >= 4) & (lane == 120 + j), 1.0, 0.0)
    strips[0:8, :] = nt(first, z[:, :L], HI) + nt(last, z[:, T - L :], HI)
    strips[8:16, :] = nt(first, inv[:, :L], HI) + nt(last, inv[:, T - L :], HI)
    rims[0:8, :] = inv[0:8]
    rims[8:16, :] = inv[T - 8 :]


def lookup_kernel(held, volt, looked):
    v1, rest = hi_lo(volt[...].T)
    v2, v3 = hi_lo(rest)
    v = jnp.concatenate([v3, v2, v1], axis=0).astype(BF16)
    for i in range(NO // 2):
        h = jnp.concatenate([held[2 * i : 2 * i + 1, :], held[2 * i + 1 : 2 * i + 2, :]], axis=1)
        y = jnp.dot(v, onehot(h >> 7, CB), preferred_element_type=F32)
        y = y[:CB] + y[CB : 2 * CB] + y[2 * CB :]
        y = jnp.where(iota((CB, 2 * L), 0) == (h & (CB - 1)), y, 0.0)
        y = jnp.sum(y, axis=0, keepdims=True)
        looked[2 * i : 2 * i + 1, :] = y[:, :L]
        looked[2 * i + 1 : 2 * i + 2, :] = y[:, L:]


def strips_kernel(vf, wt, at_via, strips, volt, a_o, send_l, send_r):
    j = iota((8, L), 0)
    colid = jnp.where(j < 4, j, T - 8 + j)
    hs, ls = [], []
    for o in range(NO):
        f = vf[o : o + 1, :]
        a_o[:, lanes(o)] = onehot(f // T, T)
        hi, lo = hi_lo(at_via[o : o + 1, :] * wt[o : o + 1, :])
        on = colid == f % T
        hs.append(jnp.where(on, hi, 0.0))
        ls.append(jnp.where(on, lo, 0.0))
    lhs = jnp.concatenate(
        [jnp.concatenate(hs, axis=1), jnp.concatenate(ls, axis=1)], axis=0
    ).astype(BF16)
    inj = nt(lhs, a_o[...])
    inv = strips[8:16, :]
    z = strips[0:8, :] + (inj[0:8] + inj[8:16]) * inv
    low = iota((8, T), 0) < 4
    send_l[:, :T] = jnp.where(low, z, pltpu.roll(inv, 4, 0))
    send_r[:, :T] = jnp.where(low, pltpu.roll(z, 4, 0), inv)
    g, lane = iota((8, CB), 0), iota((8, CB), 1)
    send_l[:, T:] = nt(jnp.where(lane == g * GROUP, 1.0, 0.0), volt[...], HI)
    send_r[:, T:] = nt(jnp.where(lane == g * GROUP + GROUP - 1, 1.0, 0.0), volt[...], HI)


def rhs_kernel(vf, wt, at_via, zl, invd, a, z, rims, b_s):
    for o in range(NO):
        hi, lo = hi_lo(at_via[o : o + 1, :] * wt[o : o + 1, :])
        on = iota((T, L), 0) == vf[o : o + 1, :] % T
        b_s[:, lanes(o)] = jnp.where(on, hi, 0.0).astype(BF16)
        b_s[:, lanes(NO + o)] = jnp.where(on, lo, 0.0).astype(BF16)
    inj = nt(a[...], b_s[:, : NO * L]) + nt(a[...], b_s[:, NO * L :])
    zz = zl[...] + inj * invd[...]
    z[...] = zz
    rims[0:8, :] = zz[0:8]
    rims[8:16, :] = zz[T - 8 :]


def halo_columns(flags, gl, gr):
    left = jnp.where(flags[1] > 0, 1.0, 0.0)
    right = jnp.where(flags[1] < NO - 1, 1.0, 0.0)
    j, lane = iota((8, L), 0), iota((8, L), 1)
    zc = tn(gr, jnp.where((j < 4) & (lane == j), right, 0.0), HI) + tn(
        gl, jnp.where((j < 4) & (lane == 124 + j), left, 0.0), HI
    )
    ic = tn(gr, jnp.where((j >= 4) & (lane == j - 4), right, 0.0), HI) + tn(
        gl, jnp.where((j >= 4) & (lane == 120 + j), left, 0.0), HI
    )
    return zc, ic


def edge_kernel(flags, zr, ir, got_l, got_r, volt, send_u, send_d):
    zt, it = halo_columns(flags, got_l[:, :L], got_r[:, :L])
    zb, ib = halo_columns(flags, got_l[:, T - L : T], got_r[:, T - L : T])
    low = iota((8, W), 0) < 4
    zt = jnp.concatenate([zr[0:8, :], zt[0:8]], axis=1)
    it = jnp.concatenate([ir[0:8, :], it[0:8]], axis=1)
    zb = jnp.concatenate([zr[8:16, :], zb[L - 8 :]], axis=1)
    ib = jnp.concatenate([ir[8:16, :], ib[L - 8 :]], axis=1)
    send_u[:, :W] = jnp.where(low, zt, pltpu.roll(it, 4, 0))
    send_d[:, :W] = jnp.where(low, pltpu.roll(zb, 4, 0), ib)
    send_u[:, W:] = volt[0:8, :]
    send_d[:, W:] = volt[CB - 8 :, :]


def beside(block):
    n = block.shape[0]
    rows = pltpu.roll(block, 1, 0) + pltpu.roll(block, n - 1, 0)
    return rows + (pltpu.roll(block, 1, 1) + pltpu.roll(block, W - 1, 1))


def beside_mid(block):
    n = block.shape[0]
    mid = block[8 : n - 8]
    rows = pltpu.roll(block, 1, 0)[8 : n - 8] + pltpu.roll(block, n - 1, 0)[8 : n - 8]
    return mid, rows + (pltpu.roll(mid, 1, 1) + pltpu.roll(mid, W - 1, 1))


def fold(p):
    return (p[:, 0:128] + p[:, 128:256]) + (p[:, 256:384] + p[:, 384:512])


def gram_step(acc, zz, w, n1, n2, n3, inv):
    d = 1.0 / inv
    bw, bn1, bn2 = w - n1, n1 - n2, n2 - n3
    e = (zz - Q0 * w - Q1 * n1 - Q2 * n2, w, n1, n2)
    be = (w - Q0 * bw - Q1 * bn1 - Q2 * bn2, bw, bn1, bn2)
    new = []
    k = 0
    for p in range(4):
        de = d * e[p]
        for q in range(p, 4):
            new.append(acc[k] + fold(de * be[q]))
            k += 1
        new.append(acc[k] + fold(de * zz))
        k += 1
    return tuple(new)


def zeros14():
    return tuple(jnp.zeros((8, L), F32) for _ in range(14))


def basis_kernel(flags, z, invd, got_l, got_r, hist, acc_o, ie, ze, we, n1e, n2e, sem):
    zc, ic = halo_columns(flags, got_l[:, :T], got_r[:, :T])
    zero = jnp.zeros((OFF, W), F32)
    for e, own, col in ((ze, z, zc), (ie, invd, ic)):
        e[0:OFF, :] = zero
        e[OFF : OFF + T, :T] = own[...]
        e[OFF : OFF + T, T:] = col
        e[OFF + T :, :] = zero
    for e in (we, n1e, n2e):
        e[0:OFF, :] = zero
        e[OFF + T :, :] = zero
    rows = 32

    def save(k, e):
        copy = pltpu.make_async_copy(e.at[pl.ds(OFF, T), pl.ds(0, T)], hist.at[k], sem.at[k])
        copy.start()
        return copy

    def apply_to(src, dst, minus):
        def step(i, carry):
            start = pl.multiple_of(OFF + i * rows, 8)
            mid, near = beside_mid(src[pl.ds(start - 8, rows + 16), :])
            near = near * ie[pl.ds(start, rows), :]
            dst[pl.ds(start, rows), :] = mid - near if minus else near
            return carry

        lax.fori_loop(0, T // rows, step, 0)

    copies = [save(0, ze)]
    apply_to(ze, we, True)
    copies.append(save(1, we))
    apply_to(we, n1e, False)
    copies.append(save(2, n1e))
    apply_to(n1e, n2e, False)
    copies.append(save(3, n2e))

    def gram(i, acc):
        start = pl.multiple_of(OFF + i * 8, 8)
        mid, near = beside_mid(n2e[pl.ds(start - 8, 24), :])
        inv = ie[pl.ds(start, 8), :T]
        rows8 = pl.ds(start, 8)
        return gram_step(
            acc, ze[rows8, :T], we[rows8, :T], n1e[rows8, :T], mid[:, :T], near[:, :T] * inv, inv
        )

    acc = lax.fori_loop(1, T // 8 - 1, gram, zeros14())
    for k in range(14):
        acc_o[8 * k : 8 * k + 8, :] = acc[k]
    for copy in copies:
        copy.wait()


def rim_kernel(flags, z, invd, got_l, got_r, got_u, got_d, acc_i, rims, part):
    up = jnp.where(flags[0] > 0, 1.0, 0.0)
    down = jnp.where(flags[0] < 7, 1.0, 0.0)
    low = iota((8, W), 0) < 4
    acc = tuple(acc_i[8 * k : 8 * k + 8, :] for k in range(14))
    top, bot = got_u[:, :W], got_d[:, :W]
    for end in (0, 1):
        cols = slice(0, L) if end == 0 else slice(T - L, T)
        rows = slice(0, 16) if end == 0 else slice(T - 16, T)
        part_of = slice(0, 16) if end == 0 else slice(L - 16, L)
        zc, ic = halo_columns(flags, got_l[:, cols], got_r[:, cols])
        z16 = jnp.concatenate([z[rows, :], zc[part_of]], axis=1)
        i16 = jnp.concatenate([invd[rows, :], ic[part_of]], axis=1)
        if end == 0:
            zb = jnp.concatenate([jnp.where(low, 0.0, pltpu.roll(top, 4, 0)) * up, z16], axis=0)
            ib = jnp.concatenate([jnp.where(low, 0.0, top) * up, i16], axis=0)
            own = slice(8, 16)
        else:
            zb = jnp.concatenate([z16, jnp.where(low, bot, 0.0) * down], axis=0)
            ib = jnp.concatenate([i16, jnp.where(low, pltpu.roll(bot, 4, 0), 0.0) * down], axis=0)
            own = slice(8, 16)
        w = zb - ib * beside(zb)
        n1 = ib * beside(w)
        n2 = ib * beside(n1)
        n3 = ib * beside(n2)
        zo, wo, n1o, n2o, n3o, io = (x[own, :T] for x in (zb, w, n1, n2, n3, ib))
        acc = gram_step(acc, zo, wo, n1o, n2o, n3o, io)
        for k, x in enumerate((wo, n1o, n2o)):
            rims[16 * k + 8 * end : 16 * k + 8 * end + 8, :] = x
    rows14 = jnp.concatenate(
        [jnp.sum(a, axis=0, keepdims=True) for a in acc] + [jnp.zeros((L - 14, L), F32)], axis=0
    )
    sums = nt(jnp.ones((8, L), F32), rows14, HI)
    part[...] = sums


def gather_kernel(hist, rims, vf, wt, g_o, x_s, hl_s, c_s, a_s, sem):
    copies = [pltpu.make_async_copy(hist.at[k], x_s.at[k], sem.at[k]) for k in range(4)]
    for copy in copies:
        copy.start()
    for o in range(NO):
        f = vf[o : o + 1, :]
        c_s[:, lanes(o)] = onehot(f % T, T)
        a_s[:, lanes(o)] = onehot(f // T, T)
        g_o[8 * o + 4 : 8 * o + 8, :] = jnp.zeros((4, L), F32)
    for k in range(4):
        copies[k].wait()
        if k:
            x_s[k, 0:8, :] = rims[16 * k - 16 : 16 * k - 8, :]
            x_s[k, T - 8 :, :] = rims[16 * k - 8 : 16 * k, :]
        hi, lo = hi_lo(x_s[k])
        hl_s[0:T, :] = hi.astype(BF16)
        hl_s[T:, :] = lo.astype(BF16)
        for i in range(NO // 2):
            two = slice(2 * i * L, 2 * (i + 1) * L)
            sel = c_s[:, two]
            y = jnp.dot(hl_s[0:T, :], sel, preferred_element_type=F32) + jnp.dot(
                hl_s[T:, :], sel, preferred_element_type=F32
            )
            y = jnp.sum(y * a_s[:, two].astype(F32), axis=0, keepdims=True)
            for o in (2 * i, 2 * i + 1):
                g_o[8 * o + k : 8 * o + k + 1, :] = y[:, (o % 2) * L : (o % 2 + 1) * L] * wt[o : o + 1, :]


def pack_kernel(g, rows, out):
    out[...] = g[...]
    total = jnp.sum(rows[...], axis=0, keepdims=True)
    for o in range(NO):
        out[8 * o + 4 : 8 * o + 5, :] = total


def solve(tot):
    lane = iota((1, L), 1)

    def pick(k):
        return jnp.sum(jnp.where(lane == k, tot, 0.0), axis=1, keepdims=True)

    h, b = {}, []
    k = 0
    for p in range(4):
        for q in range(p, 4):
            h[p, q] = pick(k)
            k += 1
        b.append(pick(k))
        k += 1
    floor = [3e-7 * h[p, p] for p in range(4)]
    inv = []
    for p in range(4):
        inv.append(jnp.where(h[p, p] > floor[p], 1.0 / h[p, p], 0.0))
        for q in range(p + 1, 4):
            f = h[p, q] * inv[p]
            for r in range(q, 4):
                h[q, r] = h[q, r] - f * h[p, r]
            b[q] = b[q] - f * b[p]
    c = [None] * 4
    for p in (3, 2, 1, 0):
        s = b[p]
        for q in range(p + 1, 4):
            s = s - h[p, q] * c[q]
        c[p] = s * inv[p]
    return c[0], c[1] - Q0 * c[0], c[2] - Q1 * c[0], c[3] - Q2 * c[0]


def combine_kernel(coef, hist, rims, x_o):
    c = [coef[k : k + 1, 0:1] for k in range(4)]
    inner = slice(8, T - 8)
    x_o[inner, :] = (c[0] * hist[0, inner, :] + c[1] * hist[1, inner, :]) + (
        c[2] * hist[2, inner, :] + c[3] * hist[3, inner, :]
    )
    for end, rows in ((0, slice(0, 8)), (1, slice(T - 8, T))):
        x = c[0] * hist[0, rows, :]
        for k in range(3):
            x += c[k + 1] * rims[16 * k + 8 * end : 16 * k + 8 * end + 8, :]
        x_o[rows, :] = x


def coarse_neighbours(flags, u, above, below, from_l, from_r):
    up = jnp.where(flags[0] > 0, 1.0, 0.0)
    down = jnp.where(flags[0] < 7, 1.0, 0.0)
    r, lane = iota((CB, CB), 0), iota((CB, CB), 1)
    g, gl = iota((8, CB), 0), iota((8, CB), 1)
    turned_l = jnp.where(g == 0, 0.0, pltpu.roll(from_l, 1, 0))
    turned_r = jnp.where(g == 7, 0.0, pltpu.roll(from_r, 7, 0))
    from_l = jnp.where(flags[1] == 0, turned_l, from_l)
    from_r = jnp.where(flags[1] == NO - 1, turned_r, from_r)
    seam_l = tn(from_l, jnp.where(gl == g * GROUP, 1.0, 0.0), HI)
    seam_r = tn(from_r, jnp.where(gl == g * GROUP + GROUP - 1, 1.0, 0.0), HI)
    near = jnp.where(r == 0, above * up, pltpu.roll(u, 1, 0))
    near += jnp.where(r == CB - 1, below * down, pltpu.roll(u, CB - 1, 0))
    near += jnp.where(lane % GROUP == 0, seam_l, pltpu.roll(u, 1, 1))
    near += jnp.where(lane % GROUP == GROUP - 1, seam_r, pltpu.roll(u, CB - 1, 1))
    return near


def base_kernel(
    flags, held, volt, cleak, got_l, got_r, got_u, got_d, cdiag, scale, base, r_o, c_o
):
    for o in range(NO):
        h = held[o : o + 1, :]
        r_o[:, lanes(o)] = onehot(h >> 7, CB)
        c_o[:, lanes(o)] = onehot(h & (CB - 1), CB)
    count = nt(r_o[...], c_o[...])
    diag = 4.0 * coarse_conductance + cleak[...] + via_conductance * count
    u = volt[...]
    near = coarse_neighbours(flags, u, got_u[7:8, W:], got_d[0:1, W:], got_l[:, T:], got_r[:, T:])
    cdiag[...] = diag
    scale[...] = relaxation / diag
    base[...] = u - relaxation * (diag * u - coarse_conductance * near) / diag


def sweep1_kernel(arrived, scale, base, r, c, coef, u_o, src_o, sl, sr, su, sd, v_s):
    tot = arrived[4:5, :]
    for o in range(1, NO):
        tot += arrived[8 * o + 4 : 8 * o + 5, :]
    d = solve(tot)
    sub = iota((8, L), 0)
    cf = jnp.zeros((8, L), F32)
    for k in range(4):
        cf = jnp.where(sub == k, d[k], cf)
    coef[...] = cf
    for o in range(NO):
        v = jnp.sum(arrived[8 * o : 8 * o + 8, :] * cf, axis=0, keepdims=True)
        hi, lo = hi_lo(v)
        on = c[:, lanes(o)]
        v_s[:, lanes(o)] = on * hi.astype(BF16)
        v_s[:, lanes(NO + o)] = on * lo.astype(BF16)
    src = nt(r[...], v_s[:, : NO * L]) + nt(r[...], v_s[:, NO * L :])
    u = base[...] + scale[...] * src
    u_o[...] = u
    src_o[...] = src
    g, gl = iota((8, CB), 0), iota((8, CB), 1)
    sl[...] = nt(jnp.where(gl == g * GROUP, 1.0, 0.0), u, HI)
    sr[...] = nt(jnp.where(gl == g * GROUP + GROUP - 1, 1.0, 0.0), u, HI)
    su[...] = u[0:8, :]
    sd[...] = u[CB - 8 :, :]


def sweep2_kernel(flags, u, src, cdiag, scale, got_l, got_r, got_u, got_d, u_o):
    near = coarse_neighbours(flags, u[...], got_u[7:8, :], got_d[0:1, :], got_l[...], got_r[...])
    u_o[...] = u[...] + scale[...] * (src[...] - (cdiag[...] * u[...] - coarse_conductance * near))


VM = pl.BlockSpec(memory_space=pltpu.VMEM)
SM = pl.BlockSpec(memory_space=pltpu.SMEM)
ANY = pl.BlockSpec(memory_space=pltpu.HBM)
vmem = pltpu.MemorySpace.VMEM
hbm = jax.ShapeDtypeStruct


def keep(*args):
    return [pltpu.with_memory_space_constraint(x, pltpu.VMEM) for x in args]


def leave(*args):
    return [pltpu.with_memory_space_constraint(x, pltpu.HBM) for x in args]


def call(body, outs, args, scratch=(), flags=None, flops=0, any_in=0, any_out=0):
    specs = ([] if flags is None else [SM]) + [ANY] * any_in + [VM] * (len(args) - any_in)
    return pl.pallas_call(
        body,
        out_shape=outs,
        in_specs=specs,
        out_specs=[ANY] * any_out + [VM] * (len(outs) - any_out),
        scratch_shapes=list(scratch),
        cost_estimate=pl.CostEstimate(flops=flops, bytes_accessed=0, transcendentals=0),
        compiler_params=pltpu.CompilerParams(vmem_limit_bytes=20 * 2**20),
    )(*([] if flags is None else [flags]), *args)


def ring(axis):
    n = lax.axis_size(axis)
    up = [(i, (i + 1) % n) for i in range(n)]
    return up, [(b, a) for a, b in up]


def swap(axis, to_low, to_high):
    up, down = ring(axis)
    return lax.ppermute(to_high, axis, up), lax.ppermute(to_low, axis, down)


def spread(x, axis=COL):
    return lax.all_to_all(x, axis, split_axis=0, concat_axis=0, tiled=True)


def per_device(load_amp, load_mask, leak, coarse_leak, coarse_init, via_fine, via_coarse, via_count):
    flags = jnp.where(
        jnp.arange(2, dtype=jnp.int32) == 0, lax.axis_index(ROW), lax.axis_index(COL)
    ).astype(jnp.int32)
    live = jnp.arange(L, dtype=jnp.int32)[None, :] < via_count.reshape(NO, 1)
    wt = jnp.where(live, via_conductance, 0.0).astype(F32)
    fine = via_fine.reshape(NO, L)
    coarse = via_coarse.reshape(NO, L)
    request = jnp.where(live, ((coarse >> 11) << 7) | (coarse & (CB - 1)), -1)
    held = spread(request)

    tile, block, slots = vmem((T, T), F32), vmem((CB, CB), F32), vmem((NO, L), F32)
    hot, chot = vmem((T, NO * L), BF16), vmem((CB, NO * L), BF16)
    hots = vmem((T, 2 * NO * L), BF16)
    rim16, side, seam = vmem((16, T), F32), vmem((8, W), F32), vmem((8, CB), F32)
    ext, packed = vmem((EXT, W), F32), ((L, L), F32)
    dmas = pltpu.SemaphoreType.DMA((4,))
    big = 20_000_000_000

    zl, invd, strips, irims = call(
        diag_kernel, [tile, tile, rim16, rim16],
        keep(fine, wt) + leave(load_amp, load_mask, leak), [hot, hot], flops=big,
    )
    looked = call(lookup_kernel, [slots], keep(held, coarse_init))[0]
    at_via = spread(looked)
    a, send_l, send_r = call(
        strips_kernel, [hot, side, side], keep(fine, wt, at_via, strips, coarse_init)
    )
    got_l, got_r = swap(COL, send_l, send_r)
    z, zrims = call(
        rhs_kernel, [tile, rim16], keep(fine, wt, at_via, zl, invd, a), [hots], flops=big
    )
    rim = vmem((8, W + CB), F32)
    send_u, send_d = call(
        edge_kernel, [rim, rim], keep(zrims, irims, got_l, got_r, coarse_init), flags=flags
    )
    got_u, got_d = swap(ROW, send_u, send_d)
    hist, acc = call(
        basis_kernel, [pltpu.MemorySpace.HBM((4, T, T), F32), vmem((112, L), F32)], keep(z, invd, got_l, got_r),
        [ext] * 5 + [dmas], flags=flags, flops=big, any_out=1,
    )
    rims, part = call(
        rim_kernel, [vmem((48, T), F32), vmem((8, L), F32)],
        keep(z, invd, got_l, got_r, got_u, got_d, acc), flags=flags,
    )
    rows = spread(part, ROW)
    g = call(
        gather_kernel, [vmem(*packed)], leave(hist) + keep(rims, fine, wt),
        [vmem((4, T, T), F32), vmem((2 * T, T), BF16), hot, hot, dmas], flops=big, any_in=1,
    )[0]
    arrived = spread(call(pack_kernel, [vmem(*packed)], keep(g, rows))[0])
    cdiag, scale, base, r_hot, c_hot = call(
        base_kernel, [block, block, block, chot, chot],
        keep(held, coarse_init, coarse_leak, got_l, got_r, got_u, got_d), flags=flags, flops=big,
    )
    coef, u, src, sl, sr, su, sd = call(
        sweep1_kernel, [seam, block, block, seam, seam, seam, seam],
        keep(arrived, scale, base, r_hot, c_hot), [vmem((CB, 2 * NO * L), BF16)],
    )
    hl, hr = swap(COL, sl, sr)
    hu, hd = swap(ROW, su, sd)
    fine_drop = call(
        combine_kernel, [hbm((T, T), F32)], keep(coef) + leave(hist) + keep(rims), flops=big // 4
    )[0]
    coarse_drop = call(
        sweep2_kernel, [hbm((CB, CB), F32)], keep(u, src, cdiag, scale, hl, hr, hu, hd), flags=flags
    )[0]
    return fine_drop, coarse_drop


def solution(mesh):
    spec = P(ROW, COL)

    return jax.shard_map(
        per_device, mesh=mesh, in_specs=(spec,) * 8, out_specs=(spec, spec), check_vma=False
    )
```

time: 130 us -> 104 us (0.80)
  blocking collectives: 25.1 us -> 0 us
  starting transfers between devices: 28.9 us -> 42.9 us
  waiting for transfers between devices: 19 us -> 12 us
  Pallas kernels: 49.7 us -> 45.3 us
  local copies, waits for them, and re-layouts: 2.98 us -> 0.71 us
    all_to_all x2 -> x0, blocking collectives: 25.1 us -> none  [the longest x1 14.7 us: per_device(): lax.all_to_all(part, (ROW, COL), split_axis=0, concat_axis=0, tiled=True)]
    all_to_all x2 -> x4, starting transfers between devices: 11 us -> 24.9 us  [spread(): return lax.all_to_all(x, axis, split_axis=0, concat_axis=0, tiled=True)]
    ppermute x8, waiting for transfers between devices: 6.97 us -> 0.02 us  [swap(): return (lax.ppermute(to_high, axis, up), lax.ppermute(to_low, axis, down))]
    pallas_call x9 -> x13, Pallas kernels: 49.7 us -> 45.3 us  [call(): pl.pallas_call(body, out_shape=outs, in_specs=specs, out_specs=[ANY] * an...]
    unnamed x18 -> x8, local copies, waits for them, and re-layouts: 2.98 us -> 0.71 us
    all_to_all x2 -> x4, waiting for transfers between devices: 12.1 us -> 12 us  [spread(): return lax.all_to_all(x, axis, split_axis=0, concat_axis=0, tiled=True)]
  transfers between devices with their start and end apart: 10 -> 12, of which waited for: 6 -> 3; matrix products, arithmetic and copies ran while one was open for 0% -> 1% of each run, Pallas kernels for 5% -> 35%
where the time goes in v2:
time: 104 us
  Pallas kernels  45.3 us (44%)
  starting transfers between devices  42.9 us (41%)
  waiting for transfers between devices  12 us (12%)
  other arithmetic  2.12 us (2%)
    pallas_call x13, Pallas kernels, call(): pl.pallas_call(body, out_shape=outs, in_specs=specs, out_specs=[ANY] * an...  45.3 us
    all_to_all x4, starting transfers between devices, spread(): return lax.all_to_all(x, axis, split_axis=0, concat_axis=0, tiled=True)  24.9 us
    ppermute x8, starting transfers between devices, swap(): return (lax.ppermute(to_high, axis, up), lax.ppermute(to_low, axis, down))  18 us
    all_to_all x4, waiting for transfers between devices, spread(): return lax.all_to_all(x, axis, split_axis=0, concat_axis=0, tiled=True)  12 us
  transfers between devices with their start and end apart: 12, of which 3 were waited for; matrix products, arithmetic and copies ran while one was open for 1% of the time, Pallas kernels for 35%

profile of v2, /device:TPU:1, one launch (start us, length us, event | category | flops | bytes accessed | tf_op | source)
XLA Modules:
  0.0 103.8 jit_solution(7109589531602133228)
XLA Ops:
  0.6 1.4 %compare_select_fusion = s32[16,1,128]{2,1,0:T(1,128)} fusion(s32[1,2048]{1,0:T(1,128)} %param.14, s32[16]{0:T(128)} %bitcast.25), kind=kLoop, calls=%fused_computation | loop fusion | flops 12288 | bytes 16448 | tf_op jit(solution)/shard_map/jit(_where)/select_n | solution.py:479
  2.0 7.6 %all-to-all-start = ((s32[16,1,128]{2,1,0:T(1,128)}), s32[16,1,128]{2,1,0:T(1,128)S(1)}, u32[]{:S(2)}, u32[]{:S(2)}) async-start(s32[16,1,128]{2,1,0:T(1,128)} %compare_select_fusion), calls=%async_computation | async-start | bytes 16384 | tf_op jit(solution)/shard_map/all_to_all | solution.py:468
  9.6 0.7 fusion.wt
  11.0 4.7 %shard_map.96 = (f32[512,512]{1,0:T(8,128)S(1)}, f32[512,512]{1,0:T(8,128)S(1)}, f32[16,512]{1,0:T(8,128)S(1)}, f32[16,512]{1,0:T(8,128)S(1)}) custom-call(s32[16,128]{1,0:T(8,128)S(1)} %bitcast.21, f32[16,128]{1,0:T(8,128)S(1)} %fusion.wt, f32[512,512]{1,0:T(8,128)} %amp.1, s32[512,512]{1,0:T(8,128)} %mask.1, f32[512,512]{1,0:T(8,128)} %leak.1), custom_call_target="tpu_custom_call" | custom-call | flops 20000000000 | tf_op jit(solution)/shard_map/pallas_call | solution.py:445
  16.0 1.3 %shard_map.95 = f32[16,128]{1,0:T(8,128)} custom-call(s32[16,128]{1,0:T(8,128)S(1)} %bitcast.16, f32[128,128]{1,0:T(8,128)S(1)} %copy-done), custom_call_target="tpu_custom_call" | custom-call | tf_op jit(solution)/shard_map/pallas_call | solution.py:445
  17.2 6.5 %all-to-all-start.1 = ((f32[16,1,128]{2,1,0:T(1,128)}), f32[16,1,128]{2,1,0:T(1,128)S(1)}, u32[]{:S(2)}, u32[]{:S(2)}) async-start(f32[16,1,128]{2,1,0:T(1,128)} %bitcast.5), calls=%async_computation.1 | async-start | bytes 16384 | tf_op jit(solution)/shard_map/all_to_all | solution.py:468
  23.7 6.3 %all-to-all-done.1 = f32[16,1,128]{2,1,0:T(1,128)S(1)} async-done(((f32[16,1,128]{2,1,0:T(1,128)}), f32[16,1,128]{2,1,0:T(1,128)S(1)}, u32[]{:S(2)}, u32[]{:S(2)}) %all-to-all-start.1) | async-done | bytes 8224 | tf_op jit(solution)/shard_map/all_to_all | solution.py:468
  30.0 1.2 %shard_map.97 = (bf16[512,2048]{1,0:T(8,128)(2,1)S(1)}, f32[8,640]{1,0:T(8,128)S(1)}, f32[8,640]{1,0:T(8,128)S(1)}) custom-call(s32[16,128]{1,0:T(8,128)S(1)} %bitcast.22, f32[16,128]{1,0:T(8,128)S(1)} %fusion.wt, f32[16,128]{1,0:T(8,128)S(1)} %bitcast.18, f32[16,512]{1,0:T(8,128)S(1)} %get-tuple-element.31.strips, f32[128,128]{1,0:T(8,128)S(1)} %copy-done), custom_call_target="tpu_custom_call" | custom-call | tf_op jit(solution)/shard_map/pallas_call | solution.py:445
  31.5 4.5 %collective-permute-start.1 = (f32[8,640]{1,0:T(8,128)S(1)}, f32[8,640]{1,0:T(8,128)S(1)}, u32[]{:S(2)}, u32[]{:S(2)}) collective-permute-start(f32[8,640]{1,0:T(8,128)S(1)} %get-tuple-element.35), channel_id=1, source_target_pairs={{1,0},{2,1},{3,2},{4,3},{5,4},{6,5},{7,6},{8,7},{9,8},{10,9},{11,1... | collective-permute-start | bytes 61448 | tf_op jit(solution)/shard_map/ppermute | solution.py:464
  36.0 2.8 %shard_map.98 = (f32[512,512]{1,0:T(8,128)S(1)}, f32[16,512]{1,0:T(8,128)S(1)}) custom-call(s32[16,128]{1,0:T(8,128)S(1)} %bitcast.23, f32[16,128]{1,0:T(8,128)S(1)} %fusion.wt, f32[16,128]{1,0:T(8,128)S(1)} %bitcast.19, f32[512,512]{1,0:T(8,128)S(1)} %get-tuple-element.29.zl, f32[512,512]{1,0:T(8,128)S(1)} %get-tuple-element.30.invd, ...), custom_call_target="tpu_custom_call" | custom-call | flops 20000000000 | tf_op jit(solution)/shard_map/pallas_call | solution.py:445
  38.9 1.1 %shard_map.100 = (f32[8,768]{1,0:T(8,128)S(1)}, f32[8,768]{1,0:T(8,128)S(1)}) custom-call(s32[2]{0:T(128)S(1)} %compare_select_fusion.1.flags, f32[16,512]{1,0:T(8,128)S(1)} %get-tuple-element.37.zr, f32[16,512]{1,0:T(8,128)S(1)} %get-tuple-element.38.ir, f32[8,640]{1,0:T(8,128)S(1)} %collective-permute-done.got_l, ...), custom_call_target="tpu_custom_call" | custom-call | tf_op jit(solution)/shard_map/pallas_call | solution.py:445
  40.0 4.8 %collective-permute-start.2 = (f32[8,768]{1,0:T(8,128)S(1)}, f32[8,768]{1,0:T(8,128)S(1)}, u32[]{:S(2)}, u32[]{:S(2)}) collective-permute-start(f32[8,768]{1,0:T(8,128)S(1)} %get-tuple-element.39), channel_id=1, source_target_pairs={{0,16},{16,32},{32,48},{48,64},{64,80},{80,96},{96,112},{112,0},{1... | collective-permute-start | bytes 73736 | tf_op jit(solution)/shard_map/ppermute | solution.py:464
  44.8 12.9 %shard_map.99 = (f32[4,512,512]{2,1,0:T(8,128)}, f32[112,128]{1,0:T(8,128)S(1)}) custom-call(s32[2]{0:T(128)S(1)} %compare_select_fusion.1.flags, f32[512,512]{1,0:T(8,128)S(1)} %get-tuple-element.33.z, f32[512,512]{1,0:T(8,128)S(1)} %get-tuple-element.30.invd, f32[8,640]{1,0:T(8,128)S(1)} %collective-permute-done.got_l, ...), custom_call_target="tpu_custom_call" | custom-call | flops 20000000000 | tf_op jit(solution)/shard_map/pallas_call | solution.py:445
  57.7 2.2 %shard_map.101 = (f32[48,512]{1,0:T(8,128)S(1)}, f32[8,128]{1,0:T(8,128)}) custom-call(s32[2]{0:T(128)S(1)} %compare_select_fusion.1.flags, f32[512,512]{1,0:T(8,128)S(1)} %get-tuple-element.33.z, f32[512,512]{1,0:T(8,128)S(1)} %get-tuple-element.30.invd, f32[8,640]{1,0:T(8,128)S(1)} %collective-permute-done.got_l, ...), custom_call_target="tpu_custom_call" | custom-call | tf_op jit(solution)/shard_map/pallas_call | solution.py:445
  59.9 5.5 %all-to-all-start.2 = ((f32[8,1,128]{2,1,0:T(1,128)}), f32[8,1,128]{2,1,0:T(1,128)S(1)}, u32[]{:S(2)}, u32[]{:S(2)}) async-start(f32[8,1,128]{2,1,0:T(1,128)} %bitcast.8), calls=%async_computation.2 | async-start | bytes 8192 | tf_op jit(solution)/shard_map/all_to_all | solution.py:468
  65.5 10.8 %shard_map.102.g = f32[128,128]{1,0:T(8,128)S(1)} custom-call(f32[4,512,512]{2,1,0:T(8,128)} %get-tuple-element.36.hist, f32[48,512]{1,0:T(8,128)S(1)} %get-tuple-element.42.rims, s32[16,128]{1,0:T(8,128)S(1)} %bitcast.24, f32[16,128]{1,0:T(8,128)S(1)} %fusion.wt), custom_call_target="tpu_custom_call" | custom-call | flops 20000000000 | tf_op jit(solution)/shard_map/pallas_call | solution.py:445
  76.9 5.4 %all-to-all-start.3 = ((f32[16,8,128]{2,1,0:T(8,128)}), f32[16,8,128]{2,1,0:T(8,128)S(1)}, u32[]{:S(2)}, u32[]{:S(2)}) async-start(f32[16,8,128]{2,1,0:T(8,128)} %bitcast.10), calls=%async_computation.3 | async-start | bytes 131072 | tf_op jit(solution)/shard_map/all_to_all | solution.py:468
  82.3 1.1 %shard_map.104 = (f32[128,128]{1,0:T(8,128)S(1)}, f32[128,128]{1,0:T(8,128)S(1)}, f32[128,128]{1,0:T(8,128)S(1)}, bf16[128,2048]{1,0:T(8,128)(2,1)S(1)}, bf16[128,2048]{1,0:T(8,128)(2,1)S(1)}) custom-call(s32[2]{0:T(128)S(1)} %compare_select_fusion.1.flags, s32[16,128]{1,0:T(8,128)S(1)} %bitcast.17, f32[128,128]{1,0:T(8,128)S(1)} %copy-done, ...), custom_call_target="tpu_custom_call" | custom-call | flops 20000000000 | tf_op jit(solution)/shard_map/pallas_call | solution.py:445
  83.4 5.4 %all-to-all-done.3 = f32[16,8,128]{2,1,0:T(8,128)S(1)} async-done(((f32[16,8,128]{2,1,0:T(8,128)}), f32[16,8,128]{2,1,0:T(8,128)S(1)}, u32[]{:S(2)}, u32[]{:S(2)}) %all-to-all-start.3) | async-done | bytes 65568 | tf_op jit(solution)/shard_map/all_to_all | solution.py:468
  88.8 1.3 %shard_map.105 = (f32[8,128]{1,0:T(8,128)S(1)}, f32[128,128]{1,0:T(8,128)S(1)}, f32[128,128]{1,0:T(8,128)S(1)}, f32[8,128]{1,0:T(8,128)S(1)}, f32[8,128]{1,0:T(8...) custom-call(f32[128,128]{1,0:T(8,128)S(1)} %bitcast.15, f32[128,128]{1,0:T(8,128)S(1)} %get-tuple-element.44.scale, ...), custom_call_target="tpu_custom_call" | custom-call | tf_op jit(solution)/shard_map/pallas_call | solution.py:445
  90.4 4.5 %collective-permute-start.5 = (f32[8,128]{1,0:T(8,128)S(1)}, f32[8,128]{1,0:T(8,128)S(1)}, u32[]{:S(2)}, u32[]{:S(2)}) collective-permute-start(f32[8,128]{1,0:T(8,128)S(1)} %get-tuple-element.53), channel_id=1, source_target_pairs={{1,0},{2,1},{3,2},{4,3},{5,4},{6,5},{7,6},{8,7},{9,8},{10,9},{11,1... | collective-permute-start | bytes 12296 | tf_op jit(solution)/shard_map/ppermute | solution.py:464
  94.9 3.6 %collective-permute-start.6 = (f32[8,128]{1,0:T(8,128)S(1)}, f32[8,128]{1,0:T(8,128)S(1)}, u32[]{:S(2)}, u32[]{:S(2)}) collective-permute-start(f32[8,128]{1,0:T(8,128)S(1)} %get-tuple-element.54), channel_id=1, source_target_pairs={{0,16},{16,32},{32,48},{48,64},{64,80},{80,96},{96,112},{112,0},{1... | collective-permute-start | bytes 12296 | tf_op jit(solution)/shard_map/ppermute | solution.py:464
  98.5 3.7 %shard_map.106 = f32[512,512]{1,0:T(8,128)} custom-call(f32[8,128]{1,0:T(8,128)S(1)} %get-tuple-element.48.coef, f32[4,512,512]{2,1,0:T(8,128)} %get-tuple-element.36.hist, f32[48,512]{1,0:T(8,128)S(1)} %get-tuple-element.42.rims), custom_call_target="tpu_custom_call" | custom-call | flops 5000000000 | tf_op jit(solution)/shard_map/pallas_call | solution.py:445
  102.3 1.5 %shard_map.107 = f32[128,128]{1,0:T(8,128)} custom-call(s32[2]{0:T(128)S(1)} %compare_select_fusion.1.flags, f32[128,128]{1,0:T(8,128)S(1)} %get-tuple-element.49.u, f32[128,128]{1,0:T(8,128)S(1)} %get-tuple-element.50.src, f32[128,128]{1,0:T(8,128)S(1)} %get-tuple-element.51.cdiag, f32[128,128]{1,0:T(8,128)S(1)} %get-tuple-element.44.scale, ...), custom_call_target="tpu_custom_call" | custom-call | tf_op jit(solution)/shard_map/pallas_call | solution.py:445
  (24 shorter events, 2.3 us)
Async XLA Ops:
  2.0 13.9 %all-to-all-start = ((s32[16,1,128]{2,1,0:T(1,128)}), s32[16,1,128]{2,1,0:T(1,128)S(1)}, u32[]{:S(2)}, u32[]{:S(2)}) async-start(s32[16,1,128]{2,1,0:T(1,128)} %compare_select_fusion), calls=%async_computation | async-start | bytes 16384 | tf_op jit(solution)/shard_map/all_to_all | solution.py:468
  10.3 0.7 copy-start.1
  11.0 4.9 %copy-start = (f32[128,128]{1,0:T(8,128)S(1)}, f32[128,128]{1,0:T(8,128)}, u32[]{:S(2)}) copy-start(f32[128,128]{1,0:T(8,128)} %volt.7) | copy-start | bytes 196612
  11.0 19.0 %copy-start.2 = (s32[1,2048]{1,0:T(1,128)S(1)}, s32[1,2048]{1,0:T(1,128)}, u32[]{:S(2)}) copy-start(s32[1,2048]{1,0:T(1,128)} %param.13) | copy-start | bytes 24580
  17.2 12.8 %all-to-all-start.1 = ((f32[16,1,128]{2,1,0:T(1,128)}), f32[16,1,128]{2,1,0:T(1,128)S(1)}, u32[]{:S(2)}, u32[]{:S(2)}) async-start(f32[16,1,128]{2,1,0:T(1,128)} %bitcast.5), calls=%async_computation.1 | async-start | bytes 16384 | tf_op jit(solution)/shard_map/all_to_all | solution.py:468
  31.2 7.6 %collective-permute-start = (f32[8,640]{1,0:T(8,128)S(1)}, f32[8,640]{1,0:T(8,128)S(1)}, u32[]{:S(2)}, u32[]{:S(2)}) collective-permute-start(f32[8,640]{1,0:T(8,128)S(1)} %get-tuple-element.34), channel_id=1, source_target_pairs={{0,1},{1,2},{2,3},{3,4},{4,5},{5,6},{6,7},{7,8},{8,9},{9,10},{10,1... | collective-permute-start | bytes 61448 | tf_op jit(solution)/shard_map/ppermute | solution.py:464
  31.5 7.3 %collective-permute-start.1 = (f32[8,640]{1,0:T(8,128)S(1)}, f32[8,640]{1,0:T(8,128)S(1)}, u32[]{:S(2)}, u32[]{:S(2)}) collective-permute-start(f32[8,640]{1,0:T(8,128)S(1)} %get-tuple-element.35), channel_id=1, source_target_pairs={{1,0},{2,1},{3,2},{4,3},{5,4},{6,5},{7,6},{8,7},{9,8},{10,9},{11,1... | collective-permute-start | bytes 61448 | tf_op jit(solution)/shard_map/ppermute | solution.py:464
  40.0 17.7 %collective-permute-start.2 = (f32[8,768]{1,0:T(8,128)S(1)}, f32[8,768]{1,0:T(8,128)S(1)}, u32[]{:S(2)}, u32[]{:S(2)}) collective-permute-start(f32[8,768]{1,0:T(8,128)S(1)} %get-tuple-element.39), channel_id=1, source_target_pairs={{0,16},{16,32},{32,48},{48,64},{64,80},{80,96},{96,112},{112,0},{1... | collective-permute-start | bytes 73736 | tf_op jit(solution)/shard_map/ppermute | solution.py:464
  44.8 12.9 %collective-permute-start.3 = (f32[8,768]{1,0:T(8,128)S(1)}, f32[8,768]{1,0:T(8,128)S(1)}, u32[]{:S(2)}, u32[]{:S(2)}) collective-permute-start(f32[8,768]{1,0:T(8,128)S(1)} %get-tuple-element.40), channel_id=1, source_target_pairs={{16,0},{32,16},{48,32},{64,48},{80,64},{96,80},{112,96},{0,112},{1... | collective-permute-start | bytes 73736 | tf_op jit(solution)/shard_map/ppermute | solution.py:464
  59.9 16.3 %all-to-all-start.2 = ((f32[8,1,128]{2,1,0:T(1,128)}), f32[8,1,128]{2,1,0:T(1,128)S(1)}, u32[]{:S(2)}, u32[]{:S(2)}) async-start(f32[8,1,128]{2,1,0:T(1,128)} %bitcast.8), calls=%async_computation.2 | async-start | bytes 8192 | tf_op jit(solution)/shard_map/all_to_all | solution.py:468
  65.5 16.8 %copy-start.3 = (f32[128,128]{1,0:T(8,128)S(1)}, f32[128,128]{1,0:T(8,128)}, u32[]{:S(2)}) copy-start(f32[128,128]{1,0:T(8,128)} %cleak.1) | copy-start | bytes 196612
  76.9 11.9 %all-to-all-start.3 = ((f32[16,8,128]{2,1,0:T(8,128)}), f32[16,8,128]{2,1,0:T(8,128)S(1)}, u32[]{:S(2)}, u32[]{:S(2)}) async-start(f32[16,8,128]{2,1,0:T(8,128)} %bitcast.10), calls=%async_computation.3 | async-start | bytes 131072 | tf_op jit(solution)/shard_map/all_to_all | solution.py:468
  90.1 12.2 %collective-permute-start.4 = (f32[8,128]{1,0:T(8,128)S(1)}, f32[8,128]{1,0:T(8,128)S(1)}, u32[]{:S(2)}, u32[]{:S(2)}) collective-permute-start(f32[8,128]{1,0:T(8,128)S(1)} %get-tuple-element.52), channel_id=1, source_target_pairs={{0,1},{1,2},{2,3},{3,4},{4,5},{5,6},{6,7},{7,8},{8,9},{9,10},{10,1... | collective-permute-start | bytes 12296 | tf_op jit(solution)/shard_map/ppermute | solution.py:464
  90.4 11.8 %collective-permute-start.5 = (f32[8,128]{1,0:T(8,128)S(1)}, f32[8,128]{1,0:T(8,128)S(1)}, u32[]{:S(2)}, u32[]{:S(2)}) collective-permute-start(f32[8,128]{1,0:T(8,128)S(1)} %get-tuple-element.53), channel_id=1, source_target_pairs={{1,0},{2,1},{3,2},{4,3},{5,4},{6,5},{7,6},{8,7},{9,8},{10,9},{11,1... | collective-permute-start | bytes 12296 | tf_op jit(solution)/shard_map/ppermute | solution.py:464
  94.9 7.3 %collective-permute-start.6 = (f32[8,128]{1,0:T(8,128)S(1)}, f32[8,128]{1,0:T(8,128)S(1)}, u32[]{:S(2)}, u32[]{:S(2)}) collective-permute-start(f32[8,128]{1,0:T(8,128)S(1)} %get-tuple-element.54), channel_id=1, source_target_pairs={{0,16},{16,32},{32,48},{48,64},{64,80},{80,96},{96,112},{112,0},{1... | collective-permute-start | bytes 12296 | tf_op jit(solution)/shard_map/ppermute | solution.py:464
  98.5 3.7 %collective-permute-start.7 = (f32[8,128]{1,0:T(8,128)S(1)}, f32[8,128]{1,0:T(8,128)S(1)}, u32[]{:S(2)}, u32[]{:S(2)}) collective-permute-start(f32[8,128]{1,0:T(8,128)S(1)} %get-tuple-element.55), channel_id=1, source_target_pairs={{16,0},{32,16},{48,32},{64,48},{80,64},{96,80},{112,96},{0,112},{1... | collective-permute-start | bytes 12296 | tf_op jit(solution)/shard_map/ppermute | solution.py:464

commit v3 on v2

--- a/solution.py
+++ b/solution.py
@@ -24,7 +24,12 @@
 EXT = OFF + T + 16
 W = T + L
 
-Q0, Q1, Q2 = 1.08976773, 1.76773384, 1.28562461
+Q = (1.08976773, 1.76773384, 1.28562461)
+RHO = (1.0 - Q[0], Q[0] - Q[1], Q[1] - Q[2], Q[2])
+LT = T // L
+SLAB = 4 * LT + 1
+SUMS = 8
+STEPS = 4
 
 
 def iota(shape, dim):
@@ -159,62 +164,57 @@
     return rows + (pltpu.roll(block, 1, 1) + pltpu.roll(block, W - 1, 1))
 
 
-def beside_mid(block):
-    n = block.shape[0]
-    mid = block[8 : n - 8]
-    rows = pltpu.roll(block, 1, 0)[8 : n - 8] + pltpu.roll(block, n - 1, 0)[8 : n - 8]
-    return mid, rows + (pltpu.roll(mid, 1, 1) + pltpu.roll(mid, W - 1, 1))
+def near_tiles(ref, start, rows):
+    mid = [ref[t, pl.ds(start, rows), :] for t in range(LT + 1)]
+    low = [pltpu.roll(m, 1, 1) for m in mid]
+    high = [pltpu.roll(m, L - 1, 1) for m in mid]
+    lane = iota((rows, L), 1)
+    near = []
+    for t in range(LT + 1):
+        rows_sum = ref[t, pl.ds(start - 1, rows), :] + ref[t, pl.ds(start + 1, rows), :]
+        left = jnp.where(lane == 0, low[t - 1], low[t])
+        right = jnp.where(lane == L - 1, high[(t + 1) % (LT + 1)], high[t])
+        near.append(rows_sum + (left + right))
+    return mid, near
 
 
 def fold(p):
     return (p[:, 0:128] + p[:, 128:256]) + (p[:, 256:384] + p[:, 384:512])
 
 
-def gram_step(acc, zz, w, n1, n2, n3, inv):
+def moments(z, w, n1, n2, dn3, inv):
     d = 1.0 / inv
-    bw, bn1, bn2 = w - n1, n1 - n2, n2 - n3
-    e = (zz - Q0 * w - Q1 * n1 - Q2 * n2, w, n1, n2)
-    be = (w - Q0 * bw - Q1 * bn1 - Q2 * bn2, bw, bn1, bn2)
-    new = []
-    k = 0
-    for p in range(4):
-        de = d * e[p]
-        for q in range(p, 4):
-            new.append(acc[k] + fold(de * be[q]))
-            k += 1
-        new.append(acc[k] + fold(de * zz))
-        k += 1
-    return tuple(new)
-
-
-def zeros14():
-    return tuple(jnp.zeros((8, L), F32) for _ in range(14))
+    dz, dw, dn1, dn2 = d * z, d * w, d * n1, d * n2
+    return dz * z, dz * w, dw * w, dw * n1, dn1 * n1, dn1 * n2, dn2 * n2, n2 * dn3
 
 
 def basis_kernel(flags, z, invd, got_l, got_r, hist, acc_o, ie, ze, we, n1e, n2e, sem):
     zc, ic = halo_columns(flags, got_l[:, :T], got_r[:, :T])
-    zero = jnp.zeros((OFF, W), F32)
-    for e, own, col in ((ze, z, zc), (ie, invd, ic)):
-        e[0:OFF, :] = zero
-        e[OFF : OFF + T, :T] = own[...]
-        e[OFF : OFF + T, T:] = col
-        e[OFF + T :, :] = zero
-    for e in (we, n1e, n2e):
-        e[0:OFF, :] = zero
-        e[OFF + T :, :] = zero
-    rows = 32
+    zero = jnp.zeros((OFF, L), F32)
+    own = pl.ds(OFF, T)
+    for e in (ie, ze, we, n1e, n2e):
+        for t in range(LT + 1):
+            e[t, 0:OFF, :] = zero
+            e[t, OFF + T :, :] = zero
+    for t in range(LT):
+        ze[t, own, :] = z[:, lanes(t)]
+        ie[t, own, :] = invd[:, lanes(t)]
+    ze[LT, own, :] = zc
+    ie[LT, own, :] = ic
+    rows = 16
 
     def save(k, e):
-        copy = pltpu.make_async_copy(e.at[pl.ds(OFF, T), pl.ds(0, T)], hist.at[k], sem.at[k])
+        copy = pltpu.make_async_copy(e.at[pl.ds(0, LT), own, :], hist.at[k], sem.at[k])
         copy.start()
         return copy
 
     def apply_to(src, dst, minus):
         def step(i, carry):
             start = pl.multiple_of(OFF + i * rows, 8)
-            mid, near = beside_mid(src[pl.ds(start - 8, rows + 16), :])
-            near = near * ie[pl.ds(start, rows), :]
-            dst[pl.ds(start, rows), :] = mid - near if minus else near
+            mid, near = near_tiles(src, start, rows)
+            for t in range(LT + 1):
+                y = near[t] * ie[t, pl.ds(start, rows), :]
+                dst[t, pl.ds(start, rows), :] = mid[t] - y if minus else y
             return carry
 
         lax.fori_loop(0, T // rows, step, 0)
@@ -229,15 +229,18 @@
 
     def gram(i, acc):
         start = pl.multiple_of(OFF + i * 8, 8)
-        mid, near = beside_mid(n2e[pl.ds(start - 8, 24), :])
-        inv = ie[pl.ds(start, 8), :T]
-        rows8 = pl.ds(start, 8)
-        return gram_step(
-            acc, ze[rows8, :T], we[rows8, :T], n1e[rows8, :T], mid[:, :T], near[:, :T] * inv, inv
-        )
-
-    acc = lax.fori_loop(1, T // 8 - 1, gram, zeros14())
-    for k in range(14):
+        n2, dn3 = near_tiles(n2e, start, 8)
+        acc = list(acc)
+        for t in range(LT):
+            z8, w8, n18, i8 = (e[t, pl.ds(start, 8), :] for e in (ze, we, n1e, ie))
+            for k, p in enumerate(moments(z8, w8, n18, n2[t], dn3[t], i8)):
+                acc[k] = acc[k] + p
+        return tuple(acc)
+
+    acc = lax.fori_loop(
+        1, T // 8 - 1, gram, tuple(jnp.zeros((8, L), F32) for _ in range(SUMS))
+    )
+    for k in range(SUMS):
         acc_o[8 * k : 8 * k + 8, :] = acc[k]
     for copy in copies:
         copy.wait()
@@ -247,7 +250,7 @@
     up = jnp.where(flags[0] > 0, 1.0, 0.0)
     down = jnp.where(flags[0] < 7, 1.0, 0.0)
     low = iota((8, W), 0) < 4
-    acc = tuple(acc_i[8 * k : 8 * k + 8, :] for k in range(14))
+    acc = [acc_i[8 * k : 8 * k + 8, :] for k in range(SUMS)]
     top, bot = got_u[:, :W], got_d[:, :W]
     for end in (0, 1):
         cols = slice(0, L) if end == 0 else slice(T - L, T)
@@ -267,44 +270,57 @@
         w = zb - ib * beside(zb)
         n1 = ib * beside(w)
         n2 = ib * beside(n1)
-        n3 = ib * beside(n2)
-        zo, wo, n1o, n2o, n3o, io = (x[own, :T] for x in (zb, w, n1, n2, n3, ib))
-        acc = gram_step(acc, zo, wo, n1o, n2o, n3o, io)
+        near = beside(n2)
+        zo, wo, n1o, n2o, dn3, io = (x[own, :T] for x in (zb, w, n1, n2, near, ib))
+        for k, p in enumerate(moments(zo, wo, n1o, n2o, dn3, io)):
+            acc[k] = acc[k] + fold(p)
         for k, x in enumerate((wo, n1o, n2o)):
             rims[16 * k + 8 * end : 16 * k + 8 * end + 8, :] = x
-    rows14 = jnp.concatenate(
-        [jnp.sum(a, axis=0, keepdims=True) for a in acc] + [jnp.zeros((L - 14, L), F32)], axis=0
-    )
-    sums = nt(jnp.ones((8, L), F32), rows14, HI)
+    rows8 = jnp.concatenate(
+        [jnp.sum(a, axis=0, keepdims=True) for a in acc] + [jnp.zeros((L - SUMS, L), F32)], axis=0
+    )
+    sums = nt(jnp.ones((8, L), F32), rows8, HI)
     part[...] = sums
 
 
-def gather_kernel(hist, rims, vf, wt, g_o, x_s, hl_s, c_s, a_s, sem):
+def gather_kernel(slots, hist, rims, vf, wt, g_o, x_s, slab, sem):
     copies = [pltpu.make_async_copy(hist.at[k], x_s.at[k], sem.at[k]) for k in range(4)]
     for copy in copies:
         copy.start()
-    for o in range(NO):
-        f = vf[o : o + 1, :]
-        c_s[:, lanes(o)] = onehot(f % T, T)
-        a_s[:, lanes(o)] = onehot(f // T, T)
-        g_o[8 * o + 4 : 8 * o + 8, :] = jnp.zeros((4, L), F32)
     for k in range(4):
         copies[k].wait()
         if k:
-            x_s[k, 0:8, :] = rims[16 * k - 16 : 16 * k - 8, :]
-            x_s[k, T - 8 :, :] = rims[16 * k - 8 : 16 * k, :]
-        hi, lo = hi_lo(x_s[k])
-        hl_s[0:T, :] = hi.astype(BF16)
-        hl_s[T:, :] = lo.astype(BF16)
-        for i in range(NO // 2):
-            two = slice(2 * i * L, 2 * (i + 1) * L)
-            sel = c_s[:, two]
-            y = jnp.dot(hl_s[0:T, :], sel, preferred_element_type=F32) + jnp.dot(
-                hl_s[T:, :], sel, preferred_element_type=F32
-            )
-            y = jnp.sum(y * a_s[:, two].astype(F32), axis=0, keepdims=True)
-            for o in (2 * i, 2 * i + 1):
-                g_o[8 * o + k : 8 * o + k + 1, :] = y[:, (o % 2) * L : (o % 2 + 1) * L] * wt[o : o + 1, :]
+            for t in range(LT):
+                x_s[k, t, 0:8, :] = rims[16 * k - 16 : 16 * k - 8, lanes(t)]
+                x_s[k, t, T - 8 :, :] = rims[16 * k - 8 : 16 * k, lanes(t)]
+
+        def lay(i, carry):
+            for b in range(4):
+                for t in range(LT):
+                    start = pl.multiple_of(i * 32 + 8 * b, 8)
+                    to = (i * 32 + 8 * b) * SLAB + 4 * k + t
+                    slab[pl.ds(to, 8, stride=SLAB), :] = x_s[k, t, pl.ds(start, 8), :]
+            return carry
+
+        lax.fori_loop(0, T // 32, lay, 0)
+    lane, sub = iota((16, L), 1), iota((16, L), 0)
+
+    def owner(o, carry):
+        acc = jnp.zeros((16, L), F32)
+        for j in range(L):
+            node = slots[o, j]
+            x = slab[pl.ds((node >> 9) * SLAB, 16), :]
+            x = pltpu.roll(x, (j - node) & (L - 1), 1)
+            acc = jnp.where(lane == j, x, acc)
+        f = vf[pl.ds(o, 1), :]
+        acc = jnp.where((sub & 3) == ((f >> 7) & 3), acc * wt[pl.ds(o, 1), :], 0.0)
+        rows = [jnp.sum(acc[4 * k : 4 * k + 4, :], axis=0, keepdims=True) for k in range(4)]
+        g_o[pl.ds(pl.multiple_of(8 * o, 8), 8), :] = jnp.concatenate(
+            rows + [jnp.zeros((4, L), F32)], axis=0
+        )
+        return carry
+
+    lax.fori_loop(0, NO, owner, 0)
 
 
 def pack_kernel(g, rows, out):
@@ -320,14 +336,22 @@
     def pick(k):
         return jnp.sum(jnp.where(lane == k, tot, 0.0), axis=1, keepdims=True)
 
-    h, b = {}, []
-    k = 0
-    for p in range(4):
-        for q in range(p, 4):
-            h[p, q] = pick(k)
-            k += 1
-        b.append(pick(k))
-        k += 1
+    g0, q0 = pick(0), pick(1)
+    m = [pick(2 + k) for k in range(6)]
+    r = [q0, q0 - m[0], q0 - m[0] - m[1]]
+    h = {(0, 0): q0, **{(0, j): RHO[0] * m[j - 1] for j in (1, 2, 3)}}
+    b = [g0] + r
+    for k in range(3):
+        h[0, 0] = h[0, 0] - Q[k] * m[k]
+        b[0] = b[0] - Q[k] * r[k]
+    for k in range(6):
+        f = sum(Q[j] * RHO[k - j] for j in range(3) if 0 <= k - j < 4)
+        h[0, 0] = h[0, 0] - f * m[k]
+    for j in (1, 2, 3):
+        for k in (1, 2, 3):
+            h[0, j] = h[0, j] + RHO[k] * m[j - 1 + k]
+            if j <= k:
+                h[j, k] = m[j + k - 2] - m[j + k - 1]
     floor = [3e-7 * h[p, p] for p in range(4)]
     inv = []
     for p in range(4):
@@ -343,20 +367,25 @@
         for q in range(p + 1, 4):
             s = s - h[p, q] * c[q]
         c[p] = s * inv[p]
-    return c[0], c[1] - Q0 * c[0], c[2] - Q1 * c[0], c[3] - Q2 * c[0]
+    return [c[0]] + [c[k + 1] - Q[k] * c[0] for k in range(3)]
 
 
 def combine_kernel(coef, hist, rims, x_o):
     c = [coef[k : k + 1, 0:1] for k in range(4)]
-    inner = slice(8, T - 8)
-    x_o[inner, :] = (c[0] * hist[0, inner, :] + c[1] * hist[1, inner, :]) + (
-        c[2] * hist[2, inner, :] + c[3] * hist[3, inner, :]
-    )
-    for end, rows in ((0, slice(0, 8)), (1, slice(T - 8, T))):
-        x = c[0] * hist[0, rows, :]
-        for k in range(3):
-            x += c[k + 1] * rims[16 * k + 8 * end : 16 * k + 8 * end + 8, :]
-        x_o[rows, :] = x
+    i = pl.program_id(0)
+    for t in range(LT):
+        x_o[:, lanes(t)] = (c[0] * hist[0, t] + c[1] * hist[1, t]) + (
+            c[2] * hist[2, t] + c[3] * hist[3, t]
+        )
+    for end, step, rows in ((0, 0, slice(0, 8)), (1, STEPS - 1, slice(T // STEPS - 8, T // STEPS))):
+
+        @pl.when(i == step)
+        def _(end=end, rows=rows):
+            for t in range(LT):
+                x = c[0] * hist[0, t, rows, :]
+                for k in range(3):
+                    x += c[k + 1] * rims[16 * k + 8 * end : 16 * k + 8 * end + 8, lanes(t)]
+                x_o[rows, lanes(t)] = x
 
 
 def coarse_neighbours(flags, u, above, below, from_l, from_r):
@@ -483,7 +512,7 @@
     hot, chot = vmem((T, NO * L), BF16), vmem((CB, NO * L), BF16)
     hots = vmem((T, 2 * NO * L), BF16)
     rim16, side, seam = vmem((16, T), F32), vmem((8, W), F32), vmem((8, CB), F32)
-    ext, packed = vmem((EXT, W), F32), ((L, L), F32)
+    ext, packed = vmem((LT + 1, EXT, L), F32), ((L, L), F32)
     dmas = pltpu.SemaphoreType.DMA((4,))
     big = 20_000_000_000
 
@@ -506,7 +535,7 @@
     )
     got_u, got_d = swap(ROW, send_u, send_d)
     hist, acc = call(
-        basis_kernel, [pltpu.MemorySpace.HBM((4, T, T), F32), vmem((112, L), F32)], keep(z, invd, got_l, got_r),
+        basis_kernel, [pltpu.MemorySpace.HBM((4, LT, T, L), F32), vmem((8 * SUMS, L), F32)], keep(z, invd, got_l, got_r),
         [ext] * 5 + [dmas], flags=flags, flops=big, any_out=1,
     )
     rims, part = call(
@@ -516,7 +545,7 @@
     rows = spread(part, ROW)
     g = call(
         gather_kernel, [vmem(*packed)], leave(hist) + keep(rims, fine, wt),
-        [vmem((4, T, T), F32), vmem((2 * T, T), BF16), hot, hot, dmas], flops=big, any_in=1,
+        [vmem((4, LT, T, L), F32), vmem((T * SLAB, L), F32), dmas], flags=fine, flops=big, any_in=1,
     )[0]
     arrived = spread(call(pack_kernel, [vmem(*packed)], keep(g, rows))[0])
     cdiag, scale, base, r_hot, c_hot = call(
@@ -529,9 +558,19 @@
     )
     hl, hr = swap(COL, sl, sr)
     hu, hd = swap(ROW, su, sd)
-    fine_drop = call(
-        combine_kernel, [hbm((T, T), F32)], keep(coef) + leave(hist) + keep(rims), flops=big // 4
-    )[0]
+    fine_drop = pl.pallas_call(
+        combine_kernel,
+        grid=(STEPS,),
+        out_shape=hbm((T, T), F32),
+        in_specs=[
+            pl.BlockSpec((8, L), lambda i: (0, 0)),
+            pl.BlockSpec((4, LT, T // STEPS, L), lambda i: (0, 0, i, 0)),
+            pl.BlockSpec((48, T), lambda i: (0, 0)),
+        ],
+        out_specs=pl.BlockSpec((T // STEPS, T), lambda i: (i, 0)),
+        cost_estimate=pl.CostEstimate(flops=big // 4, bytes_accessed=0, transcendentals=0),
+        compiler_params=pltpu.CompilerParams(vmem_limit_bytes=20 * 2**20),
+    )(*keep(coef), *leave(hist), *keep(rims))
     coarse_drop = call(
         sweep2_kernel, [hbm((CB, CB), F32)], keep(u, src, cdiag, scale, hl, hr, hu, hd), flags=flags
     )[0]

time: 104 us -> 106 us (1.019)
  Pallas kernels: 45.3 us -> 46.6 us
    pallas_call x0 -> x1, Pallas kernels: none -> 4.17 us  [per_device(): pl.pallas_call(combine_kernel, grid=(STEPS,), out_shape=hbm((T, T), F32),...]
    pallas_call x13 -> x12, Pallas kernels: 45.3 us -> 42.4 us  [call(): pl.pallas_call(body, out_shape=outs, in_specs=specs, out_specs=[ANY] * an...]
where the time goes in v3:
time: 106 us; the launch traced here: 105 us
  Pallas kernels  46.6 us (44%)
  starting transfers between devices  42.9 us (40%)
  waiting for transfers between devices  12 us (11%)
  other arithmetic  2.12 us (2%)
    pallas_call x12, Pallas kernels, call(): pl.pallas_call(body, out_shape=outs, in_specs=specs, out_specs=[ANY] * an...  42.4 us
    all_to_all x4, starting transfers between devices, spread(): return lax.all_to_all(x, axis, split_axis=0, concat_axis=0, tiled=True)  24.9 us
    ppermute x8, starting transfers between devices, swap(): return (lax.ppermute(to_high, axis, up), lax.ppermute(to_low, axis, down))  18 us
    all_to_all x4, waiting for transfers between devices, spread(): return lax.all_to_all(x, axis, split_axis=0, concat_axis=0, tiled=True)  11.9 us
    pallas_call x1, Pallas kernels, per_device(): pl.pallas_call(combine_kernel, grid=(STEPS,), out_shape=hbm((T, T), F32),...  4.17 us
  transfers between devices with their start and end apart: 12, of which 3 were waited for; matrix products, arithmetic and copies ran while one was open for 1% of the time, Pallas kernels for 35%

profile of v3, /device:TPU:1, one launch (start us, length us, event | category | flops | bytes accessed | tf_op | source)
XLA Modules:
  0.0 105.1 jit_solution(16496878958988878627)
XLA Ops:
  0.6 1.4 %compare_select_fusion = s32[16,1,128]{2,1,0:T(1,128)} fusion(s32[1,2048]{1,0:T(1,128)} %param.14, s32[16]{0:T(128)} %bitcast.26), kind=kLoop, calls=%fused_computation | loop fusion | flops 12288 | bytes 16448 | tf_op jit(solution)/shard_map/jit(_where)/select_n | solution.py:508
  2.0 7.6 %all-to-all-start = ((s32[16,1,128]{2,1,0:T(1,128)}), s32[16,1,128]{2,1,0:T(1,128)S(1)}, u32[]{:S(2)}, u32[]{:S(2)}) async-start(s32[16,1,128]{2,1,0:T(1,128)} %compare_select_fusion), calls=%async_computation | async-start | bytes 16384 | tf_op jit(solution)/shard_map/all_to_all | solution.py:497
  9.6 0.7 fusion.wt
  11.0 4.7 %shard_map.96 = (f32[512,512]{1,0:T(8,128)S(1)}, f32[512,512]{1,0:T(8,128)S(1)}, f32[16,512]{1,0:T(8,128)S(1)}, f32[16,512]{1,0:T(8,128)S(1)}) custom-call(s32[16,128]{1,0:T(8,128)S(1)} %bitcast.21, f32[16,128]{1,0:T(8,128)S(1)} %fusion.wt, f32[512,512]{1,0:T(8,128)} %amp.1, s32[512,512]{1,0:T(8,128)} %mask.1, f32[512,512]{1,0:T(8,128)} %leak.1), custom_call_target="tpu_custom_call" | custom-call | flops 20000000000 | tf_op jit(solution)/shard_map/pallas_call | solution.py:474
  16.0 1.3 %shard_map.95 = f32[16,128]{1,0:T(8,128)} custom-call(s32[16,128]{1,0:T(8,128)S(1)} %bitcast.16, f32[128,128]{1,0:T(8,128)S(1)} %copy-done), custom_call_target="tpu_custom_call" | custom-call | tf_op jit(solution)/shard_map/pallas_call | solution.py:474
  17.2 6.5 %all-to-all-start.1 = ((f32[16,1,128]{2,1,0:T(1,128)}), f32[16,1,128]{2,1,0:T(1,128)S(1)}, u32[]{:S(2)}, u32[]{:S(2)}) async-start(f32[16,1,128]{2,1,0:T(1,128)} %bitcast.5), calls=%async_computation.1 | async-start | bytes 16384 | tf_op jit(solution)/shard_map/all_to_all | solution.py:497
  23.7 6.3 %all-to-all-done.1 = f32[16,1,128]{2,1,0:T(1,128)S(1)} async-done(((f32[16,1,128]{2,1,0:T(1,128)}), f32[16,1,128]{2,1,0:T(1,128)S(1)}, u32[]{:S(2)}, u32[]{:S(2)}) %all-to-all-start.1) | async-done | bytes 8224 | tf_op jit(solution)/shard_map/all_to_all | solution.py:497
  30.0 1.2 %shard_map.97 = (bf16[512,2048]{1,0:T(8,128)(2,1)S(1)}, f32[8,640]{1,0:T(8,128)S(1)}, f32[8,640]{1,0:T(8,128)S(1)}) custom-call(s32[16,128]{1,0:T(8,128)S(1)} %bitcast.22, f32[16,128]{1,0:T(8,128)S(1)} %fusion.wt, f32[16,128]{1,0:T(8,128)S(1)} %bitcast.18, f32[16,512]{1,0:T(8,128)S(1)} %get-tuple-element.31.strips, f32[128,128]{1,0:T(8,128)S(1)} %copy-done), custom_call_target="tpu_custom_call" | custom-call | tf_op jit(solution)/shard_map/pallas_call | solution.py:474
  31.5 4.5 %collective-permute-start.1 = (f32[8,640]{1,0:T(8,128)S(1)}, f32[8,640]{1,0:T(8,128)S(1)}, u32[]{:S(2)}, u32[]{:S(2)}) collective-permute-start(f32[8,640]{1,0:T(8,128)S(1)} %get-tuple-element.35), channel_id=1, source_target_pairs={{1,0},{2,1},{3,2},{4,3},{5,4},{6,5},{7,6},{8,7},{9,8},{10,9},{11,1... | collective-permute-start | bytes 61448 | tf_op jit(solution)/shard_map/ppermute | solution.py:493
  36.0 2.8 %shard_map.98 = (f32[512,512]{1,0:T(8,128)S(1)}, f32[16,512]{1,0:T(8,128)S(1)}) custom-call(s32[16,128]{1,0:T(8,128)S(1)} %bitcast.23, f32[16,128]{1,0:T(8,128)S(1)} %fusion.wt, f32[16,128]{1,0:T(8,128)S(1)} %bitcast.19, f32[512,512]{1,0:T(8,128)S(1)} %get-tuple-element.29.zl, f32[512,512]{1,0:T(8,128)S(1)} %get-tuple-element.30.invd, ...), custom_call_target="tpu_custom_call" | custom-call | flops 20000000000 | tf_op jit(solution)/shard_map/pallas_call | solution.py:474
  38.9 1.1 %shard_map.100 = (f32[8,768]{1,0:T(8,128)S(1)}, f32[8,768]{1,0:T(8,128)S(1)}) custom-call(s32[2]{0:T(128)S(1)} %compare_select_fusion.1.flags, f32[16,512]{1,0:T(8,128)S(1)} %get-tuple-element.37.zr, f32[16,512]{1,0:T(8,128)S(1)} %get-tuple-element.38.ir, f32[8,640]{1,0:T(8,128)S(1)} %collective-permute-done.got_l, ...), custom_call_target="tpu_custom_call" | custom-call | tf_op jit(solution)/shard_map/pallas_call | solution.py:474
  40.0 4.8 %collective-permute-start.2 = (f32[8,768]{1,0:T(8,128)S(1)}, f32[8,768]{1,0:T(8,128)S(1)}, u32[]{:S(2)}, u32[]{:S(2)}) collective-permute-start(f32[8,768]{1,0:T(8,128)S(1)} %get-tuple-element.39), channel_id=1, source_target_pairs={{0,16},{16,32},{32,48},{48,64},{64,80},{80,96},{96,112},{112,0},{1... | collective-permute-start | bytes 73736 | tf_op jit(solution)/shard_map/ppermute | solution.py:493
  44.8 15.7 %shard_map.99 = (f32[4,4,512,128]{3,2,1,0:T(8,128)}, f32[64,128]{1,0:T(8,128)S(1)}) custom-call(s32[2]{0:T(128)S(1)} %compare_select_fusion.1.flags, f32[512,512]{1,0:T(8,128)S(1)} %get-tuple-element.33.z, f32[512,512]{1,0:T(8,128)S(1)} %get-tuple-element.30.invd, f32[8,640]{1,0:T(8,128)S(1)} %collective-permute-done.got_l, ...), custom_call_target="tpu_custom_call" | custom-call | flops 20000000000 | tf_op jit(solution)/shard_map/pallas_call | solution.py:474
  60.5 2.2 %shard_map.101 = (f32[48,512]{1,0:T(8,128)S(1)}, f32[8,128]{1,0:T(8,128)}) custom-call(s32[2]{0:T(128)S(1)} %compare_select_fusion.1.flags, f32[512,512]{1,0:T(8,128)S(1)} %get-tuple-element.33.z, f32[512,512]{1,0:T(8,128)S(1)} %get-tuple-element.30.invd, f32[8,640]{1,0:T(8,128)S(1)} %collective-permute-done.got_l, ...), custom_call_target="tpu_custom_call" | custom-call | tf_op jit(solution)/shard_map/pallas_call | solution.py:474
  62.7 5.5 %all-to-all-start.2 = ((f32[8,1,128]{2,1,0:T(1,128)}), f32[8,1,128]{2,1,0:T(1,128)S(1)}, u32[]{:S(2)}, u32[]{:S(2)}) async-start(f32[8,1,128]{2,1,0:T(1,128)} %bitcast.8), calls=%async_computation.2 | async-start | bytes 8192 | tf_op jit(solution)/shard_map/all_to_all | solution.py:497
  68.3 8.7 %shard_map.102.g = f32[128,128]{1,0:T(8,128)S(1)} custom-call(s32[16,128]{1,0:T(8,128)S(1)} %bitcast.24, f32[4,4,512,128]{3,2,1,0:T(8,128)} %get-tuple-element.36.hist, f32[48,512]{1,0:T(8,128)S(1)} %get-tuple-element.42.rims, s32[16,128]{1,0:T(8,128)S(1)} %bitcast.25, f32[16,128]{1,0:T(8,128)S(1)} %fusion.wt), custom_call_target="tpu_custom_call" | custom-call | flops 20000000000 | tf_op jit(solution)/shard_map/pallas_call | solution.py:474
  77.7 5.3 %all-to-all-start.3 = ((f32[16,8,128]{2,1,0:T(8,128)}), f32[16,8,128]{2,1,0:T(8,128)S(1)}, u32[]{:S(2)}, u32[]{:S(2)}) async-start(f32[16,8,128]{2,1,0:T(8,128)} %bitcast.10), calls=%async_computation.3 | async-start | bytes 131072 | tf_op jit(solution)/shard_map/all_to_all | solution.py:497
  83.0 1.1 %shard_map.104 = (f32[128,128]{1,0:T(8,128)S(1)}, f32[128,128]{1,0:T(8,128)S(1)}, f32[128,128]{1,0:T(8,128)S(1)}, bf16[128,2048]{1,0:T(8,128)(2,1)S(1)}, bf16[128,2048]{1,0:T(8,128)(2,1)S(1)}) custom-call(s32[2]{0:T(128)S(1)} %compare_select_fusion.1.flags, s32[16,128]{1,0:T(8,128)S(1)} %bitcast.17, f32[128,128]{1,0:T(8,128)S(1)} %copy-done, ...), custom_call_target="tpu_custom_call" | custom-call | flops 20000000000 | tf_op jit(solution)/shard_map/pallas_call | solution.py:474
  84.2 5.4 %all-to-all-done.3 = f32[16,8,128]{2,1,0:T(8,128)S(1)} async-done(((f32[16,8,128]{2,1,0:T(8,128)}), f32[16,8,128]{2,1,0:T(8,128)S(1)}, u32[]{:S(2)}, u32[]{:S(2)}) %all-to-all-start.3) | async-done | bytes 65568 | tf_op jit(solution)/shard_map/all_to_all | solution.py:497
  89.5 1.3 %shard_map.105 = (f32[8,128]{1,0:T(8,128)S(1)}, f32[128,128]{1,0:T(8,128)S(1)}, f32[128,128]{1,0:T(8,128)S(1)}, f32[8,128]{1,0:T(8,128)S(1)}, f32[8,128]{1,0:T(8...) custom-call(f32[128,128]{1,0:T(8,128)S(1)} %bitcast.15, f32[128,128]{1,0:T(8,128)S(1)} %get-tuple-element.44.scale, ...), custom_call_target="tpu_custom_call" | custom-call | tf_op jit(solution)/shard_map/pallas_call | solution.py:474
  91.2 4.5 %collective-permute-start.5 = (f32[8,128]{1,0:T(8,128)S(1)}, f32[8,128]{1,0:T(8,128)S(1)}, u32[]{:S(2)}, u32[]{:S(2)}) collective-permute-start(f32[8,128]{1,0:T(8,128)S(1)} %get-tuple-element.53), channel_id=1, source_target_pairs={{1,0},{2,1},{3,2},{4,3},{5,4},{6,5},{7,6},{8,7},{9,8},{10,9},{11,1... | collective-permute-start | bytes 12296 | tf_op jit(solution)/shard_map/ppermute | solution.py:493
  95.7 3.6 %collective-permute-start.6 = (f32[8,128]{1,0:T(8,128)S(1)}, f32[8,128]{1,0:T(8,128)S(1)}, u32[]{:S(2)}, u32[]{:S(2)}) collective-permute-start(f32[8,128]{1,0:T(8,128)S(1)} %get-tuple-element.54), channel_id=1, source_target_pairs={{0,16},{16,32},{32,48},{48,64},{64,80},{80,96},{96,112},{112,0},{1... | collective-permute-start | bytes 12296 | tf_op jit(solution)/shard_map/ppermute | solution.py:493
  99.3 4.2 %shard_map.106 = f32[512,512]{1,0:T(8,128)} custom-call(f32[8,128]{1,0:T(8,128)S(1)} %get-tuple-element.48.coef, f32[4,4,512,128]{3,2,1,0:T(8,128)} %get-tuple-element.36.hist, f32[48,512]{1,0:T(8,128)S(1)} %get-tuple-element.42.rims), custom_call_target="tpu_custom_call" | custom-call | flops 5000000000 | tf_op jit(solution)/shard_map/pallas_call | solution.py:561
  103.5 1.5 %shard_map.107 = f32[128,128]{1,0:T(8,128)} custom-call(s32[2]{0:T(128)S(1)} %compare_select_fusion.1.flags, f32[128,128]{1,0:T(8,128)S(1)} %get-tuple-element.49.u, f32[128,128]{1,0:T(8,128)S(1)} %get-tuple-element.50.src, f32[128,128]{1,0:T(8,128)S(1)} %get-tuple-element.51.cdiag, f32[128,128]{1,0:T(8,128)S(1)} %get-tuple-element.44.scale, ...), custom_call_target="tpu_custom_call" | custom-call | tf_op jit(solution)/shard_map/pallas_call | solution.py:474
  (24 shorter events, 2.2 us)
Async XLA Ops:
  2.0 13.9 %all-to-all-start = ((s32[16,1,128]{2,1,0:T(1,128)}), s32[16,1,128]{2,1,0:T(1,128)S(1)}, u32[]{:S(2)}, u32[]{:S(2)}) async-start(s32[16,1,128]{2,1,0:T(1,128)} %compare_select_fusion), calls=%async_computation | async-start | bytes 16384 | tf_op jit(solution)/shard_map/all_to_all | solution.py:497
  10.3 0.7 copy-start.1
  11.0 4.9 %copy-start = (f32[128,128]{1,0:T(8,128)S(1)}, f32[128,128]{1,0:T(8,128)}, u32[]{:S(2)}) copy-start(f32[128,128]{1,0:T(8,128)} %volt.7) | copy-start | bytes 196612
  11.0 19.0 %copy-start.2 = (s32[1,2048]{1,0:T(1,128)S(1)}, s32[1,2048]{1,0:T(1,128)}, u32[]{:S(2)}) copy-start(s32[1,2048]{1,0:T(1,128)} %param.13) | copy-start | bytes 24580
  17.2 12.8 %all-to-all-start.1 = ((f32[16,1,128]{2,1,0:T(1,128)}), f32[16,1,128]{2,1,0:T(1,128)S(1)}, u32[]{:S(2)}, u32[]{:S(2)}) async-start(f32[16,1,128]{2,1,0:T(1,128)} %bitcast.5), calls=%async_computation.1 | async-start | bytes 16384 | tf_op jit(solution)/shard_map/all_to_all | solution.py:497
  31.2 7.6 %collective-permute-start = (f32[8,640]{1,0:T(8,128)S(1)}, f32[8,640]{1,0:T(8,128)S(1)}, u32[]{:S(2)}, u32[]{:S(2)}) collective-permute-start(f32[8,640]{1,0:T(8,128)S(1)} %get-tuple-element.34), channel_id=1, source_target_pairs={{0,1},{1,2},{2,3},{3,4},{4,5},{5,6},{6,7},{7,8},{8,9},{9,10},{10,1... | collective-permute-start | bytes 61448 | tf_op jit(solution)/shard_map/ppermute | solution.py:493
  31.5 7.3 %collective-permute-start.1 = (f32[8,640]{1,0:T(8,128)S(1)}, f32[8,640]{1,0:T(8,128)S(1)}, u32[]{:S(2)}, u32[]{:S(2)}) collective-permute-start(f32[8,640]{1,0:T(8,128)S(1)} %get-tuple-element.35), channel_id=1, source_target_pairs={{1,0},{2,1},{3,2},{4,3},{5,4},{6,5},{7,6},{8,7},{9,8},{10,9},{11,1... | collective-permute-start | bytes 61448 | tf_op jit(solution)/shard_map/ppermute | solution.py:493
  40.0 20.5 %collective-permute-start.2 = (f32[8,768]{1,0:T(8,128)S(1)}, f32[8,768]{1,0:T(8,128)S(1)}, u32[]{:S(2)}, u32[]{:S(2)}) collective-permute-start(f32[8,768]{1,0:T(8,128)S(1)} %get-tuple-element.39), channel_id=1, source_target_pairs={{0,16},{16,32},{32,48},{48,64},{64,80},{80,96},{96,112},{112,0},{1... | collective-permute-start | bytes 73736 | tf_op jit(solution)/shard_map/ppermute | solution.py:493
  44.8 15.7 %collective-permute-start.3 = (f32[8,768]{1,0:T(8,128)S(1)}, f32[8,768]{1,0:T(8,128)S(1)}, u32[]{:S(2)}, u32[]{:S(2)}) collective-permute-start(f32[8,768]{1,0:T(8,128)S(1)} %get-tuple-element.40), channel_id=1, source_target_pairs={{16,0},{32,16},{48,32},{64,48},{80,64},{96,80},{112,96},{0,112},{1... | collective-permute-start | bytes 73736 | tf_op jit(solution)/shard_map/ppermute | solution.py:493
  62.7 14.3 %all-to-all-start.2 = ((f32[8,1,128]{2,1,0:T(1,128)}), f32[8,1,128]{2,1,0:T(1,128)S(1)}, u32[]{:S(2)}, u32[]{:S(2)}) async-start(f32[8,1,128]{2,1,0:T(1,128)} %bitcast.8), calls=%async_computation.2 | async-start | bytes 8192 | tf_op jit(solution)/shard_map/all_to_all | solution.py:497
  68.3 14.8 %copy-start.3 = (f32[128,128]{1,0:T(8,128)S(1)}, f32[128,128]{1,0:T(8,128)}, u32[]{:S(2)}) copy-start(f32[128,128]{1,0:T(8,128)} %cleak.1) | copy-start | bytes 196612
  77.7 11.9 %all-to-all-start.3 = ((f32[16,8,128]{2,1,0:T(8,128)}), f32[16,8,128]{2,1,0:T(8,128)S(1)}, u32[]{:S(2)}, u32[]{:S(2)}) async-start(f32[16,8,128]{2,1,0:T(8,128)} %bitcast.10), calls=%async_computation.3 | async-start | bytes 131072 | tf_op jit(solution)/shard_map/all_to_all | solution.py:497
  90.9 12.6 %collective-permute-start.4 = (f32[8,128]{1,0:T(8,128)S(1)}, f32[8,128]{1,0:T(8,128)S(1)}, u32[]{:S(2)}, u32[]{:S(2)}) collective-permute-start(f32[8,128]{1,0:T(8,128)S(1)} %get-tuple-element.52), channel_id=1, source_target_pairs={{0,1},{1,2},{2,3},{3,4},{4,5},{5,6},{6,7},{7,8},{8,9},{9,10},{10,1... | collective-permute-start | bytes 12296 | tf_op jit(solution)/shard_map/ppermute | solution.py:493
  91.2 12.3 %collective-permute-start.5 = (f32[8,128]{1,0:T(8,128)S(1)}, f32[8,128]{1,0:T(8,128)S(1)}, u32[]{:S(2)}, u32[]{:S(2)}) collective-permute-start(f32[8,128]{1,0:T(8,128)S(1)} %get-tuple-element.53), channel_id=1, source_target_pairs={{1,0},{2,1},{3,2},{4,3},{5,4},{6,5},{7,6},{8,7},{9,8},{10,9},{11,1... | collective-permute-start | bytes 12296 | tf_op jit(solution)/shard_map/ppermute | solution.py:493
  95.7 7.8 %collective-permute-start.6 = (f32[8,128]{1,0:T(8,128)S(1)}, f32[8,128]{1,0:T(8,128)S(1)}, u32[]{:S(2)}, u32[]{:S(2)}) collective-permute-start(f32[8,128]{1,0:T(8,128)S(1)} %get-tuple-element.54), channel_id=1, source_target_pairs={{0,16},{16,32},{32,48},{48,64},{64,80},{80,96},{96,112},{112,0},{1... | collective-permute-start | bytes 12296 | tf_op jit(solution)/shard_map/ppermute | solution.py:493
  99.3 4.2 %collective-permute-start.7 = (f32[8,128]{1,0:T(8,128)S(1)}, f32[8,128]{1,0:T(8,128)S(1)}, u32[]{:S(2)}, u32[]{:S(2)}) collective-permute-start(f32[8,128]{1,0:T(8,128)S(1)} %get-tuple-element.55), channel_id=1, source_target_pairs={{16,0},{32,16},{48,32},{64,48},{80,64},{96,80},{112,96},{0,112},{1... | collective-permute-start | bytes 12296 | tf_op jit(solution)/shard_map/ppermute | solution.py:493

commit v4 on v3

--- a/solution.py
+++ b/solution.py
@@ -24,12 +24,12 @@
 EXT = OFF + T + 16
 W = T + L
 
-Q = (1.08976773, 1.76773384, 1.28562461)
+Q = (1.09375, 1.765625, 1.28125)
 RHO = (1.0 - Q[0], Q[0] - Q[1], Q[1] - Q[2], Q[2])
 LT = T // L
 SLAB = 4 * LT + 1
 SUMS = 8
-STEPS = 4
+STEPS = 8
 
 
 def iota(shape, dim):
@@ -61,7 +61,9 @@
     return slice(o * L, (o + 1) * L)
 
 
-def diag_kernel(vf, wt, amp, mask, leak, zl, invd, strips, rims, a_s, b_s):
+def diag_kernel(vf, wt, amp, mask, leak, zl, invd, strips, rims, slots, a_s, b_s):
+    slots[0:NO, :] = (vf[...] >> 9) * SLAB
+    slots[NO:, :] = (iota((NO, L), 1) - vf[...]) & (L - 1)
     for o in range(NO):
         f = vf[o : o + 1, :]
         a_s[:, lanes(o)] = onehot(f // T, T)
@@ -134,19 +136,24 @@
 def halo_columns(flags, gl, gr):
     left = jnp.where(flags[1] > 0, 1.0, 0.0)
     right = jnp.where(flags[1] < NO - 1, 1.0, 0.0)
-    j, lane = iota((8, L), 0), iota((8, L), 1)
-    zc = tn(gr, jnp.where((j < 4) & (lane == j), right, 0.0), HI) + tn(
-        gl, jnp.where((j < 4) & (lane == 124 + j), left, 0.0), HI
-    )
-    ic = tn(gr, jnp.where((j >= 4) & (lane == j - 4), right, 0.0), HI) + tn(
-        gl, jnp.where((j >= 4) & (lane == 120 + j), left, 0.0), HI
-    )
-    return zc, ic
-
-
-def edge_kernel(flags, zr, ir, got_l, got_r, volt, send_u, send_d):
+    parts = []
+    for x in (gr * right, gl * left):
+        a, rest = hi_lo(x)
+        b, c = hi_lo(rest)
+        parts += [c, b, a]
+    j, lane = iota((8, 2 * L), 0), iota((8, 2 * L), 1)
+    to_r = jnp.where(lane == jnp.where(j < 4, j, L + j - 4), 1.0, 0.0)
+    to_l = jnp.where(lane == jnp.where(j < 4, 124 + j, L + 120 + j), 1.0, 0.0)
+    place = jnp.concatenate([to_r] * 3 + [to_l] * 3, axis=0)
+    out = tn(jnp.concatenate(parts, axis=0).astype(BF16), place.astype(BF16))
+    return out[:, :L], out[:, L:]
+
+
+def edge_kernel(flags, zr, ir, got_l, got_r, volt, send_u, send_d, corners):
     zt, it = halo_columns(flags, got_l[:, :L], got_r[:, :L])
     zb, ib = halo_columns(flags, got_l[:, T - L : T], got_r[:, T - L : T])
+    for k, x in enumerate((zt[0:16], zb[L - 16 :], it[0:16], ib[L - 16 :])):
+        corners[16 * k : 16 * k + 16, :] = x
     low = iota((8, W), 0) < 4
     zt = jnp.concatenate([zr[0:8, :], zt[0:8]], axis=1)
     it = jnp.concatenate([ir[0:8, :], it[0:8]], axis=1)
@@ -201,7 +208,7 @@
         ie[t, own, :] = invd[:, lanes(t)]
     ze[LT, own, :] = zc
     ie[LT, own, :] = ic
-    rows = 16
+    rows = 128
 
     def save(k, e):
         copy = pltpu.make_async_copy(e.at[pl.ds(0, LT), own, :], hist.at[k], sem.at[k])
@@ -227,38 +234,57 @@
     apply_to(n1e, n2e, False)
     copies.append(save(3, n2e))
 
-    def gram(i, acc):
-        start = pl.multiple_of(OFF + i * 8, 8)
-        n2, dn3 = near_tiles(n2e, start, 8)
-        acc = list(acc)
+    acc = [jnp.zeros((8, L), F32) for _ in range(SUMS)]
+    ends = list(range(0, T + 1, 64))
+    ends[0], ends[-1] = 8, T - 8
+    for low, high in zip(ends[:-1], ends[1:]):
+        start, rows = OFF + low, high - low
+        n2, dn3 = near_tiles(n2e, start, rows)
         for t in range(LT):
-            z8, w8, n18, i8 = (e[t, pl.ds(start, 8), :] for e in (ze, we, n1e, ie))
+            z8, w8, n18, i8 = (e[t, pl.ds(start, rows), :] for e in (ze, we, n1e, ie))
             for k, p in enumerate(moments(z8, w8, n18, n2[t], dn3[t], i8)):
-                acc[k] = acc[k] + p
-        return tuple(acc)
-
-    acc = lax.fori_loop(
-        1, T // 8 - 1, gram, tuple(jnp.zeros((8, L), F32) for _ in range(SUMS))
-    )
+                for q in range(0, rows, 8):
+                    acc[k] = acc[k] + p[q : q + 8]
     for k in range(SUMS):
         acc_o[8 * k : 8 * k + 8, :] = acc[k]
     for copy in copies:
         copy.wait()
 
 
-def rim_kernel(flags, z, invd, got_l, got_r, got_u, got_d, acc_i, rims, part):
+def gram_terms(acc):
+    g0, q0 = acc[0], acc[1]
+    m = acc[2:]
+    r = [q0, q0 - m[0], q0 - m[0] - m[1]]
+    h = {(0, 0): q0, **{(0, j): RHO[0] * m[j - 1] for j in (1, 2, 3)}}
+    b = [g0] + r
+    for k in range(3):
+        h[0, 0] = h[0, 0] - Q[k] * m[k]
+        b[0] = b[0] - Q[k] * r[k]
+    for k in range(6):
+        f = sum(Q[j] * RHO[k - j] for j in range(3) if 0 <= k - j < 4)
+        h[0, 0] = h[0, 0] - f * m[k]
+    for j in (1, 2, 3):
+        for k in (1, 2, 3):
+            h[0, j] = h[0, j] + RHO[k] * m[j - 1 + k]
+            if j <= k:
+                h[j, k] = m[j + k - 2] - m[j + k - 1]
+    out = []
+    for p in range(4):
+        out += [h[p, q] for q in range(p, 4)] + [b[p]]
+    return out
+
+
+def rim_kernel(flags, z, invd, corners, got_u, got_d, acc_i, rims, part):
     up = jnp.where(flags[0] > 0, 1.0, 0.0)
     down = jnp.where(flags[0] < 7, 1.0, 0.0)
     low = iota((8, W), 0) < 4
     acc = [acc_i[8 * k : 8 * k + 8, :] for k in range(SUMS)]
     top, bot = got_u[:, :W], got_d[:, :W]
     for end in (0, 1):
-        cols = slice(0, L) if end == 0 else slice(T - L, T)
         rows = slice(0, 16) if end == 0 else slice(T - 16, T)
-        part_of = slice(0, 16) if end == 0 else slice(L - 16, L)
-        zc, ic = halo_columns(flags, got_l[:, cols], got_r[:, cols])
-        z16 = jnp.concatenate([z[rows, :], zc[part_of]], axis=1)
-        i16 = jnp.concatenate([invd[rows, :], ic[part_of]], axis=1)
+        zc, ic = corners[16 * end : 16 * end + 16, :], corners[32 + 16 * end : 48 + 16 * end, :]
+        z16 = jnp.concatenate([z[rows, :], zc], axis=1)
+        i16 = jnp.concatenate([invd[rows, :], ic], axis=1)
         if end == 0:
             zb = jnp.concatenate([jnp.where(low, 0.0, pltpu.roll(top, 4, 0)) * up, z16], axis=0)
             ib = jnp.concatenate([jnp.where(low, 0.0, top) * up, i16], axis=0)
@@ -276,10 +302,16 @@
             acc[k] = acc[k] + fold(p)
         for k, x in enumerate((wo, n1o, n2o)):
             rims[16 * k + 8 * end : 16 * k + 8 * end + 8, :] = x
-    rows8 = jnp.concatenate(
-        [jnp.sum(a, axis=0, keepdims=True) for a in acc] + [jnp.zeros((L - SUMS, L), F32)], axis=0
-    )
-    sums = nt(jnp.ones((8, L), F32), rows8, HI)
+    terms = gram_terms(acc)
+    rows14 = jnp.concatenate(
+        [jnp.sum(a, axis=0, keepdims=True) for a in terms] + [jnp.zeros((2, L), F32)], axis=0
+    )
+    a, rest = hi_lo(rows14)
+    b, c = hi_lo(rest)
+    parts = jnp.concatenate([c, b, a], axis=0).astype(BF16)
+    sums = nt(jnp.ones((8, L), BF16), parts)
+    sums = sums[:, 0:16] + sums[:, 16:32] + sums[:, 32:48]
+    sums = jnp.concatenate([sums, jnp.zeros((8, L - 16), F32)], axis=1)
     part[...] = sums
 
 
@@ -305,12 +337,11 @@
         lax.fori_loop(0, T // 32, lay, 0)
     lane, sub = iota((16, L), 1), iota((16, L), 0)
 
-    def owner(o, carry):
+    def owner(o):
         acc = jnp.zeros((16, L), F32)
         for j in range(L):
-            node = slots[o, j]
-            x = slab[pl.ds((node >> 9) * SLAB, 16), :]
-            x = pltpu.roll(x, (j - node) & (L - 1), 1)
+            x = slab[pl.ds(slots[o, j], 16), :]
+            x = pltpu.roll(x, slots[NO + o, j], 1)
             acc = jnp.where(lane == j, x, acc)
         f = vf[pl.ds(o, 1), :]
         acc = jnp.where((sub & 3) == ((f >> 7) & 3), acc * wt[pl.ds(o, 1), :], 0.0)
@@ -318,9 +349,13 @@
         g_o[pl.ds(pl.multiple_of(8 * o, 8), 8), :] = jnp.concatenate(
             rows + [jnp.zeros((4, L), F32)], axis=0
         )
+
+    def owners(i, carry):
+        owner(2 * i)
+        owner(2 * i + 1)
         return carry
 
-    lax.fori_loop(0, NO, owner, 0)
+    lax.fori_loop(0, NO // 2, owners, 0)
 
 
 def pack_kernel(g, rows, out):
@@ -336,22 +371,14 @@
     def pick(k):
         return jnp.sum(jnp.where(lane == k, tot, 0.0), axis=1, keepdims=True)
 
-    g0, q0 = pick(0), pick(1)
-    m = [pick(2 + k) for k in range(6)]
-    r = [q0, q0 - m[0], q0 - m[0] - m[1]]
-    h = {(0, 0): q0, **{(0, j): RHO[0] * m[j - 1] for j in (1, 2, 3)}}
-    b = [g0] + r
-    for k in range(3):
-        h[0, 0] = h[0, 0] - Q[k] * m[k]
-        b[0] = b[0] - Q[k] * r[k]
-    for k in range(6):
-        f = sum(Q[j] * RHO[k - j] for j in range(3) if 0 <= k - j < 4)
-        h[0, 0] = h[0, 0] - f * m[k]
-    for j in (1, 2, 3):
-        for k in (1, 2, 3):
-            h[0, j] = h[0, j] + RHO[k] * m[j - 1 + k]
-            if j <= k:
-                h[j, k] = m[j + k - 2] - m[j + k - 1]
+    h, b = {}, []
+    k = 0
+    for p in range(4):
+        for q in range(p, 4):
+            h[p, q] = pick(k)
+            k += 1
+        b.append(pick(k))
+        k += 1
     floor = [3e-7 * h[p, p] for p in range(4)]
     inv = []
     for p in range(4):
@@ -370,22 +397,36 @@
     return [c[0]] + [c[k + 1] - Q[k] * c[0] for k in range(3)]
 
 
-def combine_kernel(coef, hist, rims, x_o):
+def combine_kernel(hist, coef, rims, out, h_s, x_s, sem_in, sem_out):
+    n = T // STEPS
+    load = [
+        pltpu.make_async_copy(hist.at[:, :, pl.ds(i * n, n), :], h_s.at[i], sem_in.at[i])
+        for i in range(STEPS)
+    ]
+    save = [
+        pltpu.make_async_copy(x_s.at[pl.ds(i * n, n), :], out.at[pl.ds(i * n, n), :], sem_out.at[i])
+        for i in range(STEPS)
+    ]
+    for copy in load:
+        copy.start()
     c = [coef[k : k + 1, 0:1] for k in range(4)]
-    i = pl.program_id(0)
-    for t in range(LT):
-        x_o[:, lanes(t)] = (c[0] * hist[0, t] + c[1] * hist[1, t]) + (
-            c[2] * hist[2, t] + c[3] * hist[3, t]
-        )
-    for end, step, rows in ((0, 0, slice(0, 8)), (1, STEPS - 1, slice(T // STEPS - 8, T // STEPS))):
-
-        @pl.when(i == step)
-        def _(end=end, rows=rows):
-            for t in range(LT):
-                x = c[0] * hist[0, t, rows, :]
-                for k in range(3):
-                    x += c[k + 1] * rims[16 * k + 8 * end : 16 * k + 8 * end + 8, lanes(t)]
-                x_o[rows, lanes(t)] = x
+    for i in range(STEPS):
+        load[i].wait()
+        for t in range(LT):
+            h = [h_s[i, k, t] for k in range(4)]
+            x_s[i * n : (i + 1) * n, lanes(t)] = (c[0] * h[0] + c[1] * h[1]) + (
+                c[2] * h[2] + c[3] * h[3]
+            )
+        for end, step, low in ((0, 0, 0), (1, STEPS - 1, n - 8)):
+            if i == step:
+                for t in range(LT):
+                    x = c[0] * h_s[i, 0, t, low : low + 8, :]
+                    for k in range(3):
+                        x += c[k + 1] * rims[16 * k + 8 * end : 16 * k + 8 * end + 8, lanes(t)]
+                    x_s[i * n + low : i * n + low + 8, lanes(t)] = x
+        save[i].start()
+    for copy in save:
+        copy.wait()
 
 
 def coarse_neighbours(flags, u, above, below, from_l, from_r):
@@ -516,8 +557,8 @@
     dmas = pltpu.SemaphoreType.DMA((4,))
     big = 20_000_000_000
 
-    zl, invd, strips, irims = call(
-        diag_kernel, [tile, tile, rim16, rim16],
+    zl, invd, strips, irims, where = call(
+        diag_kernel, [tile, tile, rim16, rim16, hbm((2 * NO, L), jnp.int32)],
         keep(fine, wt) + leave(load_amp, load_mask, leak), [hot, hot], flops=big,
     )
     looked = call(lookup_kernel, [slots], keep(held, coarse_init))[0]
@@ -530,8 +571,8 @@
         rhs_kernel, [tile, rim16], keep(fine, wt, at_via, zl, invd, a), [hots], flops=big
     )
     rim = vmem((8, W + CB), F32)
-    send_u, send_d = call(
-        edge_kernel, [rim, rim], keep(zrims, irims, got_l, got_r, coarse_init), flags=flags
+    send_u, send_d, corners = call(
+        edge_kernel, [rim, rim, vmem((64, L), F32)], keep(zrims, irims, got_l, got_r, coarse_init), flags=flags
     )
     got_u, got_d = swap(ROW, send_u, send_d)
     hist, acc = call(
@@ -540,12 +581,12 @@
     )
     rims, part = call(
         rim_kernel, [vmem((48, T), F32), vmem((8, L), F32)],
-        keep(z, invd, got_l, got_r, got_u, got_d, acc), flags=flags,
+        keep(z, invd, corners, got_u, got_d, acc), flags=flags,
     )
     rows = spread(part, ROW)
     g = call(
         gather_kernel, [vmem(*packed)], leave(hist) + keep(rims, fine, wt),
-        [vmem((4, LT, T, L), F32), vmem((T * SLAB, L), F32), dmas], flags=fine, flops=big, any_in=1,
+        [vmem((4, LT, T, L), F32), vmem((T * SLAB, L), F32), dmas], flags=where, flops=big, any_in=1,
     )[0]
     arrived = spread(call(pack_kernel, [vmem(*packed)], keep(g, rows))[0])
     cdiag, scale, base, r_hot, c_hot = call(
@@ -558,19 +599,11 @@
     )
     hl, hr = swap(COL, sl, sr)
     hu, hd = swap(ROW, su, sd)
-    fine_drop = pl.pallas_call(
-        combine_kernel,
-        grid=(STEPS,),
-        out_shape=hbm((T, T), F32),
-        in_specs=[
-            pl.BlockSpec((8, L), lambda i: (0, 0)),
-            pl.BlockSpec((4, LT, T // STEPS, L), lambda i: (0, 0, i, 0)),
-            pl.BlockSpec((48, T), lambda i: (0, 0)),
-        ],
-        out_specs=pl.BlockSpec((T // STEPS, T), lambda i: (i, 0)),
-        cost_estimate=pl.CostEstimate(flops=big // 4, bytes_accessed=0, transcendentals=0),
-        compiler_params=pltpu.CompilerParams(vmem_limit_bytes=20 * 2**20),
-    )(*keep(coef), *leave(hist), *keep(rims))
+    fine_drop = call(
+        combine_kernel, [pltpu.MemorySpace.HBM((T, T), F32)], leave(hist) + keep(coef, rims),
+        [vmem((STEPS, 4, LT, T // STEPS, L), F32), tile, pltpu.SemaphoreType.DMA((STEPS,)),
+         pltpu.SemaphoreType.DMA((STEPS,))], flops=big // 4, any_in=1, any_out=1,
+    )[0]
     coarse_drop = call(
         sweep2_kernel, [hbm((CB, CB), F32)], keep(u, src, cdiag, scale, hl, hr, hu, hd), flags=flags
     )[0]

time: 106 us -> 92.3 us (0.87)
  Pallas kernels: 46.6 us -> 33.3 us
    pallas_call x12 -> x13, Pallas kernels: 42.4 us -> 33.3 us  [call(): pl.pallas_call(body, out_shape=outs, in_specs=specs, out_specs=[ANY] * an...]
    pallas_call x1 -> x0, Pallas kernels: 4.17 us -> none  [per_device(): pl.pallas_call(combine_kernel, grid=(STEPS,), out_shape=hbm((T, T), F32),...]
  transfers between devices with their start and end apart: 12 -> 12, of which waited for: 3 -> 3; matrix products, arithmetic and copies ran while one was open for 1% -> 1% of each run, Pallas kernels for 35% -> 27%
where the time goes in v4:
time: 92.3 us; the launch traced here: 91.8 us
  starting transfers between devices  42.9 us (46%)
  Pallas kernels  33.3 us (36%)
  waiting for transfers between devices  12 us (13%)
  other arithmetic  2.12 us (2%)
    pallas_call x13, Pallas kernels, call(): pl.pallas_call(body, out_shape=outs, in_specs=specs, out_specs=[ANY] * an...  33.3 us
    all_to_all x4, starting transfers between devices, spread(): return lax.all_to_all(x, axis, split_axis=0, concat_axis=0, tiled=True)  24.9 us
    ppermute x8, starting transfers between devices, swap(): return (lax.ppermute(to_high, axis, up), lax.ppermute(to_low, axis, down))  18 us
    all_to_all x4, waiting for transfers between devices, spread(): return lax.all_to_all(x, axis, split_axis=0, concat_axis=0, tiled=True)  11.9 us
  transfers between devices with their start and end apart: 12, of which 3 were waited for; matrix products, arithmetic and copies ran while one was open for 1% of the time, Pallas kernels for 27%

profile of v4, /device:TPU:1, one launch (start us, length us, event | category | flops | bytes accessed | tf_op | source)
XLA Modules:
  0.0 91.8 jit_solution(416345095538593392)
XLA Ops:
  0.6 1.4 %compare_select_fusion = s32[16,1,128]{2,1,0:T(1,128)} fusion(s32[1,2048]{1,0:T(1,128)} %param.14, s32[16]{0:T(128)} %bitcast.25), kind=kLoop, calls=%fused_computation | loop fusion | flops 12288 | bytes 16448 | tf_op jit(solution)/shard_map/jit(_where)/select_n | solution.py:549
  2.0 7.6 %all-to-all-start = ((s32[16,1,128]{2,1,0:T(1,128)}), s32[16,1,128]{2,1,0:T(1,128)S(1)}, u32[]{:S(2)}, u32[]{:S(2)}) async-start(s32[16,1,128]{2,1,0:T(1,128)} %compare_select_fusion), calls=%async_computation | async-start | bytes 16384 | tf_op jit(solution)/shard_map/all_to_all | solution.py:538
  9.6 0.7 fusion.wt
  11.0 4.7 %shard_map.96 = (f32[512,512]{1,0:T(8,128)S(1)}, f32[512,512]{1,0:T(8,128)S(1)}, f32[16,512]{1,0:T(8,128)S(1)}, f32[16,512]{1,0:T(8,128)S(1)}, s32[32,128]{1,0:T(8,128)S(1)}) custom-call(s32[16,128]{1,0:T(8,128)S(1)} %bitcast.21, f32[16,128]{1,0:T(8,128)S(1)} %fusion.wt, f32[512,512]{1,0:T(8,128)} %amp.1, s32[512,512]{1,0:T(8,128)} %mask.1, f32[512,512]{1,0:T(8,128)} %leak.1), custom_call_target="tpu_custom_call" | custom-call | flops 20000000000 | tf_op jit(solution)/shard_map/pallas_call | solution.py:515
  16.0 1.3 %shard_map.95 = f32[16,128]{1,0:T(8,128)} custom-call(s32[16,128]{1,0:T(8,128)S(1)} %bitcast.16, f32[128,128]{1,0:T(8,128)S(1)} %copy-done), custom_call_target="tpu_custom_call" | custom-call | tf_op jit(solution)/shard_map/pallas_call | solution.py:515
  17.2 6.5 %all-to-all-start.1 = ((f32[16,1,128]{2,1,0:T(1,128)}), f32[16,1,128]{2,1,0:T(1,128)S(1)}, u32[]{:S(2)}, u32[]{:S(2)}) async-start(f32[16,1,128]{2,1,0:T(1,128)} %bitcast.5), calls=%async_computation.1 | async-start | bytes 16384 | tf_op jit(solution)/shard_map/all_to_all | solution.py:538
  23.7 6.3 %all-to-all-done.1 = f32[16,1,128]{2,1,0:T(1,128)S(1)} async-done(((f32[16,1,128]{2,1,0:T(1,128)}), f32[16,1,128]{2,1,0:T(1,128)S(1)}, u32[]{:S(2)}, u32[]{:S(2)}) %all-to-all-start.1) | async-done | bytes 8224 | tf_op jit(solution)/shard_map/all_to_all | solution.py:538
  30.0 1.2 %shard_map.97 = (bf16[512,2048]{1,0:T(8,128)(2,1)S(1)}, f32[8,640]{1,0:T(8,128)S(1)}, f32[8,640]{1,0:T(8,128)S(1)}) custom-call(s32[16,128]{1,0:T(8,128)S(1)} %bitcast.22, f32[16,128]{1,0:T(8,128)S(1)} %fusion.wt, f32[16,128]{1,0:T(8,128)S(1)} %bitcast.18, f32[16,512]{1,0:T(8,128)S(1)} %get-tuple-element.33.strips, f32[128,128]{1,0:T(8,128)S(1)} %copy-done), custom_call_target="tpu_custom_call" | custom-call | tf_op jit(solution)/shard_map/pallas_call | solution.py:515
  31.5 4.5 %collective-permute-start.1 = (f32[8,640]{1,0:T(8,128)S(1)}, f32[8,640]{1,0:T(8,128)S(1)}, u32[]{:S(2)}, u32[]{:S(2)}) collective-permute-start(f32[8,640]{1,0:T(8,128)S(1)} %get-tuple-element.37), channel_id=1, source_target_pairs={{1,0},{2,1},{3,2},{4,3},{5,4},{6,5},{7,6},{8,7},{9,8},{10,9},{11,1... | collective-permute-start | bytes 61448 | tf_op jit(solution)/shard_map/ppermute | solution.py:534
  36.0 2.8 %shard_map.98 = (f32[512,512]{1,0:T(8,128)S(1)}, f32[16,512]{1,0:T(8,128)S(1)}) custom-call(s32[16,128]{1,0:T(8,128)S(1)} %bitcast.23, f32[16,128]{1,0:T(8,128)S(1)} %fusion.wt, f32[16,128]{1,0:T(8,128)S(1)} %bitcast.19, f32[512,512]{1,0:T(8,128)S(1)} %get-tuple-element.31.zl, f32[512,512]{1,0:T(8,128)S(1)} %get-tuple-element.32.invd, ...), custom_call_target="tpu_custom_call" | custom-call | flops 20000000000 | tf_op jit(solution)/shard_map/pallas_call | solution.py:515
  38.9 0.8 shard_map.100
  39.6 4.8 %collective-permute-start.2 = (f32[8,768]{1,0:T(8,128)S(1)}, f32[8,768]{1,0:T(8,128)S(1)}, u32[]{:S(2)}, u32[]{:S(2)}) collective-permute-start(f32[8,768]{1,0:T(8,128)S(1)} %get-tuple-element.43), channel_id=1, source_target_pairs={{0,16},{16,32},{32,48},{48,64},{64,80},{80,96},{96,112},{112,0},{1... | collective-permute-start | bytes 73736 | tf_op jit(solution)/shard_map/ppermute | solution.py:534
  44.4 4.9 %shard_map.99 = (f32[4,4,512,128]{3,2,1,0:T(8,128)}, f32[64,128]{1,0:T(8,128)S(1)}) custom-call(s32[2]{0:T(128)S(1)} %compare_select_fusion.1.flags, f32[512,512]{1,0:T(8,128)S(1)} %get-tuple-element.35.z, f32[512,512]{1,0:T(8,128)S(1)} %get-tuple-element.32.invd, f32[8,640]{1,0:T(8,128)S(1)} %collective-permute-done.got_l, ...), custom_call_target="tpu_custom_call" | custom-call | flops 20000000000 | tf_op jit(solution)/shard_map/pallas_call | solution.py:515
  49.4 1.7 %shard_map.101 = (f32[48,512]{1,0:T(8,128)S(1)}, f32[8,128]{1,0:T(8,128)}) custom-call(s32[2]{0:T(128)S(1)} %compare_select_fusion.1.flags, f32[512,512]{1,0:T(8,128)S(1)} %get-tuple-element.35.z, f32[512,512]{1,0:T(8,128)S(1)} %get-tuple-element.32.invd, f32[64,128]{1,0:T(8,128)S(1)} %get-tuple-element.42.corners, ...), custom_call_target="tpu_custom_call" | custom-call | tf_op jit(solution)/shard_map/pallas_call | solution.py:515
  51.0 5.5 %all-to-all-start.2 = ((f32[8,1,128]{2,1,0:T(1,128)}), f32[8,1,128]{2,1,0:T(1,128)S(1)}, u32[]{:S(2)}, u32[]{:S(2)}) async-start(f32[8,1,128]{2,1,0:T(1,128)} %bitcast.8), calls=%async_computation.2 | async-start | bytes 8192 | tf_op jit(solution)/shard_map/all_to_all | solution.py:538
  56.6 8.3 %shard_map.102.g = f32[128,128]{1,0:T(8,128)S(1)} custom-call(s32[32,128]{1,0:T(8,128)S(1)} %get-tuple-element.39.slots, f32[4,4,512,128]{3,2,1,0:T(8,128)} %get-tuple-element.38.hist, f32[48,512]{1,0:T(8,128)S(1)} %get-tuple-element.46.rims, s32[16,128]{1,0:T(8,128)S(1)} %bitcast.24, f32[16,128]{1,0:T(8,128)S(1)} %fusion.wt), custom_call_target="tpu_custom_call" | custom-call | flops 20000000000 | tf_op jit(solution)/shard_map/pallas_call | solution.py:515
  65.5 5.3 %all-to-all-start.3 = ((f32[16,8,128]{2,1,0:T(8,128)}), f32[16,8,128]{2,1,0:T(8,128)S(1)}, u32[]{:S(2)}, u32[]{:S(2)}) async-start(f32[16,8,128]{2,1,0:T(8,128)} %bitcast.10), calls=%async_computation.3 | async-start | bytes 131072 | tf_op jit(solution)/shard_map/all_to_all | solution.py:538
  70.9 1.1 %shard_map.104 = (f32[128,128]{1,0:T(8,128)S(1)}, f32[128,128]{1,0:T(8,128)S(1)}, f32[128,128]{1,0:T(8,128)S(1)}, bf16[128,2048]{1,0:T(8,128)(2,1)S(1)}, bf16[128,2048]{1,0:T(8,128)(2,1)S(1)}) custom-call(s32[2]{0:T(128)S(1)} %compare_select_fusion.1.flags, s32[16,128]{1,0:T(8,128)S(1)} %bitcast.17, f32[128,128]{1,0:T(8,128)S(1)} %copy-done, ...), custom_call_target="tpu_custom_call" | custom-call | flops 20000000000 | tf_op jit(solution)/shard_map/pallas_call | solution.py:515
  72.0 5.4 %all-to-all-done.3 = f32[16,8,128]{2,1,0:T(8,128)S(1)} async-done(((f32[16,8,128]{2,1,0:T(8,128)}), f32[16,8,128]{2,1,0:T(8,128)S(1)}, u32[]{:S(2)}, u32[]{:S(2)}) %all-to-all-start.3) | async-done | bytes 65568 | tf_op jit(solution)/shard_map/all_to_all | solution.py:538
  77.4 1.3 %shard_map.105 = (f32[8,128]{1,0:T(8,128)S(1)}, f32[128,128]{1,0:T(8,128)S(1)}, f32[128,128]{1,0:T(8,128)S(1)}, f32[8,128]{1,0:T(8,128)S(1)}, f32[8,128]{1,0:T(8...) custom-call(f32[128,128]{1,0:T(8,128)S(1)} %bitcast.15, f32[128,128]{1,0:T(8,128)S(1)} %get-tuple-element.48.scale, ...), custom_call_target="tpu_custom_call" | custom-call | tf_op jit(solution)/shard_map/pallas_call | solution.py:515
  79.0 4.5 %collective-permute-start.5 = (f32[8,128]{1,0:T(8,128)S(1)}, f32[8,128]{1,0:T(8,128)S(1)}, u32[]{:S(2)}, u32[]{:S(2)}) collective-permute-start(f32[8,128]{1,0:T(8,128)S(1)} %get-tuple-element.57), channel_id=1, source_target_pairs={{1,0},{2,1},{3,2},{4,3},{5,4},{6,5},{7,6},{8,7},{9,8},{10,9},{11,1... | collective-permute-start | bytes 12296 | tf_op jit(solution)/shard_map/ppermute | solution.py:534
  83.5 3.6 %collective-permute-start.6 = (f32[8,128]{1,0:T(8,128)S(1)}, f32[8,128]{1,0:T(8,128)S(1)}, u32[]{:S(2)}, u32[]{:S(2)}) collective-permute-start(f32[8,128]{1,0:T(8,128)S(1)} %get-tuple-element.58), channel_id=1, source_target_pairs={{0,16},{16,32},{32,48},{48,64},{64,80},{80,96},{96,112},{112,0},{1... | collective-permute-start | bytes 12296 | tf_op jit(solution)/shard_map/ppermute | solution.py:534
  87.2 3.1 %shard_map.106 = f32[512,512]{1,0:T(8,128)} custom-call(f32[4,4,512,128]{3,2,1,0:T(8,128)} %get-tuple-element.38.hist, f32[8,128]{1,0:T(8,128)S(1)} %get-tuple-element.52.coef, f32[48,512]{1,0:T(8,128)S(1)} %get-tuple-element.46.rims), custom_call_target="tpu_custom_call" | custom-call | flops 5000000000 | tf_op jit(solution)/shard_map/pallas_call | solution.py:515
  90.3 1.5 %shard_map.107 = f32[128,128]{1,0:T(8,128)} custom-call(s32[2]{0:T(128)S(1)} %compare_select_fusion.1.flags, f32[128,128]{1,0:T(8,128)S(1)} %get-tuple-element.53.u, f32[128,128]{1,0:T(8,128)S(1)} %get-tuple-element.54.src, f32[128,128]{1,0:T(8,128)S(1)} %get-tuple-element.55.cdiag, f32[128,128]{1,0:T(8,128)S(1)} %get-tuple-element.48.scale, ...), custom_call_target="tpu_custom_call" | custom-call | tf_op jit(solution)/shard_map/pallas_call | solution.py:515
  (24 shorter events, 2.2 us)
Async XLA Ops:
  2.0 13.9 %all-to-all-start = ((s32[16,1,128]{2,1,0:T(1,128)}), s32[16,1,128]{2,1,0:T(1,128)S(1)}, u32[]{:S(2)}, u32[]{:S(2)}) async-start(s32[16,1,128]{2,1,0:T(1,128)} %compare_select_fusion), calls=%async_computation | async-start | bytes 16384 | tf_op jit(solution)/shard_map/all_to_all | solution.py:538
  10.3 0.7 copy-start.1
  11.0 4.9 %copy-start = (f32[128,128]{1,0:T(8,128)S(1)}, f32[128,128]{1,0:T(8,128)}, u32[]{:S(2)}) copy-start(f32[128,128]{1,0:T(8,128)} %volt.7) | copy-start | bytes 196612
  11.0 19.0 %copy-start.2 = (s32[1,2048]{1,0:T(1,128)S(1)}, s32[1,2048]{1,0:T(1,128)}, u32[]{:S(2)}) copy-start(s32[1,2048]{1,0:T(1,128)} %param.13) | copy-start | bytes 24580
  17.2 12.8 %all-to-all-start.1 = ((f32[16,1,128]{2,1,0:T(1,128)}), f32[16,1,128]{2,1,0:T(1,128)S(1)}, u32[]{:S(2)}, u32[]{:S(2)}) async-start(f32[16,1,128]{2,1,0:T(1,128)} %bitcast.5), calls=%async_computation.1 | async-start | bytes 16384 | tf_op jit(solution)/shard_map/all_to_all | solution.py:538
  31.2 7.6 %collective-permute-start = (f32[8,640]{1,0:T(8,128)S(1)}, f32[8,640]{1,0:T(8,128)S(1)}, u32[]{:S(2)}, u32[]{:S(2)}) collective-permute-start(f32[8,640]{1,0:T(8,128)S(1)} %get-tuple-element.36), channel_id=1, source_target_pairs={{0,1},{1,2},{2,3},{3,4},{4,5},{5,6},{6,7},{7,8},{8,9},{9,10},{10,1... | collective-permute-start | bytes 61448 | tf_op jit(solution)/shard_map/ppermute | solution.py:534
  31.5 7.4 %collective-permute-start.1 = (f32[8,640]{1,0:T(8,128)S(1)}, f32[8,640]{1,0:T(8,128)S(1)}, u32[]{:S(2)}, u32[]{:S(2)}) collective-permute-start(f32[8,640]{1,0:T(8,128)S(1)} %get-tuple-element.37), channel_id=1, source_target_pairs={{1,0},{2,1},{3,2},{4,3},{5,4},{6,5},{7,6},{8,7},{9,8},{10,9},{11,1... | collective-permute-start | bytes 61448 | tf_op jit(solution)/shard_map/ppermute | solution.py:534
  39.6 9.7 %collective-permute-start.2 = (f32[8,768]{1,0:T(8,128)S(1)}, f32[8,768]{1,0:T(8,128)S(1)}, u32[]{:S(2)}, u32[]{:S(2)}) collective-permute-start(f32[8,768]{1,0:T(8,128)S(1)} %get-tuple-element.43), channel_id=1, source_target_pairs={{0,16},{16,32},{32,48},{48,64},{64,80},{80,96},{96,112},{112,0},{1... | collective-permute-start | bytes 73736 | tf_op jit(solution)/shard_map/ppermute | solution.py:534
  44.4 5.0 %collective-permute-start.3 = (f32[8,768]{1,0:T(8,128)S(1)}, f32[8,768]{1,0:T(8,128)S(1)}, u32[]{:S(2)}, u32[]{:S(2)}) collective-permute-start(f32[8,768]{1,0:T(8,128)S(1)} %get-tuple-element.44), channel_id=1, source_target_pairs={{16,0},{32,16},{48,32},{64,48},{80,64},{96,80},{112,96},{0,112},{1... | collective-permute-start | bytes 73736 | tf_op jit(solution)/shard_map/ppermute | solution.py:534
  51.0 13.8 %all-to-all-start.2 = ((f32[8,1,128]{2,1,0:T(1,128)}), f32[8,1,128]{2,1,0:T(1,128)S(1)}, u32[]{:S(2)}, u32[]{:S(2)}) async-start(f32[8,1,128]{2,1,0:T(1,128)} %bitcast.8), calls=%async_computation.2 | async-start | bytes 8192 | tf_op jit(solution)/shard_map/all_to_all | solution.py:538
  56.6 14.3 %copy-start.3 = (f32[128,128]{1,0:T(8,128)S(1)}, f32[128,128]{1,0:T(8,128)}, u32[]{:S(2)}) copy-start(f32[128,128]{1,0:T(8,128)} %cleak.1) | copy-start | bytes 196612
  65.5 11.8 %all-to-all-start.3 = ((f32[16,8,128]{2,1,0:T(8,128)}), f32[16,8,128]{2,1,0:T(8,128)S(1)}, u32[]{:S(2)}, u32[]{:S(2)}) async-start(f32[16,8,128]{2,1,0:T(8,128)} %bitcast.10), calls=%async_computation.3 | async-start | bytes 131072 | tf_op jit(solution)/shard_map/all_to_all | solution.py:538
  78.7 11.5 %collective-permute-start.4 = (f32[8,128]{1,0:T(8,128)S(1)}, f32[8,128]{1,0:T(8,128)S(1)}, u32[]{:S(2)}, u32[]{:S(2)}) collective-permute-start(f32[8,128]{1,0:T(8,128)S(1)} %get-tuple-element.56), channel_id=1, source_target_pairs={{0,1},{1,2},{2,3},{3,4},{4,5},{5,6},{6,7},{7,8},{8,9},{9,10},{10,1... | collective-permute-start | bytes 12296 | tf_op jit(solution)/shard_map/ppermute | solution.py:534
  79.0 11.2 %collective-permute-start.5 = (f32[8,128]{1,0:T(8,128)S(1)}, f32[8,128]{1,0:T(8,128)S(1)}, u32[]{:S(2)}, u32[]{:S(2)}) collective-permute-start(f32[8,128]{1,0:T(8,128)S(1)} %get-tuple-element.57), channel_id=1, source_target_pairs={{1,0},{2,1},{3,2},{4,3},{5,4},{6,5},{7,6},{8,7},{9,8},{10,9},{11,1... | collective-permute-start | bytes 12296 | tf_op jit(solution)/shard_map/ppermute | solution.py:534
  83.5 6.7 %collective-permute-start.6 = (f32[8,128]{1,0:T(8,128)S(1)}, f32[8,128]{1,0:T(8,128)S(1)}, u32[]{:S(2)}, u32[]{:S(2)}) collective-permute-start(f32[8,128]{1,0:T(8,128)S(1)} %get-tuple-element.58), channel_id=1, source_target_pairs={{0,16},{16,32},{32,48},{48,64},{64,80},{80,96},{96,112},{112,0},{1... | collective-permute-start | bytes 12296 | tf_op jit(solution)/shard_map/ppermute | solution.py:534
  87.2 3.1 %collective-permute-start.7 = (f32[8,128]{1,0:T(8,128)S(1)}, f32[8,128]{1,0:T(8,128)S(1)}, u32[]{:S(2)}, u32[]{:S(2)}) collective-permute-start(f32[8,128]{1,0:T(8,128)S(1)} %get-tuple-element.59), channel_id=1, source_target_pairs={{16,0},{32,16},{48,32},{64,48},{80,64},{96,80},{112,96},{0,112},{1... | collective-permute-start | bytes 12296 | tf_op jit(solution)/shard_map/ppermute | solution.py:534

commit v5 on v4

--- a/solution.py
+++ b/solution.py
@@ -59,6 +59,16 @@
 
 def lanes(o):
     return slice(o * L, (o + 1) * L)
+
+
+def pair_order(place, low, high):
+    even = (place & 1) == 0
+    return jnp.where(even, high, low), jnp.where(even, low, high)
+
+
+def from_pairs(place, first, second):
+    even = (place & 1) == 0
+    return jnp.where(even, second, first), jnp.where(even, first, second)
 
 
 def diag_kernel(vf, wt, amp, mask, leak, zl, invd, strips, rims, slots, a_s, b_s):
@@ -81,10 +91,14 @@
     rims[8:16, :] = inv[T - 8 :]
 
 
-def lookup_kernel(held, volt, looked):
+def parts_kernel(volt, parts):
     v1, rest = hi_lo(volt[...].T)
     v2, v3 = hi_lo(rest)
-    v = jnp.concatenate([v3, v2, v1], axis=0).astype(BF16)
+    parts[...] = jnp.concatenate([v3, v2, v1], axis=0).astype(BF16)
+
+
+def lookup_kernel(held, parts, looked):
+    v = parts[...]
     for i in range(NO // 2):
         h = jnp.concatenate([held[2 * i : 2 * i + 1, :], held[2 * i + 1 : 2 * i + 2, :]], axis=1)
         y = jnp.dot(v, onehot(h >> 7, CB), preferred_element_type=F32)
@@ -95,7 +109,7 @@
         looked[2 * i + 1 : 2 * i + 2, :] = y[:, L:]
 
 
-def strips_kernel(vf, wt, at_via, strips, volt, a_o, send_l, send_r):
+def strips_kernel(flags, vf, wt, at_via, strips, volt, a_o, send_1, send_2):
     j = iota((8, L), 0)
     colid = jnp.where(j < 4, j, T - 8 + j)
     hs, ls = [], []
@@ -113,11 +127,13 @@
     inv = strips[8:16, :]
     z = strips[0:8, :] + (inj[0:8] + inj[8:16]) * inv
     low = iota((8, T), 0) < 4
-    send_l[:, :T] = jnp.where(low, z, pltpu.roll(inv, 4, 0))
-    send_r[:, :T] = jnp.where(low, pltpu.roll(z, 4, 0), inv)
     g, lane = iota((8, CB), 0), iota((8, CB), 1)
-    send_l[:, T:] = nt(jnp.where(lane == g * GROUP, 1.0, 0.0), volt[...], HI)
-    send_r[:, T:] = nt(jnp.where(lane == g * GROUP + GROUP - 1, 1.0, 0.0), volt[...], HI)
+    to_l = jnp.where(low, z, pltpu.roll(inv, 4, 0))
+    to_r = jnp.where(low, pltpu.roll(z, 4, 0), inv)
+    send_1[:, :T], send_2[:, :T] = pair_order(flags[1], to_l, to_r)
+    to_l = nt(jnp.where(lane == g * GROUP, 1.0, 0.0), volt[...], HI)
+    to_r = nt(jnp.where(lane == g * GROUP + GROUP - 1, 1.0, 0.0), volt[...], HI)
+    send_1[:, T:], send_2[:, T:] = pair_order(flags[1], to_l, to_r)
 
 
 def rhs_kernel(vf, wt, at_via, zl, invd, a, z, rims, b_s):
@@ -149,7 +165,8 @@
     return out[:, :L], out[:, L:]
 
 
-def edge_kernel(flags, zr, ir, got_l, got_r, volt, send_u, send_d, corners):
+def edge_kernel(flags, zr, ir, col_1, col_2, volt, send_1, send_2, corners):
+    got_l, got_r = from_pairs(flags[1], col_1[...], col_2[...])
     zt, it = halo_columns(flags, got_l[:, :L], got_r[:, :L])
     zb, ib = halo_columns(flags, got_l[:, T - L : T], got_r[:, T - L : T])
     for k, x in enumerate((zt[0:16], zb[L - 16 :], it[0:16], ib[L - 16 :])):
@@ -159,10 +176,10 @@
     it = jnp.concatenate([ir[0:8, :], it[0:8]], axis=1)
     zb = jnp.concatenate([zr[8:16, :], zb[L - 8 :]], axis=1)
     ib = jnp.concatenate([ir[8:16, :], ib[L - 8 :]], axis=1)
-    send_u[:, :W] = jnp.where(low, zt, pltpu.roll(it, 4, 0))
-    send_d[:, :W] = jnp.where(low, pltpu.roll(zb, 4, 0), ib)
-    send_u[:, W:] = volt[0:8, :]
-    send_d[:, W:] = volt[CB - 8 :, :]
+    to_u = jnp.where(low, zt, pltpu.roll(it, 4, 0))
+    to_d = jnp.where(low, pltpu.roll(zb, 4, 0), ib)
+    send_1[:, :W], send_2[:, :W] = pair_order(flags[0], to_u, to_d)
+    send_1[:, W:], send_2[:, W:] = pair_order(flags[0], volt[0:8, :], volt[CB - 8 :, :])
 
 
 def beside(block):
@@ -195,8 +212,8 @@
     return dz * z, dz * w, dw * w, dw * n1, dn1 * n1, dn1 * n2, dn2 * n2, n2 * dn3
 
 
-def basis_kernel(flags, z, invd, got_l, got_r, hist, acc_o, ie, ze, we, n1e, n2e, sem):
-    zc, ic = halo_columns(flags, got_l[:, :T], got_r[:, :T])
+def basis_kernel(flags, z, invd, col_1, col_2, hist, acc_o, ie, ze, we, n1e, n2e, sem):
+    zc, ic = halo_columns(flags, *from_pairs(flags[1], col_1[:, :T], col_2[:, :T]))
     zero = jnp.zeros((OFF, L), F32)
     own = pl.ds(OFF, T)
     for e in (ie, ze, we, n1e, n2e):
@@ -274,12 +291,12 @@
     return out
 
 
-def rim_kernel(flags, z, invd, corners, got_u, got_d, acc_i, rims, part):
+def rim_kernel(flags, z, invd, corners, row_1, row_2, acc_i, rims, part):
     up = jnp.where(flags[0] > 0, 1.0, 0.0)
     down = jnp.where(flags[0] < 7, 1.0, 0.0)
     low = iota((8, W), 0) < 4
     acc = [acc_i[8 * k : 8 * k + 8, :] for k in range(SUMS)]
-    top, bot = got_u[:, :W], got_d[:, :W]
+    top, bot = from_pairs(flags[0], row_1[:, :W], row_2[:, :W])
     for end in (0, 1):
         rows = slice(0, 16) if end == 0 else slice(T - 16, T)
         zc, ic = corners[16 * end : 16 * end + 16, :], corners[32 + 16 * end : 48 + 16 * end, :]
@@ -343,19 +360,13 @@
             x = slab[pl.ds(slots[o, j], 16), :]
             x = pltpu.roll(x, slots[NO + o, j], 1)
             acc = jnp.where(lane == j, x, acc)
-        f = vf[pl.ds(o, 1), :]
-        acc = jnp.where((sub & 3) == ((f >> 7) & 3), acc * wt[pl.ds(o, 1), :], 0.0)
+        f = vf[o : o + 1, :]
+        acc = jnp.where((sub & 3) == ((f >> 7) & 3), acc * wt[o : o + 1, :], 0.0)
         rows = [jnp.sum(acc[4 * k : 4 * k + 4, :], axis=0, keepdims=True) for k in range(4)]
-        g_o[pl.ds(pl.multiple_of(8 * o, 8), 8), :] = jnp.concatenate(
-            rows + [jnp.zeros((4, L), F32)], axis=0
-        )
-
-    def owners(i, carry):
-        owner(2 * i)
-        owner(2 * i + 1)
-        return carry
-
-    lax.fori_loop(0, NO // 2, owners, 0)
+        g_o[8 * o : 8 * o + 8, :] = jnp.concatenate(rows + [jnp.zeros((4, L), F32)], axis=0)
+
+    for o in range(NO):
+        owner(o)
 
 
 def pack_kernel(g, rows, out):
@@ -429,7 +440,10 @@
         copy.wait()
 
 
-def coarse_neighbours(flags, u, above, below, from_l, from_r):
+def coarse_neighbours(flags, u, row_1, row_2, col_1, col_2):
+    above, below = from_pairs(flags[0], row_1, row_2)
+    above, below = above[7:8, :], below[0:1, :]
+    from_l, from_r = from_pairs(flags[1], col_1, col_2)
     up = jnp.where(flags[0] > 0, 1.0, 0.0)
     down = jnp.where(flags[0] < 7, 1.0, 0.0)
     r, lane = iota((CB, CB), 0), iota((CB, CB), 1)
@@ -448,7 +462,7 @@
 
 
 def base_kernel(
-    flags, held, volt, cleak, got_l, got_r, got_u, got_d, cdiag, scale, base, r_o, c_o
+    flags, held, volt, cleak, col_1, col_2, row_1, row_2, cdiag, scale, base, r_o, c_o
 ):
     for o in range(NO):
         h = held[o : o + 1, :]
@@ -457,13 +471,13 @@
     count = nt(r_o[...], c_o[...])
     diag = 4.0 * coarse_conductance + cleak[...] + via_conductance * count
     u = volt[...]
-    near = coarse_neighbours(flags, u, got_u[7:8, W:], got_d[0:1, W:], got_l[:, T:], got_r[:, T:])
+    near = coarse_neighbours(flags, u, row_1[:, W:], row_2[:, W:], col_1[:, T:], col_2[:, T:])
     cdiag[...] = diag
     scale[...] = relaxation / diag
     base[...] = u - relaxation * (diag * u - coarse_conductance * near) / diag
 
 
-def sweep1_kernel(arrived, scale, base, r, c, coef, u_o, src_o, sl, sr, su, sd, v_s):
+def sweep1_kernel(flags, arrived, scale, base, r, c, coef, u_o, src_o, c1, c2, r1, r2, v_s):
     tot = arrived[4:5, :]
     for o in range(1, NO):
         tot += arrived[8 * o + 4 : 8 * o + 5, :]
@@ -484,14 +498,14 @@
     u_o[...] = u
     src_o[...] = src
     g, gl = iota((8, CB), 0), iota((8, CB), 1)
-    sl[...] = nt(jnp.where(gl == g * GROUP, 1.0, 0.0), u, HI)
-    sr[...] = nt(jnp.where(gl == g * GROUP + GROUP - 1, 1.0, 0.0), u, HI)
-    su[...] = u[0:8, :]
-    sd[...] = u[CB - 8 :, :]
-
-
-def sweep2_kernel(flags, u, src, cdiag, scale, got_l, got_r, got_u, got_d, u_o):
-    near = coarse_neighbours(flags, u[...], got_u[7:8, :], got_d[0:1, :], got_l[...], got_r[...])
+    to_l = nt(jnp.where(gl == g * GROUP, 1.0, 0.0), u, HI)
+    to_r = nt(jnp.where(gl == g * GROUP + GROUP - 1, 1.0, 0.0), u, HI)
+    c1[...], c2[...] = pair_order(flags[1], to_l, to_r)
+    r1[...], r2[...] = pair_order(flags[0], u[0:8, :], u[CB - 8 :, :])
+
+
+def sweep2_kernel(flags, u, src, cdiag, scale, col_1, col_2, row_1, row_2, u_o):
+    near = coarse_neighbours(flags, u[...], row_1[...], row_2[...], col_1[...], col_2[...])
     u_o[...] = u[...] + scale[...] * (src[...] - (cdiag[...] * u[...] - coarse_conductance * near))
 
 
@@ -523,15 +537,11 @@
     )(*([] if flags is None else [flags]), *args)
 
 
-def ring(axis):
+def exchange(axis, first, second):
     n = lax.axis_size(axis)
-    up = [(i, (i + 1) % n) for i in range(n)]
-    return up, [(b, a) for a, b in up]
-
-
-def swap(axis, to_low, to_high):
-    up, down = ring(axis)
-    return lax.ppermute(to_high, axis, up), lax.ppermute(to_low, axis, down)
+    near = [(i, i ^ 1) for i in range(n)]
+    far = [(i, ((i + 1) ^ 1) - 1 & (n - 1)) for i in range(n)]
+    return lax.ppermute(first, axis, near), lax.ppermute(second, axis, far)
 
 
 def spread(x, axis=COL):
@@ -561,27 +571,29 @@
         diag_kernel, [tile, tile, rim16, rim16, hbm((2 * NO, L), jnp.int32)],
         keep(fine, wt) + leave(load_amp, load_mask, leak), [hot, hot], flops=big,
     )
-    looked = call(lookup_kernel, [slots], keep(held, coarse_init))[0]
+    drops = call(parts_kernel, [vmem((3 * CB, CB), BF16)], leave(coarse_init))[0]
+    looked = call(lookup_kernel, [slots], keep(held, drops))[0]
     at_via = spread(looked)
-    a, send_l, send_r = call(
-        strips_kernel, [hot, side, side], keep(fine, wt, at_via, strips, coarse_init)
-    )
-    got_l, got_r = swap(COL, send_l, send_r)
+    a, send_1, send_2 = call(
+        strips_kernel, [hot, side, side], keep(fine, wt, at_via, strips, coarse_init), flags=flags
+    )
+    col_1, col_2 = exchange(COL, send_1, send_2)
     z, zrims = call(
         rhs_kernel, [tile, rim16], keep(fine, wt, at_via, zl, invd, a), [hots], flops=big
     )
     rim = vmem((8, W + CB), F32)
-    send_u, send_d, corners = call(
-        edge_kernel, [rim, rim, vmem((64, L), F32)], keep(zrims, irims, got_l, got_r, coarse_init), flags=flags
-    )
-    got_u, got_d = swap(ROW, send_u, send_d)
+    send_1, send_2, corners = call(
+        edge_kernel, [rim, rim, vmem((64, L), F32)],
+        keep(zrims, irims, col_1, col_2, coarse_init), flags=flags,
+    )
+    row_1, row_2 = exchange(ROW, send_1, send_2)
     hist, acc = call(
-        basis_kernel, [pltpu.MemorySpace.HBM((4, LT, T, L), F32), vmem((8 * SUMS, L), F32)], keep(z, invd, got_l, got_r),
+        basis_kernel, [pltpu.MemorySpace.HBM((4, LT, T, L), F32), vmem((8 * SUMS, L), F32)], keep(z, invd, col_1, col_2),
         [ext] * 5 + [dmas], flags=flags, flops=big, any_out=1,
     )
     rims, part = call(
         rim_kernel, [vmem((48, T), F32), vmem((8, L), F32)],
-        keep(z, invd, corners, got_u, got_d, acc), flags=flags,
+        keep(z, invd, corners, row_1, row_2, acc), flags=flags,
     )
     rows = spread(part, ROW)
     g = call(
@@ -591,21 +603,21 @@
     arrived = spread(call(pack_kernel, [vmem(*packed)], keep(g, rows))[0])
     cdiag, scale, base, r_hot, c_hot = call(
         base_kernel, [block, block, block, chot, chot],
-        keep(held, coarse_init, coarse_leak, got_l, got_r, got_u, got_d), flags=flags, flops=big,
-    )
-    coef, u, src, sl, sr, su, sd = call(
+        keep(held, coarse_init, coarse_leak, col_1, col_2, row_1, row_2), flags=flags, flops=big,
+    )
+    coef, u, src, c1, c2, r1, r2 = call(
         sweep1_kernel, [seam, block, block, seam, seam, seam, seam],
-        keep(arrived, scale, base, r_hot, c_hot), [vmem((CB, 2 * NO * L), BF16)],
-    )
-    hl, hr = swap(COL, sl, sr)
-    hu, hd = swap(ROW, su, sd)
+        keep(arrived, scale, base, r_hot, c_hot), [vmem((CB, 2 * NO * L), BF16)], flags=flags,
+    )
+    c1, c2 = exchange(COL, c1, c2)
+    r1, r2 = exchange(ROW, r1, r2)
     fine_drop = call(
         combine_kernel, [pltpu.MemorySpace.HBM((T, T), F32)], leave(hist) + keep(coef, rims),
         [vmem((STEPS, 4, LT, T // STEPS, L), F32), tile, pltpu.SemaphoreType.DMA((STEPS,)),
          pltpu.SemaphoreType.DMA((STEPS,))], flops=big // 4, any_in=1, any_out=1,
     )[0]
     coarse_drop = call(
-        sweep2_kernel, [hbm((CB, CB), F32)], keep(u, src, cdiag, scale, hl, hr, hu, hd), flags=flags
+        sweep2_kernel, [hbm((CB, CB), F32)], keep(u, src, cdiag, scale, c1, c2, r1, r2), flags=flags
     )[0]
     return fine_drop, coarse_drop
 

time: 92.3 us -> 88.9 us (0.963)
  starting transfers between devices: 42.9 us -> 36.4 us
  Pallas kernels: 33.3 us -> 34.8 us
  waiting for transfers between devices: 12 us -> 13.3 us
    ppermute x8, starting transfers between devices: 18 us -> 12.9 us  [exchange(): return (lax.ppermute(first, axis, near), lax.ppermute(second, axis, far))]
    ppermute x8, waiting for transfers between devices: 0.02 us -> 1.61 us  [exchange(): return (lax.ppermute(first, axis, near), lax.ppermute(second, axis, far))]
    pallas_call x13 -> x14, Pallas kernels: 33.3 us -> 34.8 us  [call(): pl.pallas_call(body, out_shape=outs, in_specs=specs, out_specs=[ANY] * an...]
    all_to_all x4, starting transfers between devices: 24.9 us -> 23.5 us  [spread(): return lax.all_to_all(x, axis, split_axis=0, concat_axis=0, tiled=True)]
  transfers between devices with their start and end apart: 12 -> 12, of which waited for: 3 -> 3; matrix products, arithmetic and copies ran while one was open for 1% -> 1% of each run, Pallas kernels for 27% -> 29%
where the time goes in v5:
time: 88.9 us; the launch traced here: 88 us
  starting transfers between devices  36.4 us (41%)
  Pallas kernels  34.8 us (39%)
  waiting for transfers between devices  13.3 us (15%)
  other arithmetic  2.12 us (2%)
    pallas_call x14, Pallas kernels, call(): pl.pallas_call(body, out_shape=outs, in_specs=specs, out_specs=[ANY] * an...  34.8 us
    all_to_all x4, starting transfers between devices, spread(): return lax.all_to_all(x, axis, split_axis=0, concat_axis=0, tiled=True)  23.5 us
    ppermute x8, starting transfers between devices, exchange(): return (lax.ppermute(first, axis, near), lax.ppermute(second, axis, far))  12.9 us
    all_to_all x4, waiting for transfers between devices, spread(): return lax.all_to_all(x, axis, split_axis=0, concat_axis=0, tiled=True)  11.6 us
  transfers between devices with their start and end apart: 12, of which 3 were waited for; matrix products, arithmetic and copies ran while one was open for 1% of the time, Pallas kernels for 29%

profile of v5, /device:TPU:1, one launch (start us, length us, event | category | flops | bytes accessed | tf_op | source)
XLA Modules:
  0.0 88.0 jit_solution(3253274005101361820)
XLA Ops:
  0.6 1.4 %compare_select_fusion = s32[16,1,128]{2,1,0:T(1,128)} fusion(s32[1,2048]{1,0:T(1,128)} %param.14, s32[16]{0:T(128)} %bitcast.25), kind=kLoop, calls=%fused_computation | loop fusion | flops 12288 | bytes 16448 | tf_op jit(solution)/shard_map/jit(_where)/select_n | solution.py:559
  2.0 7.6 %all-to-all-start = ((s32[16,1,128]{2,1,0:T(1,128)}), s32[16,1,128]{2,1,0:T(1,128)S(1)}, u32[]{:S(2)}, u32[]{:S(2)}) async-start(s32[16,1,128]{2,1,0:T(1,128)} %compare_select_fusion), calls=%async_computation | async-start | bytes 16384 | tf_op jit(solution)/shard_map/all_to_all | solution.py:548
  11.0 4.7 %shard_map.97 = (f32[512,512]{1,0:T(8,128)S(1)}, f32[512,512]{1,0:T(8,128)S(1)}, f32[16,512]{1,0:T(8,128)S(1)}, f32[16,512]{1,0:T(8,128)S(1)}, s32[32,128]{1,0:T(8,128)S(1)}) custom-call(s32[16,128]{1,0:T(8,128)S(1)} %bitcast.21, f32[16,128]{1,0:T(8,128)S(1)} %fusion.wt, f32[512,512]{1,0:T(8,128)} %amp.1, s32[512,512]{1,0:T(8,128)} %mask.1, f32[512,512]{1,0:T(8,128)} %leak.1), custom_call_target="tpu_custom_call" | custom-call | flops 20000000000 | tf_op jit(solution)/shard_map/pallas_call | solution.py:529
  16.7 1.2 %shard_map.96 = f32[16,128]{1,0:T(8,128)} custom-call(s32[16,128]{1,0:T(8,128)S(1)} %bitcast.16, bf16[384,128]{1,0:T(8,128)(2,1)S(1)} %shard_map.95.parts), custom_call_target="tpu_custom_call" | custom-call | tf_op jit(solution)/shard_map/pallas_call | solution.py:529
  17.9 6.7 %all-to-all-start.1 = ((f32[16,1,128]{2,1,0:T(1,128)}), f32[16,1,128]{2,1,0:T(1,128)S(1)}, u32[]{:S(2)}, u32[]{:S(2)}) async-start(f32[16,1,128]{2,1,0:T(1,128)} %bitcast.5), calls=%async_computation.1 | async-start | bytes 16384 | tf_op jit(solution)/shard_map/all_to_all | solution.py:548
  24.6 6.3 %all-to-all-done.1 = f32[16,1,128]{2,1,0:T(1,128)S(1)} async-done(((f32[16,1,128]{2,1,0:T(1,128)}), f32[16,1,128]{2,1,0:T(1,128)S(1)}, u32[]{:S(2)}, u32[]{:S(2)}) %all-to-all-start.1) | async-done | bytes 8224 | tf_op jit(solution)/shard_map/all_to_all | solution.py:548
  30.9 1.7 %shard_map.98 = (bf16[512,2048]{1,0:T(8,128)(2,1)S(1)}, f32[8,640]{1,0:T(8,128)S(1)}, f32[8,640]{1,0:T(8,128)S(1)}) custom-call(s32[2]{0:T(128)S(1)} %compare_select_fusion.1.flags, s32[16,128]{1,0:T(8,128)S(1)} %bitcast.22, f32[16,128]{1,0:T(8,128)S(1)} %fusion.wt, f32[16,128]{1,0:T(8,128)S(1)} %bitcast.18, f32[16,512]{1,0:T(8,128)S(1)} %get-tuple-element.33.strips, ...), custom_call_target="tpu_custom_call" | custom-call | tf_op jit(solution)/shard_map/pallas_call | solution.py:529
  32.9 1.5 %collective-permute-start.1 = (f32[8,640]{1,0:T(8,128)S(1)}, f32[8,640]{1,0:T(8,128)S(1)}, u32[]{:S(2)}, u32[]{:S(2)}) collective-permute-start(f32[8,640]{1,0:T(8,128)S(1)} %get-tuple-element.37), channel_id=1, source_target_pairs={{0,15},{1,2},{2,1},{3,4},{4,3},{5,6},{6,5},{7,8},{8,7},{9,10},{10,... | collective-permute-start | bytes 61448 | tf_op jit(solution)/shard_map/ppermute | solution.py:544
  34.5 2.8 %shard_map.99 = (f32[512,512]{1,0:T(8,128)S(1)}, f32[16,512]{1,0:T(8,128)S(1)}) custom-call(s32[16,128]{1,0:T(8,128)S(1)} %bitcast.23, f32[16,128]{1,0:T(8,128)S(1)} %fusion.wt, f32[16,128]{1,0:T(8,128)S(1)} %bitcast.19, f32[512,512]{1,0:T(8,128)S(1)} %get-tuple-element.31.zl, f32[512,512]{1,0:T(8,128)S(1)} %get-tuple-element.32.invd, ...), custom_call_target="tpu_custom_call" | custom-call | flops 20000000000 | tf_op jit(solution)/shard_map/pallas_call | solution.py:529
  37.3 1.6 %collective-permute-done.1.col_2 = f32[8,640]{1,0:T(8,128)S(1)} collective-permute-done((f32[8,640]{1,0:T(8,128)S(1)}, f32[8,640]{1,0:T(8,128)S(1)}, u32[]{:S(2)}, u32[]{:S(2)}) %collective-permute-start.1) | collective-permute-done | bytes 20512 | tf_op jit(solution)/shard_map/ppermute | solution.py:544
  39.7 4.2 %collective-permute-start.2 = (f32[8,768]{1,0:T(8,128)S(1)}, f32[8,768]{1,0:T(8,128)S(1)}, u32[]{:S(2)}, u32[]{:S(2)}) collective-permute-start(f32[8,768]{1,0:T(8,128)S(1)} %get-tuple-element.43), channel_id=1, source_target_pairs={{0,16},{16,0},{32,48},{48,32},{64,80},{80,64},{96,112},{112,96},{1... | collective-permute-start | bytes 73736 | tf_op jit(solution)/shard_map/ppermute | solution.py:544
  43.8 1.6 %collective-permute-start.3 = (f32[8,768]{1,0:T(8,128)S(1)}, f32[8,768]{1,0:T(8,128)S(1)}, u32[]{:S(2)}, u32[]{:S(2)}) collective-permute-start(f32[8,768]{1,0:T(8,128)S(1)} %get-tuple-element.44), channel_id=1, source_target_pairs={{0,112},{16,32},{32,16},{48,64},{64,48},{80,96},{96,80},{112,0},{1... | collective-permute-start | bytes 73736 | tf_op jit(solution)/shard_map/ppermute | solution.py:544
  45.4 4.9 %shard_map.100 = (f32[4,4,512,128]{3,2,1,0:T(8,128)}, f32[64,128]{1,0:T(8,128)S(1)}) custom-call(s32[2]{0:T(128)S(1)} %compare_select_fusion.1.flags, f32[512,512]{1,0:T(8,128)S(1)} %get-tuple-element.35.z, f32[512,512]{1,0:T(8,128)S(1)} %get-tuple-element.32.invd, f32[8,640]{1,0:T(8,128)S(1)} %collective-permute-done.col_1, ...), custom_call_target="tpu_custom_call" | custom-call | flops 20000000000 | tf_op jit(solution)/shard_map/pallas_call | solution.py:529
  50.4 1.7 %shard_map.102 = (f32[48,512]{1,0:T(8,128)S(1)}, f32[8,128]{1,0:T(8,128)}) custom-call(s32[2]{0:T(128)S(1)} %compare_select_fusion.1.flags, f32[512,512]{1,0:T(8,128)S(1)} %get-tuple-element.35.z, f32[512,512]{1,0:T(8,128)S(1)} %get-tuple-element.32.invd, f32[64,128]{1,0:T(8,128)S(1)} %get-tuple-element.42.corners, ...), custom_call_target="tpu_custom_call" | custom-call | tf_op jit(solution)/shard_map/pallas_call | solution.py:529
  52.1 5.8 %all-to-all-start.2 = ((f32[8,1,128]{2,1,0:T(1,128)}), f32[8,1,128]{2,1,0:T(1,128)S(1)}, u32[]{:S(2)}, u32[]{:S(2)}) async-start(f32[8,1,128]{2,1,0:T(1,128)} %bitcast.8), calls=%async_computation.2 | async-start | bytes 8192 | tf_op jit(solution)/shard_map/all_to_all | solution.py:548
  57.9 7.7 %shard_map.103.g = f32[128,128]{1,0:T(8,128)S(1)} custom-call(s32[32,128]{1,0:T(8,128)S(1)} %get-tuple-element.39.slots, f32[4,4,512,128]{3,2,1,0:T(8,128)} %get-tuple-element.38.hist, f32[48,512]{1,0:T(8,128)S(1)} %get-tuple-element.46.rims, s32[16,128]{1,0:T(8,128)S(1)} %bitcast.24, f32[16,128]{1,0:T(8,128)S(1)} %fusion.wt), custom_call_target="tpu_custom_call" | custom-call | flops 20000000000 | tf_op jit(solution)/shard_map/pallas_call | solution.py:529
  66.3 3.5 %all-to-all-start.3 = ((f32[16,8,128]{2,1,0:T(8,128)}), f32[16,8,128]{2,1,0:T(8,128)S(1)}, u32[]{:S(2)}, u32[]{:S(2)}) async-start(f32[16,8,128]{2,1,0:T(8,128)} %bitcast.10), calls=%async_computation.3 | async-start | bytes 131072 | tf_op jit(solution)/shard_map/all_to_all | solution.py:548
  70.9 5.3 %all-to-all-done.3 = f32[16,8,128]{2,1,0:T(8,128)S(1)} async-done(((f32[16,8,128]{2,1,0:T(8,128)}), f32[16,8,128]{2,1,0:T(8,128)S(1)}, u32[]{:S(2)}, u32[]{:S(2)}) %all-to-all-start.3) | async-done | bytes 65568 | tf_op jit(solution)/shard_map/all_to_all | solution.py:548
  76.2 1.9 %shard_map.106 = (f32[8,128]{1,0:T(8,128)S(1)}, f32[128,128]{1,0:T(8,128)S(1)}, f32[128,128]{1,0:T(8,128)S(1)}, f32[8,128]{1,0:T(8,128)S(1)}, f32[8,128]{1,0:T(8...) custom-call(s32[2]{0:T(128)S(1)} %compare_select_fusion.1.flags, f32[128,128]{1,0:T(8,128)S(1)} %bitcast.15, ...), custom_call_target="tpu_custom_call" | custom-call | tf_op jit(solution)/shard_map/pallas_call | solution.py:529
  78.4 1.9 %collective-permute-start.5 = (f32[8,128]{1,0:T(8,128)S(1)}, f32[8,128]{1,0:T(8,128)S(1)}, u32[]{:S(2)}, u32[]{:S(2)}) collective-permute-start(f32[8,128]{1,0:T(8,128)S(1)} %get-tuple-element.57), channel_id=1, source_target_pairs={{0,15},{1,2},{2,1},{3,4},{4,3},{5,6},{6,5},{7,8},{8,7},{9,10},{10,... | collective-permute-start | bytes 12296 | tf_op jit(solution)/shard_map/ppermute | solution.py:544
  80.3 1.7 %collective-permute-start.6 = (f32[8,128]{1,0:T(8,128)S(1)}, f32[8,128]{1,0:T(8,128)S(1)}, u32[]{:S(2)}, u32[]{:S(2)}) collective-permute-start(f32[8,128]{1,0:T(8,128)S(1)} %get-tuple-element.58), channel_id=1, source_target_pairs={{0,16},{16,0},{32,48},{48,32},{64,80},{80,64},{96,112},{112,96},{1... | collective-permute-start | bytes 12296 | tf_op jit(solution)/shard_map/ppermute | solution.py:544
  82.0 1.3 %collective-permute-start.7 = (f32[8,128]{1,0:T(8,128)S(1)}, f32[8,128]{1,0:T(8,128)S(1)}, u32[]{:S(2)}, u32[]{:S(2)}) collective-permute-start(f32[8,128]{1,0:T(8,128)S(1)} %get-tuple-element.59), channel_id=1, source_target_pairs={{0,112},{16,32},{32,16},{48,64},{64,48},{80,96},{96,80},{112,0},{1... | collective-permute-start | bytes 12296 | tf_op jit(solution)/shard_map/ppermute | solution.py:544
  83.4 3.1 %shard_map.107 = f32[512,512]{1,0:T(8,128)} custom-call(f32[4,4,512,128]{3,2,1,0:T(8,128)} %get-tuple-element.38.hist, f32[8,128]{1,0:T(8,128)S(1)} %get-tuple-element.52.coef, f32[48,512]{1,0:T(8,128)S(1)} %get-tuple-element.46.rims), custom_call_target="tpu_custom_call" | custom-call | flops 5000000000 | tf_op jit(solution)/shard_map/pallas_call | solution.py:529
  86.5 1.5 %shard_map.108 = f32[128,128]{1,0:T(8,128)} custom-call(s32[2]{0:T(128)S(1)} %compare_select_fusion.1.flags, f32[128,128]{1,0:T(8,128)S(1)} %get-tuple-element.53.u, f32[128,128]{1,0:T(8,128)S(1)} %get-tuple-element.54.src, f32[128,128]{1,0:T(8,128)S(1)} %get-tuple-element.55.cdiag, f32[128,128]{1,0:T(8,128)S(1)} %get-tuple-element.48.scale, ...), custom_call_target="tpu_custom_call" | custom-call | tf_op jit(solution)/shard_map/pallas_call | solution.py:529
  (25 shorter events, 5.6 us)
Async XLA Ops:
  2.0 14.7 %all-to-all-start = ((s32[16,1,128]{2,1,0:T(1,128)}), s32[16,1,128]{2,1,0:T(1,128)S(1)}, u32[]{:S(2)}, u32[]{:S(2)}) async-start(s32[16,1,128]{2,1,0:T(1,128)} %compare_select_fusion), calls=%async_computation | async-start | bytes 16384 | tf_op jit(solution)/shard_map/all_to_all | solution.py:548
  10.3 0.7 copy-start.1
  11.0 19.9 %copy-start = (f32[128,128]{1,0:T(8,128)S(1)}, f32[128,128]{1,0:T(8,128)}, u32[]{:S(2)}) copy-start(f32[128,128]{1,0:T(8,128)} %volt.7) | copy-start | bytes 196612
  11.0 19.9 %copy-start.2 = (s32[1,2048]{1,0:T(1,128)S(1)}, s32[1,2048]{1,0:T(1,128)}, u32[]{:S(2)}) copy-start(s32[1,2048]{1,0:T(1,128)} %param.13) | copy-start | bytes 24580
  17.9 13.0 %all-to-all-start.1 = ((f32[16,1,128]{2,1,0:T(1,128)}), f32[16,1,128]{2,1,0:T(1,128)S(1)}, u32[]{:S(2)}, u32[]{:S(2)}) async-start(f32[16,1,128]{2,1,0:T(1,128)} %bitcast.5), calls=%async_computation.1 | async-start | bytes 16384 | tf_op jit(solution)/shard_map/all_to_all | solution.py:548
  32.6 4.7 %collective-permute-start = (f32[8,640]{1,0:T(8,128)S(1)}, f32[8,640]{1,0:T(8,128)S(1)}, u32[]{:S(2)}, u32[]{:S(2)}) collective-permute-start(f32[8,640]{1,0:T(8,128)S(1)} %get-tuple-element.36), channel_id=1, source_target_pairs={{0,1},{1,0},{2,3},{3,2},{4,5},{5,4},{6,7},{7,6},{8,9},{9,8},{10,11... | collective-permute-start | bytes 61448 | tf_op jit(solution)/shard_map/ppermute | solution.py:544
  32.9 6.0 %collective-permute-start.1 = (f32[8,640]{1,0:T(8,128)S(1)}, f32[8,640]{1,0:T(8,128)S(1)}, u32[]{:S(2)}, u32[]{:S(2)}) collective-permute-start(f32[8,640]{1,0:T(8,128)S(1)} %get-tuple-element.37), channel_id=1, source_target_pairs={{0,15},{1,2},{2,1},{3,4},{4,3},{5,6},{6,5},{7,8},{8,7},{9,10},{10,... | collective-permute-start | bytes 61448 | tf_op jit(solution)/shard_map/ppermute | solution.py:544
  39.7 10.7 %collective-permute-start.2 = (f32[8,768]{1,0:T(8,128)S(1)}, f32[8,768]{1,0:T(8,128)S(1)}, u32[]{:S(2)}, u32[]{:S(2)}) collective-permute-start(f32[8,768]{1,0:T(8,128)S(1)} %get-tuple-element.43), channel_id=1, source_target_pairs={{0,16},{16,0},{32,48},{48,32},{64,80},{80,64},{96,112},{112,96},{1... | collective-permute-start | bytes 73736 | tf_op jit(solution)/shard_map/ppermute | solution.py:544
  43.8 6.6 %collective-permute-start.3 = (f32[8,768]{1,0:T(8,128)S(1)}, f32[8,768]{1,0:T(8,128)S(1)}, u32[]{:S(2)}, u32[]{:S(2)}) collective-permute-start(f32[8,768]{1,0:T(8,128)S(1)} %get-tuple-element.44), channel_id=1, source_target_pairs={{0,112},{16,32},{32,16},{48,64},{64,48},{80,96},{96,80},{112,0},{1... | collective-permute-start | bytes 73736 | tf_op jit(solution)/shard_map/ppermute | solution.py:544
  52.1 13.5 %all-to-all-start.2 = ((f32[8,1,128]{2,1,0:T(1,128)}), f32[8,1,128]{2,1,0:T(1,128)S(1)}, u32[]{:S(2)}, u32[]{:S(2)}) async-start(f32[8,1,128]{2,1,0:T(1,128)} %bitcast.8), calls=%async_computation.2 | async-start | bytes 8192 | tf_op jit(solution)/shard_map/all_to_all | solution.py:548
  57.8 11.9 %copy-start.3 = (f32[128,128]{1,0:T(8,128)S(1)}, f32[128,128]{1,0:T(8,128)}, u32[]{:S(2)}) copy-start(f32[128,128]{1,0:T(8,128)} %cleak.1) | copy-start | bytes 196612
  66.3 10.0 %all-to-all-start.3 = ((f32[16,8,128]{2,1,0:T(8,128)}), f32[16,8,128]{2,1,0:T(8,128)S(1)}, u32[]{:S(2)}, u32[]{:S(2)}) async-start(f32[16,8,128]{2,1,0:T(8,128)} %bitcast.10), calls=%async_computation.3 | async-start | bytes 131072 | tf_op jit(solution)/shard_map/all_to_all | solution.py:548
  78.1 8.4 %collective-permute-start.4 = (f32[8,128]{1,0:T(8,128)S(1)}, f32[8,128]{1,0:T(8,128)S(1)}, u32[]{:S(2)}, u32[]{:S(2)}) collective-permute-start(f32[8,128]{1,0:T(8,128)S(1)} %get-tuple-element.56), channel_id=1, source_target_pairs={{0,1},{1,0},{2,3},{3,2},{4,5},{5,4},{6,7},{7,6},{8,9},{9,8},{10,11... | collective-permute-start | bytes 12296 | tf_op jit(solution)/shard_map/ppermute | solution.py:544
  78.4 8.0 %collective-permute-start.5 = (f32[8,128]{1,0:T(8,128)S(1)}, f32[8,128]{1,0:T(8,128)S(1)}, u32[]{:S(2)}, u32[]{:S(2)}) collective-permute-start(f32[8,128]{1,0:T(8,128)S(1)} %get-tuple-element.57), channel_id=1, source_target_pairs={{0,15},{1,2},{2,1},{3,4},{4,3},{5,6},{6,5},{7,8},{8,7},{9,10},{10,... | collective-permute-start | bytes 12296 | tf_op jit(solution)/shard_map/ppermute | solution.py:544
  80.3 6.2 %collective-permute-start.6 = (f32[8,128]{1,0:T(8,128)S(1)}, f32[8,128]{1,0:T(8,128)S(1)}, u32[]{:S(2)}, u32[]{:S(2)}) collective-permute-start(f32[8,128]{1,0:T(8,128)S(1)} %get-tuple-element.58), channel_id=1, source_target_pairs={{0,16},{16,0},{32,48},{48,32},{64,80},{80,64},{96,112},{112,96},{1... | collective-permute-start | bytes 12296 | tf_op jit(solution)/shard_map/ppermute | solution.py:544
  82.0 4.5 %collective-permute-start.7 = (f32[8,128]{1,0:T(8,128)S(1)}, f32[8,128]{1,0:T(8,128)S(1)}, u32[]{:S(2)}, u32[]{:S(2)}) collective-permute-start(f32[8,128]{1,0:T(8,128)S(1)} %get-tuple-element.59), channel_id=1, source_target_pairs={{0,112},{16,32},{32,16},{48,64},{64,48},{80,96},{96,80},{112,0},{1... | collective-permute-start | bytes 12296 | tf_op jit(solution)/shard_map/ppermute | solution.py:544

commit v6 on v5

--- a/solution.py
+++ b/solution.py
@@ -61,25 +61,36 @@
     return slice(o * L, (o + 1) * L)
 
 
-def pair_order(place, low, high):
-    even = (place & 1) == 0
+def at(pos, k, like):
+    return jnp.broadcast_to(pos[k : k + 1, : like.shape[1]], like.shape)
+
+
+def pair_order(pos, k, low, high):
+    even = (at(pos, k, low) & 1) == 0
     return jnp.where(even, high, low), jnp.where(even, low, high)
 
 
-def from_pairs(place, first, second):
-    even = (place & 1) == 0
+def from_pairs(pos, k, first, second):
+    even = (at(pos, k, first) & 1) == 0
     return jnp.where(even, second, first), jnp.where(even, first, second)
 
 
-def diag_kernel(vf, wt, amp, mask, leak, zl, invd, strips, rims, slots, a_s, b_s):
-    slots[0:NO, :] = (vf[...] >> 9) * SLAB
-    slots[NO:, :] = (iota((NO, L), 1) - vf[...]) & (L - 1)
+def diag_kernel(amp, mask, leak, vf, wt, zl, invd, strips, rims, a_s, b_s, amp_s, mask_s, leak_s, sem):
+    copies = [
+        pltpu.make_async_copy(x, y, sem.at[k])
+        for k, (x, y) in enumerate(((leak, leak_s), (amp, amp_s), (mask, mask_s)))
+    ]
+    for copy in copies:
+        copy.start()
     for o in range(NO):
         f = vf[o : o + 1, :]
         a_s[:, lanes(o)] = onehot(f // T, T)
         b_s[:, lanes(o)] = jnp.where(iota((T, L), 0) == f % T, wt[o : o + 1, :], 0.0).astype(BF16)
-    inv = 1.0 / (4.0 + leak[...] + nt(a_s[...], b_s[...]))
-    z = amp[...] * mask[...].astype(F32) * inv
+    via = nt(a_s[...], b_s[...])
+    for copy in copies:
+        copy.wait()
+    inv = 1.0 / (4.0 + leak_s[...] + via)
+    z = amp_s[...] * mask_s[...].astype(F32) * inv
     zl[...] = z
     invd[...] = inv
     j, lane = iota((8, L), 0), iota((8, L), 1)
@@ -91,7 +102,12 @@
     rims[8:16, :] = inv[T - 8 :]
 
 
-def parts_kernel(volt, parts):
+def parts_kernel(volt, vf, parts, slots, volt_o, vf_o):
+    volt_o[...] = volt[...]
+    vf_o[...] = vf[...]
+    f = vf[...]
+    slots[0:NO, :] = (f >> 9) * SLAB + ((f >> 7) & 3) * 4
+    slots[NO:, :] = (iota((NO, L), 1) - f) & (L - 1)
     v1, rest = hi_lo(volt[...].T)
     v2, v3 = hi_lo(rest)
     parts[...] = jnp.concatenate([v3, v2, v1], axis=0).astype(BF16)
@@ -109,7 +125,7 @@
         looked[2 * i + 1 : 2 * i + 2, :] = y[:, L:]
 
 
-def strips_kernel(flags, vf, wt, at_via, strips, volt, a_o, send_1, send_2):
+def strips_kernel(pos, vf, wt, at_via, strips, volt, a_o, send_1, send_2):
     j = iota((8, L), 0)
     colid = jnp.where(j < 4, j, T - 8 + j)
     hs, ls = [], []
@@ -130,10 +146,10 @@
     g, lane = iota((8, CB), 0), iota((8, CB), 1)
     to_l = jnp.where(low, z, pltpu.roll(inv, 4, 0))
     to_r = jnp.where(low, pltpu.roll(z, 4, 0), inv)
-    send_1[:, :T], send_2[:, :T] = pair_order(flags[1], to_l, to_r)
+    send_1[:, :T], send_2[:, :T] = pair_order(pos, 1, to_l, to_r)
     to_l = nt(jnp.where(lane == g * GROUP, 1.0, 0.0), volt[...], HI)
     to_r = nt(jnp.where(lane == g * GROUP + GROUP - 1, 1.0, 0.0), volt[...], HI)
-    send_1[:, T:], send_2[:, T:] = pair_order(flags[1], to_l, to_r)
+    send_1[:, T:], send_2[:, T:] = pair_order(pos, 1, to_l, to_r)
 
 
 def rhs_kernel(vf, wt, at_via, zl, invd, a, z, rims, b_s):
@@ -149,11 +165,10 @@
     rims[8:16, :] = zz[T - 8 :]
 
 
-def halo_columns(flags, gl, gr):
-    left = jnp.where(flags[1] > 0, 1.0, 0.0)
-    right = jnp.where(flags[1] < NO - 1, 1.0, 0.0)
+def halo_columns(pos, gl, gr):
+    place = at(pos, 1, gl)
     parts = []
-    for x in (gr * right, gl * left):
+    for x in (jnp.where(place < NO - 1, gr, 0.0), jnp.where(place > 0, gl, 0.0)):
         a, rest = hi_lo(x)
         b, c = hi_lo(rest)
         parts += [c, b, a]
@@ -165,10 +180,10 @@
     return out[:, :L], out[:, L:]
 
 
-def edge_kernel(flags, zr, ir, col_1, col_2, volt, send_1, send_2, corners):
-    got_l, got_r = from_pairs(flags[1], col_1[...], col_2[...])
-    zt, it = halo_columns(flags, got_l[:, :L], got_r[:, :L])
-    zb, ib = halo_columns(flags, got_l[:, T - L : T], got_r[:, T - L : T])
+def edge_kernel(pos, zr, ir, col_1, col_2, volt, send_1, send_2, corners):
+    got_l, got_r = from_pairs(pos, 1, col_1[...], col_2[...])
+    zt, it = halo_columns(pos, got_l[:, :L], got_r[:, :L])
+    zb, ib = halo_columns(pos, got_l[:, T - L : T], got_r[:, T - L : T])
     for k, x in enumerate((zt[0:16], zb[L - 16 :], it[0:16], ib[L - 16 :])):
         corners[16 * k : 16 * k + 16, :] = x
     low = iota((8, W), 0) < 4
@@ -178,8 +193,8 @@
     ib = jnp.concatenate([ir[8:16, :], ib[L - 8 :]], axis=1)
     to_u = jnp.where(low, zt, pltpu.roll(it, 4, 0))
     to_d = jnp.where(low, pltpu.roll(zb, 4, 0), ib)
-    send_1[:, :W], send_2[:, :W] = pair_order(flags[0], to_u, to_d)
-    send_1[:, W:], send_2[:, W:] = pair_order(flags[0], volt[0:8, :], volt[CB - 8 :, :])
+    send_1[:, :W], send_2[:, :W] = pair_order(pos, 0, to_u, to_d)
+    send_1[:, W:], send_2[:, W:] = pair_order(pos, 0, volt[0:8, :], volt[CB - 8 :, :])
 
 
 def beside(block):
@@ -212,8 +227,8 @@
     return dz * z, dz * w, dw * w, dw * n1, dn1 * n1, dn1 * n2, dn2 * n2, n2 * dn3
 
 
-def basis_kernel(flags, z, invd, col_1, col_2, hist, acc_o, ie, ze, we, n1e, n2e, sem):
-    zc, ic = halo_columns(flags, *from_pairs(flags[1], col_1[:, :T], col_2[:, :T]))
+def basis_kernel(pos, z, invd, col_1, col_2, hist, acc_o, ie, ze, we, n1e, n2e, sem):
+    zc, ic = halo_columns(pos, *from_pairs(pos, 1, col_1[:, :T], col_2[:, :T]))
     zero = jnp.zeros((OFF, L), F32)
     own = pl.ds(OFF, T)
     for e in (ie, ze, we, n1e, n2e):
@@ -291,24 +306,24 @@
     return out
 
 
-def rim_kernel(flags, z, invd, corners, row_1, row_2, acc_i, rims, part):
-    up = jnp.where(flags[0] > 0, 1.0, 0.0)
-    down = jnp.where(flags[0] < 7, 1.0, 0.0)
-    low = iota((8, W), 0) < 4
+def rim_kernel(pos, z, invd, corners, row_1, row_2, acc_i, rims, part):
+    sub = iota((8, W), 0)
+    ours = at(pos, 0, sub)
+    above, below = (sub >= 4) & (ours > 0), (sub < 4) & (ours < 7)
+    top, bot = from_pairs(pos, 0, row_1[:, :W], row_2[:, :W])
     acc = [acc_i[8 * k : 8 * k + 8, :] for k in range(SUMS)]
-    top, bot = from_pairs(flags[0], row_1[:, :W], row_2[:, :W])
     for end in (0, 1):
         rows = slice(0, 16) if end == 0 else slice(T - 16, T)
         zc, ic = corners[16 * end : 16 * end + 16, :], corners[32 + 16 * end : 48 + 16 * end, :]
         z16 = jnp.concatenate([z[rows, :], zc], axis=1)
         i16 = jnp.concatenate([invd[rows, :], ic], axis=1)
         if end == 0:
-            zb = jnp.concatenate([jnp.where(low, 0.0, pltpu.roll(top, 4, 0)) * up, z16], axis=0)
-            ib = jnp.concatenate([jnp.where(low, 0.0, top) * up, i16], axis=0)
+            zb = jnp.concatenate([jnp.where(above, pltpu.roll(top, 4, 0), 0.0), z16], axis=0)
+            ib = jnp.concatenate([jnp.where(above, top, 0.0), i16], axis=0)
             own = slice(8, 16)
         else:
-            zb = jnp.concatenate([z16, jnp.where(low, bot, 0.0) * down], axis=0)
-            ib = jnp.concatenate([i16, jnp.where(low, pltpu.roll(bot, 4, 0), 0.0) * down], axis=0)
+            zb = jnp.concatenate([z16, jnp.where(below, bot, 0.0)], axis=0)
+            ib = jnp.concatenate([i16, jnp.where(below, pltpu.roll(bot, 4, 0), 0.0)], axis=0)
             own = slice(8, 16)
         w = zb - ib * beside(zb)
         n1 = ib * beside(w)
@@ -332,8 +347,10 @@
     part[...] = sums
 
 
-def gather_kernel(slots, hist, rims, vf, wt, g_o, x_s, slab, sem):
+def gather_kernel(hist, table, rims, wt, g_o, x_s, slab, slots, sem):
     copies = [pltpu.make_async_copy(hist.at[k], x_s.at[k], sem.at[k]) for k in range(4)]
+    ready = pltpu.make_async_copy(table, slots, sem.at[4])
+    ready.start()
     for copy in copies:
         copy.start()
     for k in range(4):
@@ -347,26 +364,19 @@
             for b in range(4):
                 for t in range(LT):
                     start = pl.multiple_of(i * 32 + 8 * b, 8)
-                    to = (i * 32 + 8 * b) * SLAB + 4 * k + t
+                    to = (i * 32 + 8 * b) * SLAB + 4 * t + k
                     slab[pl.ds(to, 8, stride=SLAB), :] = x_s[k, t, pl.ds(start, 8), :]
             return carry
 
         lax.fori_loop(0, T // 32, lay, 0)
-    lane, sub = iota((16, L), 1), iota((16, L), 0)
-
-    def owner(o):
-        acc = jnp.zeros((16, L), F32)
+    lane, sub = iota((8, L), 1), iota((8, L), 0)
+    ready.wait()
+    for o in range(NO):
+        acc = jnp.zeros((8, L), F32)
         for j in range(L):
-            x = slab[pl.ds(slots[o, j], 16), :]
-            x = pltpu.roll(x, slots[NO + o, j], 1)
-            acc = jnp.where(lane == j, x, acc)
-        f = vf[o : o + 1, :]
-        acc = jnp.where((sub & 3) == ((f >> 7) & 3), acc * wt[o : o + 1, :], 0.0)
-        rows = [jnp.sum(acc[4 * k : 4 * k + 4, :], axis=0, keepdims=True) for k in range(4)]
-        g_o[8 * o : 8 * o + 8, :] = jnp.concatenate(rows + [jnp.zeros((4, L), F32)], axis=0)
-
-    for o in range(NO):
-        owner(o)
+            x = slab[pl.ds(slots[o, j], 8), :]
+            acc = jnp.where(lane == j, pltpu.roll(x, slots[NO + o, j], 1), acc)
+        g_o[8 * o : 8 * o + 8, :] = jnp.where(sub < 4, acc * wt[o : o + 1, :], 0.0)
 
 
 def pack_kernel(g, rows, out):
@@ -408,10 +418,12 @@
     return [c[0]] + [c[k + 1] - Q[k] * c[0] for k in range(3)]
 
 
-def combine_kernel(hist, coef, rims, out, h_s, x_s, sem_in, sem_out):
+def combine_kernel(hist, ahead, coef, rims, out, h_s, x_s, sem_in, sem_out):
     n = T // STEPS
     load = [
-        pltpu.make_async_copy(hist.at[:, :, pl.ds(i * n, n), :], h_s.at[i], sem_in.at[i])
+        pltpu.make_async_copy(
+            hist.at[pl.ds(1, 3), :, pl.ds(i * n, n), :], h_s.at[i], sem_in.at[i]
+        )
         for i in range(STEPS)
     ]
     save = [
@@ -424,14 +436,14 @@
     for i in range(STEPS):
         load[i].wait()
         for t in range(LT):
-            h = [h_s[i, k, t] for k in range(4)]
+            h = [ahead[0, t, i * n : (i + 1) * n, :]] + [h_s[i, k, t] for k in range(3)]
             x_s[i * n : (i + 1) * n, lanes(t)] = (c[0] * h[0] + c[1] * h[1]) + (
                 c[2] * h[2] + c[3] * h[3]
             )
         for end, step, low in ((0, 0, 0), (1, STEPS - 1, n - 8)):
             if i == step:
                 for t in range(LT):
-                    x = c[0] * h_s[i, 0, t, low : low + 8, :]
+                    x = c[0] * ahead[0, t, i * n + low : i * n + low + 8, :]
                     for k in range(3):
                         x += c[k + 1] * rims[16 * k + 8 * end : 16 * k + 8 * end + 8, lanes(t)]
                     x_s[i * n + low : i * n + low + 8, lanes(t)] = x
@@ -440,30 +452,34 @@
         copy.wait()
 
 
-def coarse_neighbours(flags, u, row_1, row_2, col_1, col_2):
-    above, below = from_pairs(flags[0], row_1, row_2)
+def coarse_neighbours(pos, u, row_1, row_2, col_1, col_2):
+    above, below = from_pairs(pos, 0, row_1, row_2)
     above, below = above[7:8, :], below[0:1, :]
-    from_l, from_r = from_pairs(flags[1], col_1, col_2)
-    up = jnp.where(flags[0] > 0, 1.0, 0.0)
-    down = jnp.where(flags[0] < 7, 1.0, 0.0)
+    from_l, from_r = from_pairs(pos, 1, col_1, col_2)
+    above = jnp.where(at(pos, 0, above) > 0, above, 0.0)
+    below = jnp.where(at(pos, 0, below) < 7, below, 0.0)
     r, lane = iota((CB, CB), 0), iota((CB, CB), 1)
     g, gl = iota((8, CB), 0), iota((8, CB), 1)
     turned_l = jnp.where(g == 0, 0.0, pltpu.roll(from_l, 1, 0))
     turned_r = jnp.where(g == 7, 0.0, pltpu.roll(from_r, 7, 0))
-    from_l = jnp.where(flags[1] == 0, turned_l, from_l)
-    from_r = jnp.where(flags[1] == NO - 1, turned_r, from_r)
+    place = at(pos, 1, from_l)
+    from_l = jnp.where(place == 0, turned_l, from_l)
+    from_r = jnp.where(place == NO - 1, turned_r, from_r)
     seam_l = tn(from_l, jnp.where(gl == g * GROUP, 1.0, 0.0), HI)
     seam_r = tn(from_r, jnp.where(gl == g * GROUP + GROUP - 1, 1.0, 0.0), HI)
-    near = jnp.where(r == 0, above * up, pltpu.roll(u, 1, 0))
-    near += jnp.where(r == CB - 1, below * down, pltpu.roll(u, CB - 1, 0))
+    near = jnp.where(r == 0, above, pltpu.roll(u, 1, 0))
+    near += jnp.where(r == CB - 1, below, pltpu.roll(u, CB - 1, 0))
     near += jnp.where(lane % GROUP == 0, seam_l, pltpu.roll(u, 1, 1))
     near += jnp.where(lane % GROUP == GROUP - 1, seam_r, pltpu.roll(u, CB - 1, 1))
     return near
 
 
 def base_kernel(
-    flags, held, volt, cleak, col_1, col_2, row_1, row_2, cdiag, scale, base, r_o, c_o
+    hist, pos, held, volt, cleak, col_1, col_2, row_1, row_2,
+    cdiag, scale, base, r_o, c_o, ahead, sem,
 ):
+    copy = pltpu.make_async_copy(hist.at[pl.ds(0, 1)], ahead, sem.at[0])
+    copy.start()
     for o in range(NO):
         h = held[o : o + 1, :]
         r_o[:, lanes(o)] = onehot(h >> 7, CB)
@@ -471,13 +487,14 @@
     count = nt(r_o[...], c_o[...])
     diag = 4.0 * coarse_conductance + cleak[...] + via_conductance * count
     u = volt[...]
-    near = coarse_neighbours(flags, u, row_1[:, W:], row_2[:, W:], col_1[:, T:], col_2[:, T:])
+    near = coarse_neighbours(pos, u, row_1[:, W:], row_2[:, W:], col_1[:, T:], col_2[:, T:])
     cdiag[...] = diag
     scale[...] = relaxation / diag
     base[...] = u - relaxation * (diag * u - coarse_conductance * near) / diag
-
-
-def sweep1_kernel(flags, arrived, scale, base, r, c, coef, u_o, src_o, c1, c2, r1, r2, v_s):
+    copy.wait()
+
+
+def sweep1_kernel(pos, arrived, scale, base, r, c, coef, u_o, src_o, c1, c2, r1, r2, v_s):
     tot = arrived[4:5, :]
     for o in range(1, NO):
         tot += arrived[8 * o + 4 : 8 * o + 5, :]
@@ -500,17 +517,16 @@
     g, gl = iota((8, CB), 0), iota((8, CB), 1)
     to_l = nt(jnp.where(gl == g * GROUP, 1.0, 0.0), u, HI)
     to_r = nt(jnp.where(gl == g * GROUP + GROUP - 1, 1.0, 0.0), u, HI)
-    c1[...], c2[...] = pair_order(flags[1], to_l, to_r)
-    r1[...], r2[...] = pair_order(flags[0], u[0:8, :], u[CB - 8 :, :])
-
-
-def sweep2_kernel(flags, u, src, cdiag, scale, col_1, col_2, row_1, row_2, u_o):
-    near = coarse_neighbours(flags, u[...], row_1[...], row_2[...], col_1[...], col_2[...])
+    c1[...], c2[...] = pair_order(pos, 1, to_l, to_r)
+    r1[...], r2[...] = pair_order(pos, 0, u[0:8, :], u[CB - 8 :, :])
+
+
+def sweep2_kernel(pos, u, src, cdiag, scale, col_1, col_2, row_1, row_2, u_o):
+    near = coarse_neighbours(pos, u[...], row_1[...], row_2[...], col_1[...], col_2[...])
     u_o[...] = u[...] + scale[...] * (src[...] - (cdiag[...] * u[...] - coarse_conductance * near))
 
 
 VM = pl.BlockSpec(memory_space=pltpu.VMEM)
-SM = pl.BlockSpec(memory_space=pltpu.SMEM)
 ANY = pl.BlockSpec(memory_space=pltpu.HBM)
 vmem = pltpu.MemorySpace.VMEM
 hbm = jax.ShapeDtypeStruct
@@ -524,8 +540,8 @@
     return [pltpu.with_memory_space_constraint(x, pltpu.HBM) for x in args]
 
 
-def call(body, outs, args, scratch=(), flags=None, flops=0, any_in=0, any_out=0):
-    specs = ([] if flags is None else [SM]) + [ANY] * any_in + [VM] * (len(args) - any_in)
+def call(body, outs, args, scratch=(), flops=0, any_in=0, any_out=0):
+    specs = [ANY] * any_in + [VM] * (len(args) - any_in)
     return pl.pallas_call(
         body,
         out_shape=outs,
@@ -534,7 +550,7 @@
         scratch_shapes=list(scratch),
         cost_estimate=pl.CostEstimate(flops=flops, bytes_accessed=0, transcendentals=0),
         compiler_params=pltpu.CompilerParams(vmem_limit_bytes=20 * 2**20),
-    )(*([] if flags is None else [flags]), *args)
+    )(*args)
 
 
 def exchange(axis, first, second):
@@ -549,8 +565,8 @@
 
 
 def per_device(load_amp, load_mask, leak, coarse_leak, coarse_init, via_fine, via_coarse, via_count):
-    flags = jnp.where(
-        jnp.arange(2, dtype=jnp.int32) == 0, lax.axis_index(ROW), lax.axis_index(COL)
+    pos = jnp.where(
+        lax.broadcasted_iota(jnp.int32, (8, W + CB), 0) == 0, lax.axis_index(ROW), lax.axis_index(COL)
     ).astype(jnp.int32)
     live = jnp.arange(L, dtype=jnp.int32)[None, :] < via_count.reshape(NO, 1)
     wt = jnp.where(live, via_conductance, 0.0).astype(F32)
@@ -567,16 +583,20 @@
     dmas = pltpu.SemaphoreType.DMA((4,))
     big = 20_000_000_000
 
-    zl, invd, strips, irims, where = call(
-        diag_kernel, [tile, tile, rim16, rim16, hbm((2 * NO, L), jnp.int32)],
-        keep(fine, wt) + leave(load_amp, load_mask, leak), [hot, hot], flops=big,
-    )
-    drops = call(parts_kernel, [vmem((3 * CB, CB), BF16)], leave(coarse_init))[0]
+    drops, where, volt, fine = call(
+        parts_kernel,
+        [vmem((3 * CB, CB), BF16), hbm((2 * NO, L), jnp.int32), block, vmem((NO, L), jnp.int32)],
+        leave(coarse_init, fine),
+    )
+    zl, invd, strips, irims = call(
+        diag_kernel, [tile, tile, rim16, rim16],
+        leave(load_amp, load_mask, leak) + keep(fine, wt),
+        [hot, hot, tile, vmem((T, T), jnp.int32), tile, dmas], flops=big, any_in=3,
+    )
     looked = call(lookup_kernel, [slots], keep(held, drops))[0]
     at_via = spread(looked)
     a, send_1, send_2 = call(
-        strips_kernel, [hot, side, side], keep(fine, wt, at_via, strips, coarse_init), flags=flags
-    )
+        strips_kernel, [hot, side, side], keep(pos, fine, wt, at_via, strips, volt)    )
     col_1, col_2 = exchange(COL, send_1, send_2)
     z, zrims = call(
         rhs_kernel, [tile, rim16], keep(fine, wt, at_via, zl, invd, a), [hots], flops=big
@@ -584,41 +604,40 @@
     rim = vmem((8, W + CB), F32)
     send_1, send_2, corners = call(
         edge_kernel, [rim, rim, vmem((64, L), F32)],
-        keep(zrims, irims, col_1, col_2, coarse_init), flags=flags,
-    )
+        keep(pos, zrims, irims, col_1, col_2, volt)    )
     row_1, row_2 = exchange(ROW, send_1, send_2)
     hist, acc = call(
-        basis_kernel, [pltpu.MemorySpace.HBM((4, LT, T, L), F32), vmem((8 * SUMS, L), F32)], keep(z, invd, col_1, col_2),
-        [ext] * 5 + [dmas], flags=flags, flops=big, any_out=1,
+        basis_kernel, [pltpu.MemorySpace.HBM((4, LT, T, L), F32), vmem((8 * SUMS, L), F32)], keep(pos, z, invd, col_1, col_2),
+        [ext] * 5 + [dmas], flops=big, any_out=1,
     )
     rims, part = call(
         rim_kernel, [vmem((48, T), F32), vmem((8, L), F32)],
-        keep(z, invd, corners, row_1, row_2, acc), flags=flags,
-    )
+        keep(pos, z, invd, corners, row_1, row_2, acc)    )
     rows = spread(part, ROW)
     g = call(
-        gather_kernel, [vmem(*packed)], leave(hist) + keep(rims, fine, wt),
-        [vmem((4, LT, T, L), F32), vmem((T * SLAB, L), F32), dmas], flags=where, flops=big, any_in=1,
+        gather_kernel, [vmem(*packed)], leave(hist, where) + keep(rims, wt),
+        [vmem((4, LT, T, L), F32), vmem((T * SLAB + 8, L), F32),
+         pltpu.MemorySpace.SMEM((2 * NO, L), jnp.int32), pltpu.SemaphoreType.DMA((5,))],
+        flops=big, any_in=2,
     )[0]
     arrived = spread(call(pack_kernel, [vmem(*packed)], keep(g, rows))[0])
-    cdiag, scale, base, r_hot, c_hot = call(
-        base_kernel, [block, block, block, chot, chot],
-        keep(held, coarse_init, coarse_leak, col_1, col_2, row_1, row_2), flags=flags, flops=big,
+    cdiag, scale, base, r_hot, c_hot, ahead = call(
+        base_kernel, [block, block, block, chot, chot, vmem((1, LT, T, L), F32)],
+        leave(hist) + keep(pos, held, volt, coarse_leak, col_1, col_2, row_1, row_2),
+        [dmas], flops=big, any_in=1,
     )
     coef, u, src, c1, c2, r1, r2 = call(
         sweep1_kernel, [seam, block, block, seam, seam, seam, seam],
-        keep(arrived, scale, base, r_hot, c_hot), [vmem((CB, 2 * NO * L), BF16)], flags=flags,
-    )
+        keep(pos, arrived, scale, base, r_hot, c_hot), [vmem((CB, 2 * NO * L), BF16)]    )
     c1, c2 = exchange(COL, c1, c2)
     r1, r2 = exchange(ROW, r1, r2)
     fine_drop = call(
-        combine_kernel, [pltpu.MemorySpace.HBM((T, T), F32)], leave(hist) + keep(coef, rims),
-        [vmem((STEPS, 4, LT, T // STEPS, L), F32), tile, pltpu.SemaphoreType.DMA((STEPS,)),
+        combine_kernel, [pltpu.MemorySpace.HBM((T, T), F32)], leave(hist) + keep(ahead, coef, rims),
+        [vmem((STEPS, 3, LT, T // STEPS, L), F32), tile, pltpu.SemaphoreType.DMA((STEPS,)),
          pltpu.SemaphoreType.DMA((STEPS,))], flops=big // 4, any_in=1, any_out=1,
     )[0]
     coarse_drop = call(
-        sweep2_kernel, [hbm((CB, CB), F32)], keep(u, src, cdiag, scale, c1, c2, r1, r2), flags=flags
-    )[0]
+        sweep2_kernel, [hbm((CB, CB), F32)], keep(pos, u, src, cdiag, scale, c1, c2, r1, r2)    )[0]
     return fine_drop, coarse_drop
 
 

time: 88.9 us -> 82 us (0.922)
  Pallas kernels: 34.8 us -> 28.5 us
    pallas_call x14, Pallas kernels: 34.8 us -> 28.5 us  [call(): pl.pallas_call(body, out_shape=outs, in_specs=specs, out_specs=[ANY] * an...]
  transfers between devices with their start and end apart: 12 -> 12, of which waited for: 3 -> 3; matrix products, arithmetic and copies ran while one was open for 1% -> 1% of each run, Pallas kernels for 29% -> 27%
where the time goes in v6:
time: 82 us; the launch traced here: 81.2 us
  starting transfers between devices  36.4 us (44%)
  Pallas kernels  28.5 us (35%)
  waiting for transfers between devices  12.7 us (15%)
  other arithmetic  2.12 us (3%)
  between operations  0.83 us (1%)
    pallas_call x14, Pallas kernels, call(): pl.pallas_call(body, out_shape=outs, in_specs=specs, out_specs=[ANY] * an...  28.5 us
    all_to_all x4, starting transfers between devices, spread(): return lax.all_to_all(x, axis, split_axis=0, concat_axis=0, tiled=True)  23.5 us
    ppermute x8, starting transfers between devices, exchange(): return (lax.ppermute(first, axis, near), lax.ppermute(second, axis, far))  12.9 us
    all_to_all x4, waiting for transfers between devices, spread(): return lax.all_to_all(x, axis, split_axis=0, concat_axis=0, tiled=True)  11 us
  transfers between devices with their start and end apart: 12, of which 3 were waited for; matrix products, arithmetic and copies ran while one was open for 1% of the time, Pallas kernels for 27%

profile of v6, /device:TPU:1, one launch (start us, length us, event | category | flops | bytes accessed | tf_op | source)
XLA Modules:
  0.0 81.2 jit_solution(4071466901858763912)
XLA Ops:
  0.6 1.4 %compare_select_fusion = s32[16,1,128]{2,1,0:T(1,128)} fusion(s32[1,2048]{1,0:T(1,128)} %param.14, s32[16]{0:T(128)} %bitcast.22), kind=kLoop, calls=%fused_computation | loop fusion | flops 12288 | bytes 16448 | tf_op jit(solution)/shard_map/jit(_where)/select_n | solution.py:575
  2.0 7.6 %all-to-all-start = ((s32[16,1,128]{2,1,0:T(1,128)}), s32[16,1,128]{2,1,0:T(1,128)S(1)}, u32[]{:S(2)}, u32[]{:S(2)}) async-start(s32[16,1,128]{2,1,0:T(1,128)} %compare_select_fusion), calls=%async_computation | async-start | bytes 16384 | tf_op jit(solution)/shard_map/all_to_all | solution.py:564
  11.9 4.6 %shard_map.97 = (f32[512,512]{1,0:T(8,128)S(1)}, f32[512,512]{1,0:T(8,128)S(1)}, f32[16,512]{1,0:T(8,128)S(1)}, f32[16,512]{1,0:T(8,128)S(1)}) custom-call(f32[512,512]{1,0:T(8,128)} %amp.1, s32[512,512]{1,0:T(8,128)} %mask.1, f32[512,512]{1,0:T(8,128)} %leak.1, s32[16,128]{1,0:T(8,128)S(1)} %get-tuple-element.35.vf, f32[16,128]{1,0:T(8,128)S(1)} %fusion.wt), custom_call_target="tpu_custom_call" | custom-call | flops 20000000000 | tf_op jit(solution)/shard_map/pallas_call | solution.py:545
  16.5 1.2 %shard_map.96 = f32[16,128]{1,0:T(8,128)} custom-call(s32[16,128]{1,0:T(8,128)S(1)} %bitcast.16, bf16[384,128]{1,0:T(8,128)(2,1)S(1)} %get-tuple-element.36.parts), custom_call_target="tpu_custom_call" | custom-call | tf_op jit(solution)/shard_map/pallas_call | solution.py:545
  17.7 6.7 %all-to-all-start.1 = ((f32[16,1,128]{2,1,0:T(1,128)}), f32[16,1,128]{2,1,0:T(1,128)S(1)}, u32[]{:S(2)}, u32[]{:S(2)}) async-start(f32[16,1,128]{2,1,0:T(1,128)} %bitcast.5), calls=%async_computation.1 | async-start | bytes 16384 | tf_op jit(solution)/shard_map/all_to_all | solution.py:564
  24.4 6.3 %all-to-all-done.1 = f32[16,1,128]{2,1,0:T(1,128)S(1)} async-done(((f32[16,1,128]{2,1,0:T(1,128)}), f32[16,1,128]{2,1,0:T(1,128)S(1)}, u32[]{:S(2)}, u32[]{:S(2)}) %all-to-all-start.1) | async-done | bytes 8224 | tf_op jit(solution)/shard_map/all_to_all | solution.py:564
  30.8 1.2 %shard_map.98 = (bf16[512,2048]{1,0:T(8,128)(2,1)S(1)}, f32[8,640]{1,0:T(8,128)S(1)}, f32[8,640]{1,0:T(8,128)S(1)}) custom-call(s32[8,768]{1,0:T(8,128)S(1)} %iota.14.pos, s32[16,128]{1,0:T(8,128)S(1)} %get-tuple-element.35.vf, f32[16,128]{1,0:T(8,128)S(1)} %fusion.wt, f32[16,128]{1,0:T(8,128)S(1)} %bitcast.18, f32[16,512]{1,0:T(8,128)S(1)} %get-tuple-element.39.strips, ...), custom_call_target="tpu_custom_call" | custom-call | tf_op jit(solution)/shard_map/pallas_call | solution.py:545
  32.3 1.5 %collective-permute-start.1 = (f32[8,640]{1,0:T(8,128)S(1)}, f32[8,640]{1,0:T(8,128)S(1)}, u32[]{:S(2)}, u32[]{:S(2)}) collective-permute-start(f32[8,640]{1,0:T(8,128)S(1)} %get-tuple-element.44), channel_id=1, source_target_pairs={{0,15},{1,2},{2,1},{3,4},{4,3},{5,6},{6,5},{7,8},{8,7},{9,10},{10,... | collective-permute-start | bytes 61448 | tf_op jit(solution)/shard_map/ppermute | solution.py:560
  33.8 2.8 %shard_map.99 = (f32[512,512]{1,0:T(8,128)S(1)}, f32[16,512]{1,0:T(8,128)S(1)}) custom-call(s32[16,128]{1,0:T(8,128)S(1)} %get-tuple-element.35.vf, f32[16,128]{1,0:T(8,128)S(1)} %fusion.wt, f32[16,128]{1,0:T(8,128)S(1)} %bitcast.19, f32[512,512]{1,0:T(8,128)S(1)} %get-tuple-element.37.zl, f32[512,512]{1,0:T(8,128)S(1)} %get-tuple-element.38.invd, ...), custom_call_target="tpu_custom_call" | custom-call | flops 20000000000 | tf_op jit(solution)/shard_map/pallas_call | solution.py:545
  36.6 1.6 %collective-permute-done.1.col_2 = f32[8,640]{1,0:T(8,128)S(1)} collective-permute-done((f32[8,640]{1,0:T(8,128)S(1)}, f32[8,640]{1,0:T(8,128)S(1)}, u32[]{:S(2)}, u32[]{:S(2)}) %collective-permute-start.1) | collective-permute-done | bytes 20512 | tf_op jit(solution)/shard_map/ppermute | solution.py:560
  38.5 4.2 %collective-permute-start.2 = (f32[8,768]{1,0:T(8,128)S(1)}, f32[8,768]{1,0:T(8,128)S(1)}, u32[]{:S(2)}, u32[]{:S(2)}) collective-permute-start(f32[8,768]{1,0:T(8,128)S(1)} %get-tuple-element.48), channel_id=1, source_target_pairs={{0,16},{16,0},{32,48},{48,32},{64,80},{80,64},{96,112},{112,96},{1... | collective-permute-start | bytes 73736 | tf_op jit(solution)/shard_map/ppermute | solution.py:560
  42.7 1.6 %collective-permute-start.3 = (f32[8,768]{1,0:T(8,128)S(1)}, f32[8,768]{1,0:T(8,128)S(1)}, u32[]{:S(2)}, u32[]{:S(2)}) collective-permute-start(f32[8,768]{1,0:T(8,128)S(1)} %get-tuple-element.49), channel_id=1, source_target_pairs={{0,112},{16,32},{32,16},{48,64},{64,48},{80,96},{96,80},{112,0},{1... | collective-permute-start | bytes 73736 | tf_op jit(solution)/shard_map/ppermute | solution.py:560
  44.3 4.4 %shard_map.100 = (f32[4,4,512,128]{3,2,1,0:T(8,128)}, f32[64,128]{1,0:T(8,128)S(1)}) custom-call(s32[8,768]{1,0:T(8,128)S(1)} %iota.14.pos, f32[512,512]{1,0:T(8,128)S(1)} %get-tuple-element.42.z, f32[512,512]{1,0:T(8,128)S(1)} %get-tuple-element.38.invd, f32[8,640]{1,0:T(8,128)S(1)} %collective-permute-done.col_1, f32[8,640]{1,0:T(8,128)S(1)} %collective-permute-done.1.col_2), custom_call_target="tpu_custom_call" | custom-call | flops 20000000000 | tf_op jit(solution)/shard_map/pallas_call | solution.py:545
  48.7 1.1 %shard_map.103 = (f32[48,512]{1,0:T(8,128)S(1)}, f32[8,128]{1,0:T(8,128)}) custom-call(s32[8,768]{1,0:T(8,128)S(1)} %iota.14.pos, f32[512,512]{1,0:T(8,128)S(1)} %get-tuple-element.42.z, f32[512,512]{1,0:T(8,128)S(1)} %get-tuple-element.38.invd, f32[64,128]{1,0:T(8,128)S(1)} %get-tuple-element.52.corners, f32[8,768]{1,0:T(8,128)S(1)} %collective-permute-done.2.row_1, ...), custom_call_target="tpu_custom_call" | custom-call | tf_op jit(solution)/shard_map/pallas_call | solution.py:545
  49.8 5.8 %all-to-all-start.2 = ((f32[8,1,128]{2,1,0:T(1,128)}), f32[8,1,128]{2,1,0:T(1,128)S(1)}, u32[]{:S(2)}, u32[]{:S(2)}) async-start(f32[8,1,128]{2,1,0:T(1,128)} %bitcast.8), calls=%async_computation.2 | async-start | bytes 8192 | tf_op jit(solution)/shard_map/all_to_all | solution.py:564
  55.6 4.6 %shard_map.104.g = f32[128,128]{1,0:T(8,128)S(1)} custom-call(f32[4,4,512,128]{3,2,1,0:T(8,128)} %get-tuple-element.45.hist, s32[32,128]{1,0:T(8,128)} %copy-done.1, f32[48,512]{1,0:T(8,128)S(1)} %get-tuple-element.54.rims, f32[16,128]{1,0:T(8,128)S(1)} %fusion.wt), custom_call_target="tpu_custom_call" | custom-call | flops 20000000000 | tf_op jit(solution)/shard_map/pallas_call | solution.py:545
  60.9 3.5 %all-to-all-start.3 = ((f32[16,8,128]{2,1,0:T(8,128)}), f32[16,8,128]{2,1,0:T(8,128)S(1)}, u32[]{:S(2)}, u32[]{:S(2)}) async-start(f32[16,8,128]{2,1,0:T(8,128)} %bitcast.10), calls=%async_computation.3 | async-start | bytes 131072 | tf_op jit(solution)/shard_map/all_to_all | solution.py:564
  64.4 1.7 %shard_map.102 = (f32[128,128]{1,0:T(8,128)S(1)}, f32[128,128]{1,0:T(8,128)S(1)}, f32[128,128]{1,0:T(8,128)S(1)}, bf16[128,2048]{1,0:T(8,128)(2,1)S(1)}, bf16[12...) custom-call(f32[4,4,512,128]{3,2,1,0:T(8,128)} %get-tuple-element.45.hist, s32[8,768]{1,0:T(8,128)S(1)} %iota.14.pos, ...), custom_call_target="tpu_custom_call" | custom-call | flops 20000000000 | tf_op jit(solution)/shard_map/pallas_call | solution.py:545
  66.2 4.7 %all-to-all-done.3 = f32[16,8,128]{2,1,0:T(8,128)S(1)} async-done(((f32[16,8,128]{2,1,0:T(8,128)}), f32[16,8,128]{2,1,0:T(8,128)S(1)}, u32[]{:S(2)}, u32[]{:S(2)}) %all-to-all-start.3) | async-done | bytes 65568 | tf_op jit(solution)/shard_map/all_to_all | solution.py:564
  70.9 1.3 %shard_map.106 = (f32[8,128]{1,0:T(8,128)S(1)}, f32[128,128]{1,0:T(8,128)S(1)}, f32[128,128]{1,0:T(8,128)S(1)}, f32[8,128]{1,0:T(8,128)S(1)}, f32[8,128]{1,0:T(8...) custom-call(s32[8,768]{1,0:T(8,128)S(1)} %iota.14.pos, f32[128,128]{1,0:T(8,128)S(1)} %bitcast.15, ...), custom_call_target="tpu_custom_call" | custom-call | tf_op jit(solution)/shard_map/pallas_call | solution.py:545
  72.5 1.9 %collective-permute-start.5 = (f32[8,128]{1,0:T(8,128)S(1)}, f32[8,128]{1,0:T(8,128)S(1)}, u32[]{:S(2)}, u32[]{:S(2)}) collective-permute-start(f32[8,128]{1,0:T(8,128)S(1)} %get-tuple-element.65), channel_id=1, source_target_pairs={{0,15},{1,2},{2,1},{3,4},{4,3},{5,6},{6,5},{7,8},{8,7},{9,10},{10,... | collective-permute-start | bytes 12296 | tf_op jit(solution)/shard_map/ppermute | solution.py:560
  74.4 2.0 %collective-permute-start.6 = (f32[8,128]{1,0:T(8,128)S(1)}, f32[8,128]{1,0:T(8,128)S(1)}, u32[]{:S(2)}, u32[]{:S(2)}) collective-permute-start(f32[8,128]{1,0:T(8,128)S(1)} %get-tuple-element.66), channel_id=1, source_target_pairs={{0,16},{16,0},{32,48},{48,32},{64,80},{80,64},{96,112},{112,96},{1... | collective-permute-start | bytes 12296 | tf_op jit(solution)/shard_map/ppermute | solution.py:560
  76.4 1.1 %collective-permute-start.7 = (f32[8,128]{1,0:T(8,128)S(1)}, f32[8,128]{1,0:T(8,128)S(1)}, u32[]{:S(2)}, u32[]{:S(2)}) collective-permute-start(f32[8,128]{1,0:T(8,128)S(1)} %get-tuple-element.67), channel_id=1, source_target_pairs={{0,112},{16,32},{32,16},{48,64},{64,48},{80,96},{96,80},{112,0},{1... | collective-permute-start | bytes 12296 | tf_op jit(solution)/shard_map/ppermute | solution.py:560
  77.5 2.7 %shard_map.107 = f32[512,512]{1,0:T(8,128)} custom-call(f32[4,4,512,128]{3,2,1,0:T(8,128)} %get-tuple-element.45.hist, f32[1,4,512,128]{3,2,1,0:T(8,128)S(1)} %get-tuple-element.50.ahead, f32[8,128]{1,0:T(8,128)S(1)} %get-tuple-element.60.coef, f32[48,512]{1,0:T(8,128)S(1)} %get-tuple-element.54.rims), custom_call_target="tpu_custom_call" | custom-call | flops 5000000000 | tf_op jit(solution)/shard_map/pallas_call | solution.py:545
  (22 shorter events, 4.8 us)
Async XLA Ops:
  2.0 14.5 %all-to-all-start = ((s32[16,1,128]{2,1,0:T(1,128)}), s32[16,1,128]{2,1,0:T(1,128)S(1)}, u32[]{:S(2)}, u32[]{:S(2)}) async-start(s32[16,1,128]{2,1,0:T(1,128)} %compare_select_fusion), calls=%async_computation | async-start | bytes 16384 | tf_op jit(solution)/shard_map/all_to_all | solution.py:564
  11.3 0.6 copy-start.1
  17.7 13.0 %all-to-all-start.1 = ((f32[16,1,128]{2,1,0:T(1,128)}), f32[16,1,128]{2,1,0:T(1,128)S(1)}, u32[]{:S(2)}, u32[]{:S(2)}) async-start(f32[16,1,128]{2,1,0:T(1,128)} %bitcast.5), calls=%async_computation.1 | async-start | bytes 16384 | tf_op jit(solution)/shard_map/all_to_all | solution.py:564
  32.0 4.6 %collective-permute-start = (f32[8,640]{1,0:T(8,128)S(1)}, f32[8,640]{1,0:T(8,128)S(1)}, u32[]{:S(2)}, u32[]{:S(2)}) collective-permute-start(f32[8,640]{1,0:T(8,128)S(1)} %get-tuple-element.43), channel_id=1, source_target_pairs={{0,1},{1,0},{2,3},{3,2},{4,5},{5,4},{6,7},{7,6},{8,9},{9,8},{10,11... | collective-permute-start | bytes 61448 | tf_op jit(solution)/shard_map/ppermute | solution.py:560
  32.3 6.0 %collective-permute-start.1 = (f32[8,640]{1,0:T(8,128)S(1)}, f32[8,640]{1,0:T(8,128)S(1)}, u32[]{:S(2)}, u32[]{:S(2)}) collective-permute-start(f32[8,640]{1,0:T(8,128)S(1)} %get-tuple-element.44), channel_id=1, source_target_pairs={{0,15},{1,2},{2,1},{3,4},{4,3},{5,6},{6,5},{7,8},{8,7},{9,10},{10,... | collective-permute-start | bytes 61448 | tf_op jit(solution)/shard_map/ppermute | solution.py:560
  38.5 10.2 %collective-permute-start.2 = (f32[8,768]{1,0:T(8,128)S(1)}, f32[8,768]{1,0:T(8,128)S(1)}, u32[]{:S(2)}, u32[]{:S(2)}) collective-permute-start(f32[8,768]{1,0:T(8,128)S(1)} %get-tuple-element.48), channel_id=1, source_target_pairs={{0,16},{16,0},{32,48},{48,32},{64,80},{80,64},{96,112},{112,96},{1... | collective-permute-start | bytes 73736 | tf_op jit(solution)/shard_map/ppermute | solution.py:560
  42.7 6.0 %collective-permute-start.3 = (f32[8,768]{1,0:T(8,128)S(1)}, f32[8,768]{1,0:T(8,128)S(1)}, u32[]{:S(2)}, u32[]{:S(2)}) collective-permute-start(f32[8,768]{1,0:T(8,128)S(1)} %get-tuple-element.49), channel_id=1, source_target_pairs={{0,112},{16,32},{32,16},{48,64},{64,48},{80,96},{96,80},{112,0},{1... | collective-permute-start | bytes 73736 | tf_op jit(solution)/shard_map/ppermute | solution.py:560
  49.8 10.4 %all-to-all-start.2 = ((f32[8,1,128]{2,1,0:T(1,128)}), f32[8,1,128]{2,1,0:T(1,128)S(1)}, u32[]{:S(2)}, u32[]{:S(2)}) async-start(f32[8,1,128]{2,1,0:T(1,128)} %bitcast.8), calls=%async_computation.2 | async-start | bytes 8192 | tf_op jit(solution)/shard_map/all_to_all | solution.py:564
  55.6 8.8 %copy-start = (f32[128,128]{1,0:T(8,128)S(1)}, f32[128,128]{1,0:T(8,128)}, u32[]{:S(2)}) copy-start(f32[128,128]{1,0:T(8,128)} %cleak.1) | copy-start | bytes 196612
  60.9 10.0 %all-to-all-start.3 = ((f32[16,8,128]{2,1,0:T(8,128)}), f32[16,8,128]{2,1,0:T(8,128)S(1)}, u32[]{:S(2)}, u32[]{:S(2)}) async-start(f32[16,8,128]{2,1,0:T(8,128)} %bitcast.10), calls=%async_computation.3 | async-start | bytes 131072 | tf_op jit(solution)/shard_map/all_to_all | solution.py:564
  72.2 8.0 %collective-permute-start.4 = (f32[8,128]{1,0:T(8,128)S(1)}, f32[8,128]{1,0:T(8,128)S(1)}, u32[]{:S(2)}, u32[]{:S(2)}) collective-permute-start(f32[8,128]{1,0:T(8,128)S(1)} %get-tuple-element.64), channel_id=1, source_target_pairs={{0,1},{1,0},{2,3},{3,2},{4,5},{5,4},{6,7},{7,6},{8,9},{9,8},{10,11... | collective-permute-start | bytes 12296 | tf_op jit(solution)/shard_map/ppermute | solution.py:560
  72.5 7.6 %collective-permute-start.5 = (f32[8,128]{1,0:T(8,128)S(1)}, f32[8,128]{1,0:T(8,128)S(1)}, u32[]{:S(2)}, u32[]{:S(2)}) collective-permute-start(f32[8,128]{1,0:T(8,128)S(1)} %get-tuple-element.65), channel_id=1, source_target_pairs={{0,15},{1,2},{2,1},{3,4},{4,3},{5,6},{6,5},{7,8},{8,7},{9,10},{10,... | collective-permute-start | bytes 12296 | tf_op jit(solution)/shard_map/ppermute | solution.py:560
  74.4 5.8 %collective-permute-start.6 = (f32[8,128]{1,0:T(8,128)S(1)}, f32[8,128]{1,0:T(8,128)S(1)}, u32[]{:S(2)}, u32[]{:S(2)}) collective-permute-start(f32[8,128]{1,0:T(8,128)S(1)} %get-tuple-element.66), channel_id=1, source_target_pairs={{0,16},{16,0},{32,48},{48,32},{64,80},{80,64},{96,112},{112,96},{1... | collective-permute-start | bytes 12296 | tf_op jit(solution)/shard_map/ppermute | solution.py:560
  76.4 3.8 %collective-permute-start.7 = (f32[8,128]{1,0:T(8,128)S(1)}, f32[8,128]{1,0:T(8,128)S(1)}, u32[]{:S(2)}, u32[]{:S(2)}) collective-permute-start(f32[8,128]{1,0:T(8,128)S(1)} %get-tuple-element.67), channel_id=1, source_target_pairs={{0,112},{16,32},{32,16},{48,64},{64,48},{80,96},{96,80},{112,0},{1... | collective-permute-start | bytes 12296 | tf_op jit(solution)/shard_map/ppermute | solution.py:560

commit v7 on v6

--- a/solution.py
+++ b/solution.py
@@ -75,42 +75,56 @@
     return jnp.where(even, second, first), jnp.where(even, first, second)
 
 
-def diag_kernel(amp, mask, leak, vf, wt, zl, invd, strips, rims, a_s, b_s, amp_s, mask_s, leak_s, sem):
+def diag_kernel(
+    amp, mask, leak, via, zl, invd, strips, rims, amp_s, mask_s, leak_s, via_s, sem
+):
     copies = [
         pltpu.make_async_copy(x, y, sem.at[k])
-        for k, (x, y) in enumerate(((leak, leak_s), (amp, amp_s), (mask, mask_s)))
+        for k, (x, y) in enumerate(
+            ((leak, leak_s), (via, via_s), (amp, amp_s), (mask, mask_s))
+        )
     ]
     for copy in copies:
         copy.start()
+    for copy in copies:
+        copy.wait()
+    inv = 1.0 / (4.0 + leak_s[...] + via_s[...])
+    z = amp_s[...] * mask_s[...].astype(F32) * inv
+    zl[...] = z
+    invd[...] = inv
+    j, lane = iota((8, 2 * L), 0), iota((8, 2 * L), 1)
+    pick = jnp.where(lane == jnp.where(j < 4, j, 2 * L - 8 + j), 1.0, 0.0).astype(BF16)
+    for k, x in enumerate((z, inv)):
+        hi, rest = hi_lo(jnp.concatenate([x[:, :L], x[:, T - L :]], axis=1))
+        mid, lo = hi_lo(rest)
+        strips[8 * k : 8 * k + 8, :] = (
+            nt(pick, lo.astype(BF16)) + nt(pick, mid.astype(BF16)) + nt(pick, hi.astype(BF16))
+        )
+    rims[0:8, :] = inv[0:8]
+    rims[8:16, :] = inv[T - 8 :]
+
+
+def parts_kernel(volt, vf, wt, pos, parts, slots, volt_o, vf_o, seams, round_o, via, a_s, b_s):
+    u = volt[...]
+    f = vf[...]
+    volt_o[...] = u
+    vf_o[...] = f
+    slots[0:NO, :] = (f >> 9) * SLAB + ((f >> 7) & 3) * 4
+    slots[NO:, :] = (iota((NO, L), 1) - f) & (L - 1)
+    v1, rest = hi_lo(u.T)
+    v2, v3 = hi_lo(rest)
+    parts[...] = jnp.concatenate([v3, v2, v1], axis=0).astype(BF16)
+    g, lane = iota((8, CB), 0), iota((8, CB), 1)
+    to_l = nt(jnp.where(lane == g * GROUP, 1.0, 0.0), u, HI)
+    to_r = nt(jnp.where(lane == g * GROUP + GROUP - 1, 1.0, 0.0), u, HI)
+    seams[0:8, :] = to_l
+    seams[8:16, :] = to_r
+    round_o[...] = jnp.where(at(pos, 1, to_l) == 0, to_l, to_r)
     for o in range(NO):
         f = vf[o : o + 1, :]
         a_s[:, lanes(o)] = onehot(f // T, T)
         b_s[:, lanes(o)] = jnp.where(iota((T, L), 0) == f % T, wt[o : o + 1, :], 0.0).astype(BF16)
-    via = nt(a_s[...], b_s[...])
-    for copy in copies:
-        copy.wait()
-    inv = 1.0 / (4.0 + leak_s[...] + via)
-    z = amp_s[...] * mask_s[...].astype(F32) * inv
-    zl[...] = z
-    invd[...] = inv
-    j, lane = iota((8, L), 0), iota((8, L), 1)
-    first = jnp.where((j < 4) & (lane == j), 1.0, 0.0)
-    last = jnp.where((j >= 4) & (lane == 120 + j), 1.0, 0.0)
-    strips[0:8, :] = nt(first, z[:, :L], HI) + nt(last, z[:, T - L :], HI)
-    strips[8:16, :] = nt(first, inv[:, :L], HI) + nt(last, inv[:, T - L :], HI)
-    rims[0:8, :] = inv[0:8]
-    rims[8:16, :] = inv[T - 8 :]
-
-
-def parts_kernel(volt, vf, parts, slots, volt_o, vf_o):
-    volt_o[...] = volt[...]
-    vf_o[...] = vf[...]
-    f = vf[...]
-    slots[0:NO, :] = (f >> 9) * SLAB + ((f >> 7) & 3) * 4
-    slots[NO:, :] = (iota((NO, L), 1) - f) & (L - 1)
-    v1, rest = hi_lo(volt[...].T)
-    v2, v3 = hi_lo(rest)
-    parts[...] = jnp.concatenate([v3, v2, v1], axis=0).astype(BF16)
+    via[...] = nt(a_s[...], b_s[...])
 
 
 def lookup_kernel(held, parts, looked):
@@ -125,7 +139,7 @@
         looked[2 * i + 1 : 2 * i + 2, :] = y[:, L:]
 
 
-def strips_kernel(pos, vf, wt, at_via, strips, volt, a_o, send_1, send_2):
+def strips_kernel(pos, vf, wt, at_via, strips, seams, a_o, send_1, send_2):
     j = iota((8, L), 0)
     colid = jnp.where(j < 4, j, T - 8 + j)
     hs, ls = [], []
@@ -143,13 +157,10 @@
     inv = strips[8:16, :]
     z = strips[0:8, :] + (inj[0:8] + inj[8:16]) * inv
     low = iota((8, T), 0) < 4
-    g, lane = iota((8, CB), 0), iota((8, CB), 1)
     to_l = jnp.where(low, z, pltpu.roll(inv, 4, 0))
     to_r = jnp.where(low, pltpu.roll(z, 4, 0), inv)
     send_1[:, :T], send_2[:, :T] = pair_order(pos, 1, to_l, to_r)
-    to_l = nt(jnp.where(lane == g * GROUP, 1.0, 0.0), volt[...], HI)
-    to_r = nt(jnp.where(lane == g * GROUP + GROUP - 1, 1.0, 0.0), volt[...], HI)
-    send_1[:, T:], send_2[:, T:] = pair_order(pos, 1, to_l, to_r)
+    send_1[:, T:], send_2[:, T:] = pair_order(pos, 1, seams[0:8, :], seams[8:16, :])
 
 
 def rhs_kernel(vf, wt, at_via, zl, invd, a, z, rims, b_s):
@@ -475,7 +486,7 @@
 
 
 def base_kernel(
-    hist, pos, held, volt, cleak, col_1, col_2, row_1, row_2,
+    hist, pos, held, volt, cleak, col_1, col_2, row_1, row_2, around,
     cdiag, scale, base, r_o, c_o, ahead, sem,
 ):
     copy = pltpu.make_async_copy(hist.at[pl.ds(0, 1)], ahead, sem.at[0])
@@ -487,7 +498,10 @@
     count = nt(r_o[...], c_o[...])
     diag = 4.0 * coarse_conductance + cleak[...] + via_conductance * count
     u = volt[...]
-    near = coarse_neighbours(pos, u, row_1[:, W:], row_2[:, W:], col_1[:, T:], col_2[:, T:])
+    second = col_2[:, T:]
+    place = at(pos, 1, second)
+    second = jnp.where((place == 0) | (place == NO - 1), around[...], second)
+    near = coarse_neighbours(pos, u, row_1[:, W:], row_2[:, W:], col_1[:, T:], second)
     cdiag[...] = diag
     scale[...] = relaxation / diag
     base[...] = u - relaxation * (diag * u - coarse_conductance * near) / diag
@@ -553,10 +567,11 @@
     )(*args)
 
 
-def exchange(axis, first, second):
+def exchange(axis, first, second, wrap=False):
     n = lax.axis_size(axis)
     near = [(i, i ^ 1) for i in range(n)]
-    far = [(i, ((i + 1) ^ 1) - 1 & (n - 1)) for i in range(n)]
+    ends = (n - 1, 0) if wrap else (0, n - 1)
+    far = [(0, ends[0])] + [(i, ((i + 1) ^ 1) - 1) for i in range(1, n - 1)] + [(n - 1, ends[1])]
     return lax.ppermute(first, axis, near), lax.ppermute(second, axis, far)
 
 
@@ -583,20 +598,24 @@
     dmas = pltpu.SemaphoreType.DMA((4,))
     big = 20_000_000_000
 
-    drops, where, volt, fine = call(
+    drops, where, volt, fine, seams, around, via = call(
         parts_kernel,
-        [vmem((3 * CB, CB), BF16), hbm((2 * NO, L), jnp.int32), block, vmem((NO, L), jnp.int32)],
-        leave(coarse_init, fine),
-    )
+        [vmem((3 * CB, CB), BF16), pltpu.MemorySpace.HBM((2 * NO, L), jnp.int32), block,
+         vmem((NO, L), jnp.int32), vmem((16, CB), F32), seam,
+         pltpu.MemorySpace.HBM((T, T), F32)],
+        leave(coarse_init, fine) + keep(wt, pos), [hot, hot], flops=big,
+    )
+    last = lax.axis_size(COL) - 1
+    around = lax.ppermute(around, COL, [(0, last)] + [(i, i) for i in range(1, last)] + [(last, 0)])
     zl, invd, strips, irims = call(
         diag_kernel, [tile, tile, rim16, rim16],
-        leave(load_amp, load_mask, leak) + keep(fine, wt),
-        [hot, hot, tile, vmem((T, T), jnp.int32), tile, dmas], flops=big, any_in=3,
+        leave(load_amp, load_mask, leak, via),
+        [tile, vmem((T, T), jnp.int32), tile, tile, dmas], flops=big, any_in=4,
     )
     looked = call(lookup_kernel, [slots], keep(held, drops))[0]
     at_via = spread(looked)
     a, send_1, send_2 = call(
-        strips_kernel, [hot, side, side], keep(pos, fine, wt, at_via, strips, volt)    )
+        strips_kernel, [hot, side, side], keep(pos, fine, wt, at_via, strips, seams)    )
     col_1, col_2 = exchange(COL, send_1, send_2)
     z, zrims = call(
         rhs_kernel, [tile, rim16], keep(fine, wt, at_via, zl, invd, a), [hots], flops=big
@@ -623,13 +642,13 @@
     arrived = spread(call(pack_kernel, [vmem(*packed)], keep(g, rows))[0])
     cdiag, scale, base, r_hot, c_hot, ahead = call(
         base_kernel, [block, block, block, chot, chot, vmem((1, LT, T, L), F32)],
-        leave(hist) + keep(pos, held, volt, coarse_leak, col_1, col_2, row_1, row_2),
+        leave(hist) + keep(pos, held, volt, coarse_leak, col_1, col_2, row_1, row_2, around),
         [dmas], flops=big, any_in=1,
     )
     coef, u, src, c1, c2, r1, r2 = call(
         sweep1_kernel, [seam, block, block, seam, seam, seam, seam],
         keep(pos, arrived, scale, base, r_hot, c_hot), [vmem((CB, 2 * NO * L), BF16)]    )
-    c1, c2 = exchange(COL, c1, c2)
+    c1, c2 = exchange(COL, c1, c2, wrap=True)
     r1, r2 = exchange(ROW, r1, r2)
     fine_drop = call(
         combine_kernel, [pltpu.MemorySpace.HBM((T, T), F32)], leave(hist) + keep(ahead, coef, rims),

time: 82 us -> 85.9 us (1.048)
  starting transfers between devices: 36.4 us -> 45 us
  waiting for transfers between devices: 12.7 us -> 7.96 us
    ppermute x0 -> x1, starting transfers between devices: none -> 6.58 us  [per_device(): lax.ppermute(around, COL, [(0, last)] + [(i, i) for i in range(1, last)]...]
    all_to_all x4, waiting for transfers between devices: 11 us -> 7.94 us  [spread(): return lax.all_to_all(x, axis, split_axis=0, concat_axis=0, tiled=True)]
    ppermute x8, starting transfers between devices: 12.9 us -> 14.9 us  [exchange(): return (lax.ppermute(first, axis, near), lax.ppermute(second, axis, far))]
    ppermute x8, waiting for transfers between devices: 1.64 us -> 0.02 us  [exchange(): return (lax.ppermute(first, axis, near), lax.ppermute(second, axis, far))]
  transfers between devices with their start and end apart: 12 -> 13, of which waited for: 3 -> 2; matrix products, arithmetic and copies ran while one was open for 1% -> 1% of each run, Pallas kernels for 27% -> 32%
where the time goes in v7:
time: 85.9 us; the launch traced here: 85.3 us
  starting transfers between devices  45 us (52%)
  Pallas kernels  29.3 us (34%)
  waiting for transfers between devices  7.96 us (9%)
  other arithmetic  2.11 us (2%)
  between operations  0.86 us (1%)
    pallas_call x14, Pallas kernels, call(): pl.pallas_call(body, out_shape=outs, in_specs=specs, out_specs=[ANY] * an...  29.3 us
    all_to_all x4, starting transfers between devices, spread(): return lax.all_to_all(x, axis, split_axis=0, concat_axis=0, tiled=True)  23.5 us
    ppermute x8, starting transfers between devices, exchange(): return (lax.ppermute(first, axis, near), lax.ppermute(second, axis, far))  14.9 us
    all_to_all x4, waiting for transfers between devices, spread(): return lax.all_to_all(x, axis, split_axis=0, concat_axis=0, tiled=True)  7.94 us
    ppermute x1, starting transfers between devices, per_device(): lax.ppermute(around, COL, [(0, last)] + [(i, i) for i in range(1, last)]...  6.58 us
  transfers between devices with their start and end apart: 13, of which 2 were waited for; matrix products, arithmetic and copies ran while one was open for 1% of the time, Pallas kernels for 32%

profile of v7, /device:TPU:1, one launch (start us, length us, event | category | flops | bytes accessed | tf_op | source)
XLA Modules:
  0.0 85.3 jit_solution(3994871061790877234)
XLA Ops:
  0.6 1.4 %compare_select_fusion = s32[16,1,128]{2,1,0:T(1,128)} fusion(s32[1,2048]{1,0:T(1,128)} %param.14, s32[16]{0:T(128)} %bitcast.21), kind=kLoop, calls=%fused_computation | loop fusion | flops 12288 | bytes 16448 | tf_op jit(solution)/shard_map/jit(_where)/select_n | solution.py:590
  2.0 7.6 %all-to-all-start = ((s32[16,1,128]{2,1,0:T(1,128)}), s32[16,1,128]{2,1,0:T(1,128)S(1)}, u32[]{:S(2)}, u32[]{:S(2)}) async-start(s32[16,1,128]{2,1,0:T(1,128)} %compare_select_fusion), calls=%async_computation | async-start | bytes 16384 | tf_op jit(solution)/shard_map/all_to_all | solution.py:579
  10.4 3.5 %shard_map.95 = (bf16[384,128]{1,0:T(8,128)(2,1)S(1)}, s32[32,128]{1,0:T(8,128)}, f32[128,128]{1,0:T(8,128)S(1)}, s32[16,128]{1,0:T(8,128)S(1)}, f32[16,128]{1,0...) custom-call(f32[128,128]{1,0:T(8,128)} %volt.1, s32[16,128]{1,0:T(8,128)} %bitcast.23, f32[16,128]{1,0:T(8,128)S(1)} %fusion.wt, ...), custom_call_target="tpu_custom_call" | custom-call | flops 20000000000 | tf_op jit(solution)/shard_map/pallas_call | solution.py:559
  13.9 6.6 %collective-permute-start.4 = (f32[8,128]{1,0:T(8,128)S(1)}, f32[8,128]{1,0:T(8,128)S(1)}, u32[]{:S(2)}, u32[]{:S(2)}) collective-permute-start(f32[8,128]{1,0:T(8,128)S(1)} %get-tuple-element.55), channel_id=1, source_target_pairs={{0,15},{1,1},{2,2},{3,3},{4,4},{5,5},{6,6},{7,7},{8,8},{9,9},{10,1... | collective-permute-start | bytes 12296 | tf_op jit(solution)/shard_map/ppermute | solution.py:609
  20.5 1.2 %shard_map.96 = f32[16,128]{1,0:T(8,128)} custom-call(s32[16,128]{1,0:T(8,128)S(1)} %bitcast.16, bf16[384,128]{1,0:T(8,128)(2,1)S(1)} %get-tuple-element.39.parts), custom_call_target="tpu_custom_call" | custom-call | tf_op jit(solution)/shard_map/pallas_call | solution.py:559
  21.7 3.4 %all-to-all-start.1 = ((f32[16,1,128]{2,1,0:T(1,128)}), f32[16,1,128]{2,1,0:T(1,128)S(1)}, u32[]{:S(2)}, u32[]{:S(2)}) async-start(f32[16,1,128]{2,1,0:T(1,128)} %bitcast.5), calls=%async_computation.1 | async-start | bytes 16384 | tf_op jit(solution)/shard_map/all_to_all | solution.py:579
  25.1 3.1 %shard_map.97 = (f32[512,512]{1,0:T(8,128)S(1)}, f32[512,512]{1,0:T(8,128)S(1)}, f32[16,512]{1,0:T(8,128)S(1)}, f32[16,512]{1,0:T(8,128)S(1)}) custom-call(f32[512,512]{1,0:T(8,128)} %amp.1, s32[512,512]{1,0:T(8,128)} %mask.1, f32[512,512]{1,0:T(8,128)} %leak.1, f32[512,512]{1,0:T(8,128)} %get-tuple-element.40.via), custom_call_target="tpu_custom_call" | custom-call | flops 20000000000 | tf_op jit(solution)/shard_map/pallas_call | solution.py:559
  28.2 3.2 %all-to-all-done.1 = f32[16,1,128]{2,1,0:T(1,128)S(1)} async-done(((f32[16,1,128]{2,1,0:T(1,128)}), f32[16,1,128]{2,1,0:T(1,128)S(1)}, u32[]{:S(2)}, u32[]{:S(2)}) %all-to-all-start.1) | async-done | bytes 8224 | tf_op jit(solution)/shard_map/all_to_all | solution.py:579
  33.5 2.8 %shard_map.99 = (f32[512,512]{1,0:T(8,128)S(1)}, f32[16,512]{1,0:T(8,128)S(1)}) custom-call(s32[16,128]{1,0:T(8,128)S(1)} %get-tuple-element.38.vf, f32[16,128]{1,0:T(8,128)S(1)} %fusion.wt, f32[16,128]{1,0:T(8,128)S(1)} %bitcast.19, f32[512,512]{1,0:T(8,128)S(1)} %get-tuple-element.41.zl, f32[512,512]{1,0:T(8,128)S(1)} %get-tuple-element.42.invd, ...), custom_call_target="tpu_custom_call" | custom-call | flops 20000000000 | tf_op jit(solution)/shard_map/pallas_call | solution.py:559
  36.6 2.9 %collective-permute-start.2 = (f32[8,768]{1,0:T(8,128)S(1)}, f32[8,768]{1,0:T(8,128)S(1)}, u32[]{:S(2)}, u32[]{:S(2)}) collective-permute-start(f32[8,768]{1,0:T(8,128)S(1)} %get-tuple-element.53), channel_id=1, source_target_pairs={{0,16},{16,0},{32,48},{48,32},{64,80},{80,64},{96,112},{112,96},{1... | collective-permute-start | bytes 73736 | tf_op jit(solution)/shard_map/ppermute | solution.py:575
  39.4 3.4 %collective-permute-start.3 = (f32[8,768]{1,0:T(8,128)S(1)}, f32[8,768]{1,0:T(8,128)S(1)}, u32[]{:S(2)}, u32[]{:S(2)}) collective-permute-start(f32[8,768]{1,0:T(8,128)S(1)} %get-tuple-element.54), channel_id=1, source_target_pairs={{0,0},{16,32},{32,16},{48,64},{64,48},{80,96},{96,80},{112,112},{1... | collective-permute-start | bytes 73736 | tf_op jit(solution)/shard_map/ppermute | solution.py:575
  42.9 4.4 %shard_map.100 = (f32[4,4,512,128]{3,2,1,0:T(8,128)}, f32[64,128]{1,0:T(8,128)S(1)}) custom-call(s32[8,768]{1,0:T(8,128)S(1)} %iota.14.pos, f32[512,512]{1,0:T(8,128)S(1)} %get-tuple-element.46.z, f32[512,512]{1,0:T(8,128)S(1)} %get-tuple-element.42.invd, f32[8,640]{1,0:T(8,128)S(1)} %collective-permute-done.col_1, f32[8,640]{1,0:T(8,128)S(1)} %collective-permute-done.1.col_2), custom_call_target="tpu_custom_call" | custom-call | flops 20000000000 | tf_op jit(solution)/shard_map/pallas_call | solution.py:559
  47.3 1.1 %shard_map.103 = (f32[48,512]{1,0:T(8,128)S(1)}, f32[8,128]{1,0:T(8,128)}) custom-call(s32[8,768]{1,0:T(8,128)S(1)} %iota.14.pos, f32[512,512]{1,0:T(8,128)S(1)} %get-tuple-element.46.z, f32[512,512]{1,0:T(8,128)S(1)} %get-tuple-element.42.invd, f32[64,128]{1,0:T(8,128)S(1)} %get-tuple-element.58.corners, f32[8,768]{1,0:T(8,128)S(1)} %collective-permute-done.2.row_1, ...), custom_call_target="tpu_custom_call" | custom-call | tf_op jit(solution)/shard_map/pallas_call | solution.py:559
  48.5 5.0 %all-to-all-start.2 = ((f32[8,1,128]{2,1,0:T(1,128)}), f32[8,1,128]{2,1,0:T(1,128)S(1)}, u32[]{:S(2)}, u32[]{:S(2)}) async-start(f32[8,1,128]{2,1,0:T(1,128)} %bitcast.8), calls=%async_computation.2 | async-start | bytes 8192 | tf_op jit(solution)/shard_map/all_to_all | solution.py:579
  53.4 4.6 %shard_map.104.g = f32[128,128]{1,0:T(8,128)S(1)} custom-call(f32[4,4,512,128]{3,2,1,0:T(8,128)} %get-tuple-element.49.hist, s32[32,128]{1,0:T(8,128)} %get-tuple-element.57.table, f32[48,512]{1,0:T(8,128)S(1)} %get-tuple-element.60.rims, f32[16,128]{1,0:T(8,128)S(1)} %fusion.wt), custom_call_target="tpu_custom_call" | custom-call | flops 20000000000 | tf_op jit(solution)/shard_map/pallas_call | solution.py:559
  58.7 7.6 %all-to-all-start.3 = ((f32[16,8,128]{2,1,0:T(8,128)}), f32[16,8,128]{2,1,0:T(8,128)S(1)}, u32[]{:S(2)}, u32[]{:S(2)}) async-start(f32[16,8,128]{2,1,0:T(8,128)} %bitcast.10), calls=%async_computation.3 | async-start | bytes 131072 | tf_op jit(solution)/shard_map/all_to_all | solution.py:579
  66.3 1.7 %shard_map.102 = (f32[128,128]{1,0:T(8,128)S(1)}, f32[128,128]{1,0:T(8,128)S(1)}, f32[128,128]{1,0:T(8,128)S(1)}, bf16[128,2048]{1,0:T(8,128)(2,1)S(1)}, bf16[12...) custom-call(f32[4,4,512,128]{3,2,1,0:T(8,128)} %get-tuple-element.49.hist, s32[8,768]{1,0:T(8,128)S(1)} %iota.14.pos, ...), custom_call_target="tpu_custom_call" | custom-call | flops 20000000000 | tf_op jit(solution)/shard_map/pallas_call | solution.py:559
  68.1 4.8 %all-to-all-done.3 = f32[16,8,128]{2,1,0:T(8,128)S(1)} async-done(((f32[16,8,128]{2,1,0:T(8,128)}), f32[16,8,128]{2,1,0:T(8,128)S(1)}, u32[]{:S(2)}, u32[]{:S(2)}) %all-to-all-start.3) | async-done | bytes 65568 | tf_op jit(solution)/shard_map/all_to_all | solution.py:579
  72.8 1.3 %shard_map.106 = (f32[8,128]{1,0:T(8,128)S(1)}, f32[128,128]{1,0:T(8,128)S(1)}, f32[128,128]{1,0:T(8,128)S(1)}, f32[8,128]{1,0:T(8,128)S(1)}, f32[8,128]{1,0:T(8...) custom-call(s32[8,768]{1,0:T(8,128)S(1)} %iota.14.pos, f32[128,128]{1,0:T(8,128)S(1)} %bitcast.15, ...), custom_call_target="tpu_custom_call" | custom-call | tf_op jit(solution)/shard_map/pallas_call | solution.py:559
  74.7 1.4 %collective-permute-start.6 = (f32[8,128]{1,0:T(8,128)S(1)}, f32[8,128]{1,0:T(8,128)S(1)}, u32[]{:S(2)}, u32[]{:S(2)}) collective-permute-start(f32[8,128]{1,0:T(8,128)S(1)} %get-tuple-element.71), channel_id=1, source_target_pairs={{0,15},{1,2},{2,1},{3,4},{4,3},{5,6},{6,5},{7,8},{8,7},{9,10},{10,... | collective-permute-start | bytes 12296 | tf_op jit(solution)/shard_map/ppermute | solution.py:575
  76.1 2.6 %collective-permute-start.7 = (f32[8,128]{1,0:T(8,128)S(1)}, f32[8,128]{1,0:T(8,128)S(1)}, u32[]{:S(2)}, u32[]{:S(2)}) collective-permute-start(f32[8,128]{1,0:T(8,128)S(1)} %get-tuple-element.72), channel_id=1, source_target_pairs={{0,16},{16,0},{32,48},{48,32},{64,80},{80,64},{96,112},{112,96},{1... | collective-permute-start | bytes 12296 | tf_op jit(solution)/shard_map/ppermute | solution.py:575
  78.6 3.0 %collective-permute-start.8 = (f32[8,128]{1,0:T(8,128)S(1)}, f32[8,128]{1,0:T(8,128)S(1)}, u32[]{:S(2)}, u32[]{:S(2)}) collective-permute-start(f32[8,128]{1,0:T(8,128)S(1)} %get-tuple-element.73), channel_id=1, source_target_pairs={{0,0},{16,32},{32,16},{48,64},{64,48},{80,96},{96,80},{112,112},{1... | collective-permute-start | bytes 12296 | tf_op jit(solution)/shard_map/ppermute | solution.py:575
  81.6 2.7 %shard_map.107 = f32[512,512]{1,0:T(8,128)} custom-call(f32[4,4,512,128]{3,2,1,0:T(8,128)} %get-tuple-element.49.hist, f32[1,4,512,128]{3,2,1,0:T(8,128)S(1)} %get-tuple-element.56.ahead, f32[8,128]{1,0:T(8,128)S(1)} %get-tuple-element.66.coef, f32[48,512]{1,0:T(8,128)S(1)} %get-tuple-element.60.rims), custom_call_target="tpu_custom_call" | custom-call | flops 5000000000 | tf_op jit(solution)/shard_map/pallas_call | solution.py:559
  84.3 1.0 %shard_map.108 = f32[128,128]{1,0:T(8,128)} custom-call(s32[8,768]{1,0:T(8,128)S(1)} %iota.14.pos, f32[128,128]{1,0:T(8,128)S(1)} %get-tuple-element.67.u, f32[128,128]{1,0:T(8,128)S(1)} %get-tuple-element.68.src, f32[128,128]{1,0:T(8,128)S(1)} %get-tuple-element.69.cdiag, f32[128,128]{1,0:T(8,128)S(1)} %get-tuple-element.62.scale, ...), custom_call_target="tpu_custom_call" | custom-call | tf_op jit(solution)/shard_map/pallas_call | solution.py:559
  (22 shorter events, 4.4 us)
Async XLA Ops:
  2.0 18.5 %all-to-all-start = ((s32[16,1,128]{2,1,0:T(1,128)}), s32[16,1,128]{2,1,0:T(1,128)S(1)}, u32[]{:S(2)}, u32[]{:S(2)}) async-start(s32[16,1,128]{2,1,0:T(1,128)} %compare_select_fusion), calls=%async_computation | async-start | bytes 16384 | tf_op jit(solution)/shard_map/all_to_all | solution.py:579
  13.9 52.4 %collective-permute-start.4 = (f32[8,128]{1,0:T(8,128)S(1)}, f32[8,128]{1,0:T(8,128)S(1)}, u32[]{:S(2)}, u32[]{:S(2)}) collective-permute-start(f32[8,128]{1,0:T(8,128)S(1)} %get-tuple-element.55), channel_id=1, source_target_pairs={{0,15},{1,1},{2,2},{3,3},{4,4},{5,5},{6,6},{7,7},{8,8},{9,9},{10,1... | collective-permute-start | bytes 12296 | tf_op jit(solution)/shard_map/ppermute | solution.py:609
  21.7 9.6 %all-to-all-start.1 = ((f32[16,1,128]{2,1,0:T(1,128)}), f32[16,1,128]{2,1,0:T(1,128)S(1)}, u32[]{:S(2)}, u32[]{:S(2)}) async-start(f32[16,1,128]{2,1,0:T(1,128)} %bitcast.5), calls=%async_computation.1 | async-start | bytes 16384 | tf_op jit(solution)/shard_map/all_to_all | solution.py:579
  32.4 4.0 %collective-permute-start = (f32[8,640]{1,0:T(8,128)S(1)}, f32[8,640]{1,0:T(8,128)S(1)}, u32[]{:S(2)}, u32[]{:S(2)}) collective-permute-start(f32[8,640]{1,0:T(8,128)S(1)} %get-tuple-element.47), channel_id=1, source_target_pairs={{0,1},{1,0},{2,3},{3,2},{4,5},{5,4},{6,7},{7,6},{8,9},{9,8},{10,11... | collective-permute-start | bytes 61448 | tf_op jit(solution)/shard_map/ppermute | solution.py:575
  32.9 3.5 %collective-permute-start.1 = (f32[8,640]{1,0:T(8,128)S(1)}, f32[8,640]{1,0:T(8,128)S(1)}, u32[]{:S(2)}, u32[]{:S(2)}) collective-permute-start(f32[8,640]{1,0:T(8,128)S(1)} %get-tuple-element.48), channel_id=1, source_target_pairs={{0,0},{1,2},{2,1},{3,4},{4,3},{5,6},{6,5},{7,8},{8,7},{9,10},{10,9... | collective-permute-start | bytes 61448 | tf_op jit(solution)/shard_map/ppermute | solution.py:575
  36.6 10.7 %collective-permute-start.2 = (f32[8,768]{1,0:T(8,128)S(1)}, f32[8,768]{1,0:T(8,128)S(1)}, u32[]{:S(2)}, u32[]{:S(2)}) collective-permute-start(f32[8,768]{1,0:T(8,128)S(1)} %get-tuple-element.53), channel_id=1, source_target_pairs={{0,16},{16,0},{32,48},{48,32},{64,80},{80,64},{96,112},{112,96},{1... | collective-permute-start | bytes 73736 | tf_op jit(solution)/shard_map/ppermute | solution.py:575
  39.4 7.9 %collective-permute-start.3 = (f32[8,768]{1,0:T(8,128)S(1)}, f32[8,768]{1,0:T(8,128)S(1)}, u32[]{:S(2)}, u32[]{:S(2)}) collective-permute-start(f32[8,768]{1,0:T(8,128)S(1)} %get-tuple-element.54), channel_id=1, source_target_pairs={{0,0},{16,32},{32,16},{48,64},{64,48},{80,96},{96,80},{112,112},{1... | collective-permute-start | bytes 73736 | tf_op jit(solution)/shard_map/ppermute | solution.py:575
  48.5 9.6 %all-to-all-start.2 = ((f32[8,1,128]{2,1,0:T(1,128)}), f32[8,1,128]{2,1,0:T(1,128)S(1)}, u32[]{:S(2)}, u32[]{:S(2)}) async-start(f32[8,1,128]{2,1,0:T(1,128)} %bitcast.8), calls=%async_computation.2 | async-start | bytes 8192 | tf_op jit(solution)/shard_map/all_to_all | solution.py:579
  53.4 12.9 %copy-start = (f32[128,128]{1,0:T(8,128)S(1)}, f32[128,128]{1,0:T(8,128)}, u32[]{:S(2)}) copy-start(f32[128,128]{1,0:T(8,128)} %cleak.1) | copy-start | bytes 196612
  58.7 14.1 %all-to-all-start.3 = ((f32[16,8,128]{2,1,0:T(8,128)}), f32[16,8,128]{2,1,0:T(8,128)S(1)}, u32[]{:S(2)}, u32[]{:S(2)}) async-start(f32[16,8,128]{2,1,0:T(8,128)} %bitcast.10), calls=%async_computation.3 | async-start | bytes 131072 | tf_op jit(solution)/shard_map/all_to_all | solution.py:579
  74.2 10.1 %collective-permute-start.5 = (f32[8,128]{1,0:T(8,128)S(1)}, f32[8,128]{1,0:T(8,128)S(1)}, u32[]{:S(2)}, u32[]{:S(2)}) collective-permute-start(f32[8,128]{1,0:T(8,128)S(1)} %get-tuple-element.70), channel_id=1, source_target_pairs={{0,1},{1,0},{2,3},{3,2},{4,5},{5,4},{6,7},{7,6},{8,9},{9,8},{10,11... | collective-permute-start | bytes 12296 | tf_op jit(solution)/shard_map/ppermute | solution.py:575
  74.7 9.6 %collective-permute-start.6 = (f32[8,128]{1,0:T(8,128)S(1)}, f32[8,128]{1,0:T(8,128)S(1)}, u32[]{:S(2)}, u32[]{:S(2)}) collective-permute-start(f32[8,128]{1,0:T(8,128)S(1)} %get-tuple-element.71), channel_id=1, source_target_pairs={{0,15},{1,2},{2,1},{3,4},{4,3},{5,6},{6,5},{7,8},{8,7},{9,10},{10,... | collective-permute-start | bytes 12296 | tf_op jit(solution)/shard_map/ppermute | solution.py:575
  76.1 8.2 %collective-permute-start.7 = (f32[8,128]{1,0:T(8,128)S(1)}, f32[8,128]{1,0:T(8,128)S(1)}, u32[]{:S(2)}, u32[]{:S(2)}) collective-permute-start(f32[8,128]{1,0:T(8,128)S(1)} %get-tuple-element.72), channel_id=1, source_target_pairs={{0,16},{16,0},{32,48},{48,32},{64,80},{80,64},{96,112},{112,96},{1... | collective-permute-start | bytes 12296 | tf_op jit(solution)/shard_map/ppermute | solution.py:575
  78.6 5.7 %collective-permute-start.8 = (f32[8,128]{1,0:T(8,128)S(1)}, f32[8,128]{1,0:T(8,128)S(1)}, u32[]{:S(2)}, u32[]{:S(2)}) collective-permute-start(f32[8,128]{1,0:T(8,128)S(1)} %get-tuple-element.73), channel_id=1, source_target_pairs={{0,0},{16,32},{32,16},{48,64},{64,48},{80,96},{96,80},{112,112},{1... | collective-permute-start | bytes 12296 | tf_op jit(solution)/shard_map/ppermute | solution.py:575

commit v8 on v7

--- a/solution.py
+++ b/solution.py
@@ -104,7 +104,7 @@
     rims[8:16, :] = inv[T - 8 :]
 
 
-def parts_kernel(volt, vf, wt, pos, parts, slots, volt_o, vf_o, seams, round_o, via, a_s, b_s):
+def parts_kernel(volt, vf, wt, parts, slots, volt_o, vf_o, seams, via, a_s, b_s):
     u = volt[...]
     f = vf[...]
     volt_o[...] = u
@@ -115,11 +115,8 @@
     v2, v3 = hi_lo(rest)
     parts[...] = jnp.concatenate([v3, v2, v1], axis=0).astype(BF16)
     g, lane = iota((8, CB), 0), iota((8, CB), 1)
-    to_l = nt(jnp.where(lane == g * GROUP, 1.0, 0.0), u, HI)
-    to_r = nt(jnp.where(lane == g * GROUP + GROUP - 1, 1.0, 0.0), u, HI)
-    seams[0:8, :] = to_l
-    seams[8:16, :] = to_r
-    round_o[...] = jnp.where(at(pos, 1, to_l) == 0, to_l, to_r)
+    seams[0:8, :] = nt(jnp.where(lane == g * GROUP, 1.0, 0.0), u, HI)
+    seams[8:16, :] = nt(jnp.where(lane == g * GROUP + GROUP - 1, 1.0, 0.0), u, HI)
     for o in range(NO):
         f = vf[o : o + 1, :]
         a_s[:, lanes(o)] = onehot(f // T, T)
@@ -486,7 +483,7 @@
 
 
 def base_kernel(
-    hist, pos, held, volt, cleak, col_1, col_2, row_1, row_2, around,
+    hist, pos, held, volt, cleak, col_1, col_2, row_1, row_2,
     cdiag, scale, base, r_o, c_o, ahead, sem,
 ):
     copy = pltpu.make_async_copy(hist.at[pl.ds(0, 1)], ahead, sem.at[0])
@@ -498,10 +495,7 @@
     count = nt(r_o[...], c_o[...])
     diag = 4.0 * coarse_conductance + cleak[...] + via_conductance * count
     u = volt[...]
-    second = col_2[:, T:]
-    place = at(pos, 1, second)
-    second = jnp.where((place == 0) | (place == NO - 1), around[...], second)
-    near = coarse_neighbours(pos, u, row_1[:, W:], row_2[:, W:], col_1[:, T:], second)
+    near = coarse_neighbours(pos, u, row_1[:, W:], row_2[:, W:], col_1[:, T:], col_2[:, T:])
     cdiag[...] = diag
     scale[...] = relaxation / diag
     base[...] = u - relaxation * (diag * u - coarse_conductance * near) / diag
@@ -567,12 +561,22 @@
     )(*args)
 
 
-def exchange(axis, first, second, wrap=False):
-    n = lax.axis_size(axis)
+def exchange_columns(first, second):
+    n = lax.axis_size(COL)
     near = [(i, i ^ 1) for i in range(n)]
-    ends = (n - 1, 0) if wrap else (0, n - 1)
-    far = [(0, ends[0])] + [(i, ((i + 1) ^ 1) - 1) for i in range(1, n - 1)] + [(n - 1, ends[1])]
-    return lax.ppermute(first, axis, near), lax.ppermute(second, axis, far)
+    far = [(i, ((i + 1) ^ 1) - 1 & (n - 1)) for i in range(n)]
+    return lax.ppermute(first, COL, near), lax.ppermute(second, COL, far)
+
+
+def exchange_rows(first, second):
+    n, m = lax.axis_size(ROW), lax.axis_size(COL)
+    near = [(i, i ^ 1) for i in range(n)]
+    far = []
+    for i in range(n):
+        for k in range(m):
+            to = (i, k ^ 1) if i in (0, n - 1) else (((i + 1) ^ 1) - 1, k)
+            far.append((i * m + k, to[0] * m + to[1]))
+    return lax.ppermute(first, ROW, near), lax.ppermute(second, (ROW, COL), far)
 
 
 def spread(x, axis=COL):
@@ -598,15 +602,13 @@
     dmas = pltpu.SemaphoreType.DMA((4,))
     big = 20_000_000_000
 
-    drops, where, volt, fine, seams, around, via = call(
+    drops, where, volt, fine, seams, via = call(
         parts_kernel,
         [vmem((3 * CB, CB), BF16), pltpu.MemorySpace.HBM((2 * NO, L), jnp.int32), block,
-         vmem((NO, L), jnp.int32), vmem((16, CB), F32), seam,
+         vmem((NO, L), jnp.int32), vmem((16, CB), F32),
          pltpu.MemorySpace.HBM((T, T), F32)],
-        leave(coarse_init, fine) + keep(wt, pos), [hot, hot], flops=big,
-    )
-    last = lax.axis_size(COL) - 1
-    around = lax.ppermute(around, COL, [(0, last)] + [(i, i) for i in range(1, last)] + [(last, 0)])
+        leave(coarse_init, fine) + keep(wt), [hot, hot], flops=big,
+    )
     zl, invd, strips, irims = call(
         diag_kernel, [tile, tile, rim16, rim16],
         leave(load_amp, load_mask, leak, via),
@@ -616,7 +618,7 @@
     at_via = spread(looked)
     a, send_1, send_2 = call(
         strips_kernel, [hot, side, side], keep(pos, fine, wt, at_via, strips, seams)    )
-    col_1, col_2 = exchange(COL, send_1, send_2)
+    col_1, col_2 = exchange_columns(send_1, send_2)
     z, zrims = call(
         rhs_kernel, [tile, rim16], keep(fine, wt, at_via, zl, invd, a), [hots], flops=big
     )
@@ -624,7 +626,7 @@
     send_1, send_2, corners = call(
         edge_kernel, [rim, rim, vmem((64, L), F32)],
         keep(pos, zrims, irims, col_1, col_2, volt)    )
-    row_1, row_2 = exchange(ROW, send_1, send_2)
+    row_1, row_2 = exchange_rows(send_1, send_2)
     hist, acc = call(
         basis_kernel, [pltpu.MemorySpace.HBM((4, LT, T, L), F32), vmem((8 * SUMS, L), F32)], keep(pos, z, invd, col_1, col_2),
         [ext] * 5 + [dmas], flops=big, any_out=1,
@@ -642,14 +644,14 @@
     arrived = spread(call(pack_kernel, [vmem(*packed)], keep(g, rows))[0])
     cdiag, scale, base, r_hot, c_hot, ahead = call(
         base_kernel, [block, block, block, chot, chot, vmem((1, LT, T, L), F32)],
-        leave(hist) + keep(pos, held, volt, coarse_leak, col_1, col_2, row_1, row_2, around),
+        leave(hist) + keep(pos, held, volt, coarse_leak, col_1, col_2, row_1, row_2),
         [dmas], flops=big, any_in=1,
     )
     coef, u, src, c1, c2, r1, r2 = call(
         sweep1_kernel, [seam, block, block, seam, seam, seam, seam],
         keep(pos, arrived, scale, base, r_hot, c_hot), [vmem((CB, 2 * NO * L), BF16)]    )
-    c1, c2 = exchange(COL, c1, c2, wrap=True)
-    r1, r2 = exchange(ROW, r1, r2)
+    c1, c2 = exchange_columns(c1, c2)
+    r1, r2 = exchange_rows(r1, r2)
     fine_drop = call(
         combine_kernel, [pltpu.MemorySpace.HBM((T, T), F32)], leave(hist) + keep(ahead, coef, rims),
         [vmem((STEPS, 3, LT, T // STEPS, L), F32), tile, pltpu.SemaphoreType.DMA((STEPS,)),

time: 85.9 us -> 81.1 us (0.944)
  starting transfers between devices: 45 us -> 35.6 us
  waiting for transfers between devices: 7.96 us -> 12.7 us
    ppermute x9 -> x8, starting transfers between devices: 21.5 us -> 12.9 us  [the longest x2 6.16 us: exchange_rows(): lax.ppermute(first, ROW, near)]
    all_to_all x4, waiting for transfers between devices: 7.94 us -> 11 us  [spread(): return lax.all_to_all(x, axis, split_axis=0, concat_axis=0, tiled=True)]
    ppermute x9 -> x8, waiting for transfers between devices: 0.02 us -> 1.64 us  [the longest x4 1.63 us: exchange_columns(): return (lax.ppermute(first, COL, near), lax.ppermute(second, COL, far))]
  transfers between devices with their start and end apart: 13 -> 12, of which waited for: 2 -> 3; matrix products, arithmetic and copies ran while one was open for 1% -> 1% of each run, Pallas kernels for 32% -> 28%
where the time goes in v8:
time: 81.1 us; the launch traced here: 80.6 us
  starting transfers between devices  35.6 us (44%)
  Pallas kernels  29.3 us (36%)
  waiting for transfers between devices  12.7 us (16%)
  other arithmetic  2.12 us (3%)
  between operations  0.82 us (1%)
    pallas_call x14, Pallas kernels, call(): pl.pallas_call(body, out_shape=outs, in_specs=specs, out_specs=[ANY] * an...  29.3 us
    all_to_all x4, starting transfers between devices, spread(): return lax.all_to_all(x, axis, split_axis=0, concat_axis=0, tiled=True)  22.7 us
    all_to_all x4, waiting for transfers between devices, spread(): return lax.all_to_all(x, axis, split_axis=0, concat_axis=0, tiled=True)  11 us
    ppermute x2, starting transfers between devices, exchange_rows(): lax.ppermute(first, ROW, near)  6.16 us
    ppermute x4, starting transfers between devices, exchange_columns(): return (lax.ppermute(first, COL, near), lax.ppermute(second, COL, far))  4.09 us
    ppermute x2, starting transfers between devices, exchange_rows(): lax.ppermute(second, (ROW, COL), far)  2.68 us
    ppermute x4, waiting for transfers between devices, exchange_columns(): return (lax.ppermute(first, COL, near), lax.ppermute(second, COL, far))  1.63 us
  transfers between devices with their start and end apart: 12, of which 3 were waited for; matrix products, arithmetic and copies ran while one was open for 1% of the time, Pallas kernels for 28%

profile of v8, /device:TPU:1, one launch (start us, length us, event | category | flops | bytes accessed | tf_op | source)
XLA Modules:
  0.0 80.6 jit_solution(2242135760729444327)
XLA Ops:
  0.6 1.4 %compare_select_fusion = s32[16,1,128]{2,1,0:T(1,128)} fusion(s32[1,2048]{1,0:T(1,128)} %param.14, s32[16]{0:T(128)} %bitcast.21), kind=kLoop, calls=%fused_computation | loop fusion | flops 12288 | bytes 16448 | tf_op jit(solution)/shard_map/jit(_where)/select_n | solution.py:594
  2.0 7.6 %all-to-all-start = ((s32[16,1,128]{2,1,0:T(1,128)}), s32[16,1,128]{2,1,0:T(1,128)S(1)}, u32[]{:S(2)}, u32[]{:S(2)}) async-start(s32[16,1,128]{2,1,0:T(1,128)} %compare_select_fusion), calls=%async_computation | async-start | bytes 16384 | tf_op jit(solution)/shard_map/all_to_all | solution.py:583
  10.3 3.5 %shard_map.95 = (bf16[384,128]{1,0:T(8,128)(2,1)S(1)}, s32[32,128]{1,0:T(8,128)}, f32[128,128]{1,0:T(8,128)S(1)}, s32[16,128]{1,0:T(8,128)S(1)}, f32[16,128]{1,0:T(8,128)S(1)}, /*index=5*/f32[512,512]{1,0:T(8,128)}) custom-call(f32[128,128]{1,0:T(8,128)} %volt.1, s32[16,128]{1,0:T(8,128)} %bitcast.23, f32[16,128]{1,0:T(8,128)S(1)} %fusion.wt), custom_call_target="tpu_custom_call" | custom-call | flops 20000000000 | tf_op jit(solution)/shard_map/pallas_call | solution.py:553
  13.8 3.1 %shard_map.97 = (f32[512,512]{1,0:T(8,128)S(1)}, f32[512,512]{1,0:T(8,128)S(1)}, f32[16,512]{1,0:T(8,128)S(1)}, f32[16,512]{1,0:T(8,128)S(1)}) custom-call(f32[512,512]{1,0:T(8,128)} %amp.1, s32[512,512]{1,0:T(8,128)} %mask.1, f32[512,512]{1,0:T(8,128)} %leak.1, f32[512,512]{1,0:T(8,128)} %get-tuple-element.39.via), custom_call_target="tpu_custom_call" | custom-call | flops 20000000000 | tf_op jit(solution)/shard_map/pallas_call | solution.py:553
  16.9 1.2 %shard_map.96 = f32[16,128]{1,0:T(8,128)} custom-call(s32[16,128]{1,0:T(8,128)S(1)} %bitcast.16, bf16[384,128]{1,0:T(8,128)(2,1)S(1)} %get-tuple-element.38.parts), custom_call_target="tpu_custom_call" | custom-call | tf_op jit(solution)/shard_map/pallas_call | solution.py:553
  18.1 6.7 %all-to-all-start.1 = ((f32[16,1,128]{2,1,0:T(1,128)}), f32[16,1,128]{2,1,0:T(1,128)S(1)}, u32[]{:S(2)}, u32[]{:S(2)}) async-start(f32[16,1,128]{2,1,0:T(1,128)} %bitcast.5), calls=%async_computation.1 | async-start | bytes 16384 | tf_op jit(solution)/shard_map/all_to_all | solution.py:583
  24.8 6.3 %all-to-all-done.1 = f32[16,1,128]{2,1,0:T(1,128)S(1)} async-done(((f32[16,1,128]{2,1,0:T(1,128)}), f32[16,1,128]{2,1,0:T(1,128)S(1)}, u32[]{:S(2)}, u32[]{:S(2)}) %all-to-all-start.1) | async-done | bytes 8224 | tf_op jit(solution)/shard_map/all_to_all | solution.py:583
  32.5 1.5 %collective-permute-start.1 = (f32[8,640]{1,0:T(8,128)S(1)}, f32[8,640]{1,0:T(8,128)S(1)}, u32[]{:S(2)}, u32[]{:S(2)}) collective-permute-start(f32[8,640]{1,0:T(8,128)S(1)} %get-tuple-element.47), channel_id=1, source_target_pairs={{0,15},{1,2},{2,1},{3,4},{4,3},{5,6},{6,5},{7,8},{8,7},{9,10},{10,... | collective-permute-start | bytes 61448 | tf_op jit(solution)/shard_map/ppermute | solution.py:568
  34.1 2.8 %shard_map.99 = (f32[512,512]{1,0:T(8,128)S(1)}, f32[16,512]{1,0:T(8,128)S(1)}) custom-call(s32[16,128]{1,0:T(8,128)S(1)} %get-tuple-element.37.vf, f32[16,128]{1,0:T(8,128)S(1)} %fusion.wt, f32[16,128]{1,0:T(8,128)S(1)} %bitcast.19, f32[512,512]{1,0:T(8,128)S(1)} %get-tuple-element.40.zl, f32[512,512]{1,0:T(8,128)S(1)} %get-tuple-element.41.invd, ...), custom_call_target="tpu_custom_call" | custom-call | flops 20000000000 | tf_op jit(solution)/shard_map/pallas_call | solution.py:553
  36.9 1.6 %collective-permute-done.1.col_2 = f32[8,640]{1,0:T(8,128)S(1)} collective-permute-done((f32[8,640]{1,0:T(8,128)S(1)}, f32[8,640]{1,0:T(8,128)S(1)}, u32[]{:S(2)}, u32[]{:S(2)}) %collective-permute-start.1) | collective-permute-done | bytes 20512 | tf_op jit(solution)/shard_map/ppermute | solution.py:568
  38.7 4.2 %collective-permute-start.2 = (f32[8,768]{1,0:T(8,128)S(1)}, f32[8,768]{1,0:T(8,128)S(1)}, u32[]{:S(2)}, u32[]{:S(2)}) collective-permute-start(f32[8,768]{1,0:T(8,128)S(1)} %get-tuple-element.52), channel_id=1, source_target_pairs={{0,16},{16,0},{32,48},{48,32},{64,80},{80,64},{96,112},{112,96},{1... | collective-permute-start | bytes 73736 | tf_op jit(solution)/shard_map/ppermute | solution.py:579
  42.9 1.6 %collective-permute-start.3 = (f32[8,768]{1,0:T(8,128)S(1)}, f32[8,768]{1,0:T(8,128)S(1)}, u32[]{:S(2)}, u32[]{:S(2)}) collective-permute-start(f32[8,768]{1,0:T(8,128)S(1)} %get-tuple-element.53), channel_id=1, source_target_pairs={{0,1},{1,0},{2,3},{3,2},{4,5},{5,4},{6,7},{7,6},{8,9},{9,8},{10,11... | collective-permute-start | bytes 73736 | tf_op jit(solution)/shard_map/ppermute | solution.py:579
  44.5 4.4 %shard_map.100 = (f32[4,4,512,128]{3,2,1,0:T(8,128)}, f32[64,128]{1,0:T(8,128)S(1)}) custom-call(s32[8,768]{1,0:T(8,128)S(1)} %iota.14.pos, f32[512,512]{1,0:T(8,128)S(1)} %get-tuple-element.45.z, f32[512,512]{1,0:T(8,128)S(1)} %get-tuple-element.41.invd, f32[8,640]{1,0:T(8,128)S(1)} %collective-permute-done.col_1, f32[8,640]{1,0:T(8,128)S(1)} %collective-permute-done.1.col_2), custom_call_target="tpu_custom_call" | custom-call | flops 20000000000 | tf_op jit(solution)/shard_map/pallas_call | solution.py:553
  48.9 1.1 %shard_map.103 = (f32[48,512]{1,0:T(8,128)S(1)}, f32[8,128]{1,0:T(8,128)}) custom-call(s32[8,768]{1,0:T(8,128)S(1)} %iota.14.pos, f32[512,512]{1,0:T(8,128)S(1)} %get-tuple-element.45.z, f32[512,512]{1,0:T(8,128)S(1)} %get-tuple-element.41.invd, f32[64,128]{1,0:T(8,128)S(1)} %get-tuple-element.56.corners, f32[8,768]{1,0:T(8,128)S(1)} %collective-permute-done.2.row_1, ...), custom_call_target="tpu_custom_call" | custom-call | tf_op jit(solution)/shard_map/pallas_call | solution.py:553
  50.1 5.0 %all-to-all-start.2 = ((f32[8,1,128]{2,1,0:T(1,128)}), f32[8,1,128]{2,1,0:T(1,128)S(1)}, u32[]{:S(2)}, u32[]{:S(2)}) async-start(f32[8,1,128]{2,1,0:T(1,128)} %bitcast.8), calls=%async_computation.2 | async-start | bytes 8192 | tf_op jit(solution)/shard_map/all_to_all | solution.py:583
  55.1 4.6 %shard_map.104.g = f32[128,128]{1,0:T(8,128)S(1)} custom-call(f32[4,4,512,128]{3,2,1,0:T(8,128)} %get-tuple-element.48.hist, s32[32,128]{1,0:T(8,128)} %get-tuple-element.55.table, f32[48,512]{1,0:T(8,128)S(1)} %get-tuple-element.58.rims, f32[16,128]{1,0:T(8,128)S(1)} %fusion.wt), custom_call_target="tpu_custom_call" | custom-call | flops 20000000000 | tf_op jit(solution)/shard_map/pallas_call | solution.py:553
  60.4 3.5 %all-to-all-start.3 = ((f32[16,8,128]{2,1,0:T(8,128)}), f32[16,8,128]{2,1,0:T(8,128)S(1)}, u32[]{:S(2)}, u32[]{:S(2)}) async-start(f32[16,8,128]{2,1,0:T(8,128)} %bitcast.10), calls=%async_computation.3 | async-start | bytes 131072 | tf_op jit(solution)/shard_map/all_to_all | solution.py:583
  63.9 1.7 %shard_map.102 = (f32[128,128]{1,0:T(8,128)S(1)}, f32[128,128]{1,0:T(8,128)S(1)}, f32[128,128]{1,0:T(8,128)S(1)}, bf16[128,2048]{1,0:T(8,128)(2,1)S(1)}, bf16[12...) custom-call(f32[4,4,512,128]{3,2,1,0:T(8,128)} %get-tuple-element.48.hist, s32[8,768]{1,0:T(8,128)S(1)} %iota.14.pos, ...), custom_call_target="tpu_custom_call" | custom-call | flops 20000000000 | tf_op jit(solution)/shard_map/pallas_call | solution.py:553
  65.6 4.7 %all-to-all-done.3 = f32[16,8,128]{2,1,0:T(8,128)S(1)} async-done(((f32[16,8,128]{2,1,0:T(8,128)}), f32[16,8,128]{2,1,0:T(8,128)S(1)}, u32[]{:S(2)}, u32[]{:S(2)}) %all-to-all-start.3) | async-done | bytes 65568 | tf_op jit(solution)/shard_map/all_to_all | solution.py:583
  70.3 1.3 %shard_map.106 = (f32[8,128]{1,0:T(8,128)S(1)}, f32[128,128]{1,0:T(8,128)S(1)}, f32[128,128]{1,0:T(8,128)S(1)}, f32[8,128]{1,0:T(8,128)S(1)}, f32[8,128]{1,0:T(8...) custom-call(s32[8,768]{1,0:T(8,128)S(1)} %iota.14.pos, f32[128,128]{1,0:T(8,128)S(1)} %bitcast.15, ...), custom_call_target="tpu_custom_call" | custom-call | tf_op jit(solution)/shard_map/pallas_call | solution.py:553
  72.0 1.9 %collective-permute-start.5 = (f32[8,128]{1,0:T(8,128)S(1)}, f32[8,128]{1,0:T(8,128)S(1)}, u32[]{:S(2)}, u32[]{:S(2)}) collective-permute-start(f32[8,128]{1,0:T(8,128)S(1)} %get-tuple-element.69), channel_id=1, source_target_pairs={{0,15},{1,2},{2,1},{3,4},{4,3},{5,6},{6,5},{7,8},{8,7},{9,10},{10,... | collective-permute-start | bytes 12296 | tf_op jit(solution)/shard_map/ppermute | solution.py:568
  73.9 2.0 %collective-permute-start.6 = (f32[8,128]{1,0:T(8,128)S(1)}, f32[8,128]{1,0:T(8,128)S(1)}, u32[]{:S(2)}, u32[]{:S(2)}) collective-permute-start(f32[8,128]{1,0:T(8,128)S(1)} %get-tuple-element.70), channel_id=1, source_target_pairs={{0,16},{16,0},{32,48},{48,32},{64,80},{80,64},{96,112},{112,96},{1... | collective-permute-start | bytes 12296 | tf_op jit(solution)/shard_map/ppermute | solution.py:579
  75.8 1.1 %collective-permute-start.7 = (f32[8,128]{1,0:T(8,128)S(1)}, f32[8,128]{1,0:T(8,128)S(1)}, u32[]{:S(2)}, u32[]{:S(2)}) collective-permute-start(f32[8,128]{1,0:T(8,128)S(1)} %get-tuple-element.71), channel_id=1, source_target_pairs={{0,1},{1,0},{2,3},{3,2},{4,5},{5,4},{6,7},{7,6},{8,9},{9,8},{10,11... | collective-permute-start | bytes 12296 | tf_op jit(solution)/shard_map/ppermute | solution.py:579
  76.9 2.7 %shard_map.107 = f32[512,512]{1,0:T(8,128)} custom-call(f32[4,4,512,128]{3,2,1,0:T(8,128)} %get-tuple-element.48.hist, f32[1,4,512,128]{3,2,1,0:T(8,128)S(1)} %get-tuple-element.54.ahead, f32[8,128]{1,0:T(8,128)S(1)} %get-tuple-element.64.coef, f32[48,512]{1,0:T(8,128)S(1)} %get-tuple-element.58.rims), custom_call_target="tpu_custom_call" | custom-call | flops 5000000000 | tf_op jit(solution)/shard_map/pallas_call | solution.py:553
  (20 shorter events, 4.3 us)
Async XLA Ops:
  2.0 14.9 %all-to-all-start = ((s32[16,1,128]{2,1,0:T(1,128)}), s32[16,1,128]{2,1,0:T(1,128)S(1)}, u32[]{:S(2)}, u32[]{:S(2)}) async-start(s32[16,1,128]{2,1,0:T(1,128)} %compare_select_fusion), calls=%async_computation | async-start | bytes 16384 | tf_op jit(solution)/shard_map/all_to_all | solution.py:583
  18.1 13.0 %all-to-all-start.1 = ((f32[16,1,128]{2,1,0:T(1,128)}), f32[16,1,128]{2,1,0:T(1,128)S(1)}, u32[]{:S(2)}, u32[]{:S(2)}) async-start(f32[16,1,128]{2,1,0:T(1,128)} %bitcast.5), calls=%async_computation.1 | async-start | bytes 16384 | tf_op jit(solution)/shard_map/all_to_all | solution.py:583
  32.2 4.7 %collective-permute-start = (f32[8,640]{1,0:T(8,128)S(1)}, f32[8,640]{1,0:T(8,128)S(1)}, u32[]{:S(2)}, u32[]{:S(2)}) collective-permute-start(f32[8,640]{1,0:T(8,128)S(1)} %get-tuple-element.46), channel_id=1, source_target_pairs={{0,1},{1,0},{2,3},{3,2},{4,5},{5,4},{6,7},{7,6},{8,9},{9,8},{10,11... | collective-permute-start | bytes 61448 | tf_op jit(solution)/shard_map/ppermute | solution.py:568
  32.5 6.0 %collective-permute-start.1 = (f32[8,640]{1,0:T(8,128)S(1)}, f32[8,640]{1,0:T(8,128)S(1)}, u32[]{:S(2)}, u32[]{:S(2)}) collective-permute-start(f32[8,640]{1,0:T(8,128)S(1)} %get-tuple-element.47), channel_id=1, source_target_pairs={{0,15},{1,2},{2,1},{3,4},{4,3},{5,6},{6,5},{7,8},{8,7},{9,10},{10,... | collective-permute-start | bytes 61448 | tf_op jit(solution)/shard_map/ppermute | solution.py:568
  38.7 10.2 %collective-permute-start.2 = (f32[8,768]{1,0:T(8,128)S(1)}, f32[8,768]{1,0:T(8,128)S(1)}, u32[]{:S(2)}, u32[]{:S(2)}) collective-permute-start(f32[8,768]{1,0:T(8,128)S(1)} %get-tuple-element.52), channel_id=1, source_target_pairs={{0,16},{16,0},{32,48},{48,32},{64,80},{80,64},{96,112},{112,96},{1... | collective-permute-start | bytes 73736 | tf_op jit(solution)/shard_map/ppermute | solution.py:579
  42.9 6.0 %collective-permute-start.3 = (f32[8,768]{1,0:T(8,128)S(1)}, f32[8,768]{1,0:T(8,128)S(1)}, u32[]{:S(2)}, u32[]{:S(2)}) collective-permute-start(f32[8,768]{1,0:T(8,128)S(1)} %get-tuple-element.53), channel_id=1, source_target_pairs={{0,1},{1,0},{2,3},{3,2},{4,5},{5,4},{6,7},{7,6},{8,9},{9,8},{10,11... | collective-permute-start | bytes 73736 | tf_op jit(solution)/shard_map/ppermute | solution.py:579
  50.1 9.6 %all-to-all-start.2 = ((f32[8,1,128]{2,1,0:T(1,128)}), f32[8,1,128]{2,1,0:T(1,128)S(1)}, u32[]{:S(2)}, u32[]{:S(2)}) async-start(f32[8,1,128]{2,1,0:T(1,128)} %bitcast.8), calls=%async_computation.2 | async-start | bytes 8192 | tf_op jit(solution)/shard_map/all_to_all | solution.py:583
  55.1 8.8 %copy-start = (f32[128,128]{1,0:T(8,128)S(1)}, f32[128,128]{1,0:T(8,128)}, u32[]{:S(2)}) copy-start(f32[128,128]{1,0:T(8,128)} %cleak.1) | copy-start | bytes 196612
  60.4 10.0 %all-to-all-start.3 = ((f32[16,8,128]{2,1,0:T(8,128)}), f32[16,8,128]{2,1,0:T(8,128)S(1)}, u32[]{:S(2)}, u32[]{:S(2)}) async-start(f32[16,8,128]{2,1,0:T(8,128)} %bitcast.10), calls=%async_computation.3 | async-start | bytes 131072 | tf_op jit(solution)/shard_map/all_to_all | solution.py:583
  71.6 7.9 %collective-permute-start.4 = (f32[8,128]{1,0:T(8,128)S(1)}, f32[8,128]{1,0:T(8,128)S(1)}, u32[]{:S(2)}, u32[]{:S(2)}) collective-permute-start(f32[8,128]{1,0:T(8,128)S(1)} %get-tuple-element.68), channel_id=1, source_target_pairs={{0,1},{1,0},{2,3},{3,2},{4,5},{5,4},{6,7},{7,6},{8,9},{9,8},{10,11... | collective-permute-start | bytes 12296 | tf_op jit(solution)/shard_map/ppermute | solution.py:568
  72.0 7.6 %collective-permute-start.5 = (f32[8,128]{1,0:T(8,128)S(1)}, f32[8,128]{1,0:T(8,128)S(1)}, u32[]{:S(2)}, u32[]{:S(2)}) collective-permute-start(f32[8,128]{1,0:T(8,128)S(1)} %get-tuple-element.69), channel_id=1, source_target_pairs={{0,15},{1,2},{2,1},{3,4},{4,3},{5,6},{6,5},{7,8},{8,7},{9,10},{10,... | collective-permute-start | bytes 12296 | tf_op jit(solution)/shard_map/ppermute | solution.py:568
  73.9 5.8 %collective-permute-start.6 = (f32[8,128]{1,0:T(8,128)S(1)}, f32[8,128]{1,0:T(8,128)S(1)}, u32[]{:S(2)}, u32[]{:S(2)}) collective-permute-start(f32[8,128]{1,0:T(8,128)S(1)} %get-tuple-element.70), channel_id=1, source_target_pairs={{0,16},{16,0},{32,48},{48,32},{64,80},{80,64},{96,112},{112,96},{1... | collective-permute-start | bytes 12296 | tf_op jit(solution)/shard_map/ppermute | solution.py:579
  75.8 3.8 %collective-permute-start.7 = (f32[8,128]{1,0:T(8,128)S(1)}, f32[8,128]{1,0:T(8,128)S(1)}, u32[]{:S(2)}, u32[]{:S(2)}) collective-permute-start(f32[8,128]{1,0:T(8,128)S(1)} %get-tuple-element.71), channel_id=1, source_target_pairs={{0,1},{1,0},{2,3},{3,2},{4,5},{5,4},{6,7},{7,6},{8,9},{9,8},{10,11... | collective-permute-start | bytes 12296 | tf_op jit(solution)/shard_map/ppermute | solution.py:579

commit v9 on v8

--- a/solution.py
+++ b/solution.py
@@ -104,16 +104,15 @@
     rims[8:16, :] = inv[T - 8 :]
 
 
-def parts_kernel(volt, vf, wt, parts, slots, volt_o, vf_o, seams, via, a_s, b_s):
+def parts_kernel(volt, vf, vc, wt, node, slots, volt_o, vf_o, seams, via, a_s, b_s):
     u = volt[...]
     f = vf[...]
     volt_o[...] = u
     vf_o[...] = f
     slots[0:NO, :] = (f >> 9) * SLAB + ((f >> 7) & 3) * 4
     slots[NO:, :] = (iota((NO, L), 1) - f) & (L - 1)
-    v1, rest = hi_lo(u.T)
-    v2, v3 = hi_lo(rest)
-    parts[...] = jnp.concatenate([v3, v2, v1], axis=0).astype(BF16)
+    place = ((vc[...] >> 11) << 7) | (vc[...] & (CB - 1))
+    node[...] = jnp.where(wt[...] > 0.0, place.astype(F32), -1.0)
     g, lane = iota((8, CB), 0), iota((8, CB), 1)
     seams[0:8, :] = nt(jnp.where(lane == g * GROUP, 1.0, 0.0), u, HI)
     seams[8:16, :] = nt(jnp.where(lane == g * GROUP + GROUP - 1, 1.0, 0.0), u, HI)
@@ -124,26 +123,23 @@
     via[...] = nt(a_s[...], b_s[...])
 
 
-def lookup_kernel(held, parts, looked):
-    v = parts[...]
-    for i in range(NO // 2):
-        h = jnp.concatenate([held[2 * i : 2 * i + 1, :], held[2 * i + 1 : 2 * i + 2, :]], axis=1)
-        y = jnp.dot(v, onehot(h >> 7, CB), preferred_element_type=F32)
+def strips_kernel(pos, blocks, node, vf, wt, strips, seams, a_o, send_1, send_2, inj_o):
+    for o in range(NO):
+        at_node = node[o : o + 1, :].astype(jnp.int32)
+        v1, rest = hi_lo(blocks[o * CB : (o + 1) * CB, :])
+        v2, v3 = hi_lo(rest)
+        v = jnp.concatenate([v3, v2, v1], axis=0).astype(BF16)
+        y = jnp.dot(v, onehot(at_node & (CB - 1), CB), preferred_element_type=F32)
         y = y[:CB] + y[CB : 2 * CB] + y[2 * CB :]
-        y = jnp.where(iota((CB, 2 * L), 0) == (h & (CB - 1)), y, 0.0)
-        y = jnp.sum(y, axis=0, keepdims=True)
-        looked[2 * i : 2 * i + 1, :] = y[:, :L]
-        looked[2 * i + 1 : 2 * i + 2, :] = y[:, L:]
-
-
-def strips_kernel(pos, vf, wt, at_via, strips, seams, a_o, send_1, send_2):
+        y = jnp.where(iota((CB, L), 0) == (at_node >> 7), y, 0.0)
+        inj_o[o : o + 1, :] = jnp.sum(y, axis=0, keepdims=True) * wt[o : o + 1, :]
     j = iota((8, L), 0)
     colid = jnp.where(j < 4, j, T - 8 + j)
     hs, ls = [], []
     for o in range(NO):
         f = vf[o : o + 1, :]
         a_o[:, lanes(o)] = onehot(f // T, T)
-        hi, lo = hi_lo(at_via[o : o + 1, :] * wt[o : o + 1, :])
+        hi, lo = hi_lo(inj_o[o : o + 1, :])
         on = colid == f % T
         hs.append(jnp.where(on, hi, 0.0))
         ls.append(jnp.where(on, lo, 0.0))
@@ -160,9 +156,9 @@
     send_1[:, T:], send_2[:, T:] = pair_order(pos, 1, seams[0:8, :], seams[8:16, :])
 
 
-def rhs_kernel(vf, wt, at_via, zl, invd, a, z, rims, b_s):
-    for o in range(NO):
-        hi, lo = hi_lo(at_via[o : o + 1, :] * wt[o : o + 1, :])
+def rhs_kernel(vf, injected, zl, invd, a, z, rims, b_s):
+    for o in range(NO):
+        hi, lo = hi_lo(injected[o : o + 1, :])
         on = iota((T, L), 0) == vf[o : o + 1, :] % T
         b_s[:, lanes(o)] = jnp.where(on, hi, 0.0).astype(BF16)
         b_s[:, lanes(NO + o)] = jnp.where(on, lo, 0.0).astype(BF16)
@@ -387,11 +383,12 @@
         g_o[8 * o : 8 * o + 8, :] = jnp.where(sub < 4, acc * wt[o : o + 1, :], 0.0)
 
 
-def pack_kernel(g, rows, out):
+def pack_kernel(g, rows, node, out):
     out[...] = g[...]
     total = jnp.sum(rows[...], axis=0, keepdims=True)
     for o in range(NO):
         out[8 * o + 4 : 8 * o + 5, :] = total
+        out[8 * o + 5 : 8 * o + 6, :] = node[o : o + 1, :]
 
 
 def solve(tot):
@@ -482,27 +479,29 @@
     return near
 
 
-def base_kernel(
-    hist, pos, held, volt, cleak, col_1, col_2, row_1, row_2,
-    cdiag, scale, base, r_o, c_o, ahead, sem,
-):
+def sweep(u, src, diag, near):
+    return u + relaxation * (src - (diag * u - coarse_conductance * near)) / diag
+
+
+def base_kernel(hist, pos, volt, col_1, col_2, row_1, row_2, near, ahead, sem):
     copy = pltpu.make_async_copy(hist.at[pl.ds(0, 1)], ahead, sem.at[0])
     copy.start()
-    for o in range(NO):
-        h = held[o : o + 1, :]
-        r_o[:, lanes(o)] = onehot(h >> 7, CB)
-        c_o[:, lanes(o)] = onehot(h & (CB - 1), CB)
-    count = nt(r_o[...], c_o[...])
-    diag = 4.0 * coarse_conductance + cleak[...] + via_conductance * count
-    u = volt[...]
-    near = coarse_neighbours(pos, u, row_1[:, W:], row_2[:, W:], col_1[:, T:], col_2[:, T:])
+    near[...] = coarse_neighbours(
+        pos, volt[...], row_1[:, W:], row_2[:, W:], col_1[:, T:], col_2[:, T:]
+    )
+    copy.wait()
+
+
+def sweep1_kernel(
+    pos, arrived, volt, cleak, near, coef, u_o, src_o, cdiag, scale, c1, c2, r1, r2, r_s, c_s, v_s
+):
+    for o in range(NO):
+        h = arrived[8 * o + 5 : 8 * o + 6, :].astype(jnp.int32)
+        r_s[:, lanes(o)] = onehot(h >> 7, CB)
+        c_s[:, lanes(o)] = onehot(h & (CB - 1), CB)
+    diag = 4.0 * coarse_conductance + cleak[...] + via_conductance * nt(r_s[...], c_s[...])
     cdiag[...] = diag
     scale[...] = relaxation / diag
-    base[...] = u - relaxation * (diag * u - coarse_conductance * near) / diag
-    copy.wait()
-
-
-def sweep1_kernel(pos, arrived, scale, base, r, c, coef, u_o, src_o, c1, c2, r1, r2, v_s):
     tot = arrived[4:5, :]
     for o in range(1, NO):
         tot += arrived[8 * o + 4 : 8 * o + 5, :]
@@ -515,11 +514,11 @@
     for o in range(NO):
         v = jnp.sum(arrived[8 * o : 8 * o + 8, :] * cf, axis=0, keepdims=True)
         hi, lo = hi_lo(v)
-        on = c[:, lanes(o)]
+        on = c_s[:, lanes(o)]
         v_s[:, lanes(o)] = on * hi.astype(BF16)
         v_s[:, lanes(NO + o)] = on * lo.astype(BF16)
-    src = nt(r[...], v_s[:, : NO * L]) + nt(r[...], v_s[:, NO * L :])
-    u = base[...] + scale[...] * src
+    src = nt(r_s[...], v_s[:, : NO * L]) + nt(r_s[...], v_s[:, NO * L :])
+    u = sweep(volt[...], src, diag, near[...])
     u_o[...] = u
     src_o[...] = src
     g, gl = iota((8, CB), 0), iota((8, CB), 1)
@@ -591,9 +590,6 @@
     wt = jnp.where(live, via_conductance, 0.0).astype(F32)
     fine = via_fine.reshape(NO, L)
     coarse = via_coarse.reshape(NO, L)
-    request = jnp.where(live, ((coarse >> 11) << 7) | (coarse & (CB - 1)), -1)
-    held = spread(request)
-
     tile, block, slots = vmem((T, T), F32), vmem((CB, CB), F32), vmem((NO, L), F32)
     hot, chot = vmem((T, NO * L), BF16), vmem((CB, NO * L), BF16)
     hots = vmem((T, 2 * NO * L), BF16)
@@ -602,25 +598,26 @@
     dmas = pltpu.SemaphoreType.DMA((4,))
     big = 20_000_000_000
 
-    drops, where, volt, fine, seams, via = call(
+    blocks = jnp.broadcast_to(coarse_init[None], (NO, CB, CB)).reshape(NO * CB, CB)
+    blocks = spread(blocks)
+    node, where, volt, fine, seams, via = call(
         parts_kernel,
-        [vmem((3 * CB, CB), BF16), pltpu.MemorySpace.HBM((2 * NO, L), jnp.int32), block,
-         vmem((NO, L), jnp.int32), vmem((16, CB), F32),
-         pltpu.MemorySpace.HBM((T, T), F32)],
-        leave(coarse_init, fine) + keep(wt), [hot, hot], flops=big,
+        [slots, pltpu.MemorySpace.HBM((2 * NO, L), jnp.int32), block,
+         vmem((NO, L), jnp.int32), vmem((16, CB), F32), pltpu.MemorySpace.HBM((T, T), F32)],
+        leave(coarse_init, fine, coarse) + keep(wt), [hot, hot], flops=big,
     )
     zl, invd, strips, irims = call(
         diag_kernel, [tile, tile, rim16, rim16],
         leave(load_amp, load_mask, leak, via),
         [tile, vmem((T, T), jnp.int32), tile, tile, dmas], flops=big, any_in=4,
     )
-    looked = call(lookup_kernel, [slots], keep(held, drops))[0]
-    at_via = spread(looked)
-    a, send_1, send_2 = call(
-        strips_kernel, [hot, side, side], keep(pos, fine, wt, at_via, strips, seams)    )
+    a, send_1, send_2, injected = call(
+        strips_kernel, [hot, side, side, slots],
+        keep(pos, blocks, node, fine, wt, strips, seams),
+    )
     col_1, col_2 = exchange_columns(send_1, send_2)
     z, zrims = call(
-        rhs_kernel, [tile, rim16], keep(fine, wt, at_via, zl, invd, a), [hots], flops=big
+        rhs_kernel, [tile, rim16], keep(fine, injected, zl, invd, a), [hots], flops=big
     )
     rim = vmem((8, W + CB), F32)
     send_1, send_2, corners = call(
@@ -641,15 +638,16 @@
          pltpu.MemorySpace.SMEM((2 * NO, L), jnp.int32), pltpu.SemaphoreType.DMA((5,))],
         flops=big, any_in=2,
     )[0]
-    arrived = spread(call(pack_kernel, [vmem(*packed)], keep(g, rows))[0])
-    cdiag, scale, base, r_hot, c_hot, ahead = call(
-        base_kernel, [block, block, block, chot, chot, vmem((1, LT, T, L), F32)],
-        leave(hist) + keep(pos, held, volt, coarse_leak, col_1, col_2, row_1, row_2),
-        [dmas], flops=big, any_in=1,
-    )
-    coef, u, src, c1, c2, r1, r2 = call(
-        sweep1_kernel, [seam, block, block, seam, seam, seam, seam],
-        keep(pos, arrived, scale, base, r_hot, c_hot), [vmem((CB, 2 * NO * L), BF16)]    )
+    arrived = spread(call(pack_kernel, [vmem(*packed)], keep(g, rows, node))[0])
+    near, ahead = call(
+        base_kernel, [block, vmem((1, LT, T, L), F32)],
+        leave(hist) + keep(pos, volt, col_1, col_2, row_1, row_2), [dmas], flops=big, any_in=1,
+    )
+    coef, u, src, cdiag, scale, c1, c2, r1, r2 = call(
+        sweep1_kernel, [seam, block, block, block, block, seam, seam, seam, seam],
+        keep(pos, arrived, volt, coarse_leak, near),
+        [chot, chot, vmem((CB, 2 * NO * L), BF16)],
+    )
     c1, c2 = exchange_columns(c1, c2)
     r1, r2 = exchange_rows(r1, r2)
     fine_drop = call(

time: 81.1 us -> 76.4 us (0.942)
  starting transfers between devices: 35.6 us -> 29.6 us
  local copies, waits for them, and re-layouts: 0.07 us -> 2.01 us
  waiting for transfers between devices: 12.7 us -> 14.1 us
  other arithmetic: 2.12 us -> 0.73 us
    all_to_all x4 -> x3, starting transfers between devices: 22.7 us -> 16 us  [spread(): return lax.all_to_all(x, axis, split_axis=0, concat_axis=0, tiled=True)]
    all_to_all x4 -> x3, waiting for transfers between devices: 11 us -> 13.7 us  [spread(): return lax.all_to_all(x, axis, split_axis=0, concat_axis=0, tiled=True)]
    broadcast_in_dim x0 -> x1, local copies, waits for them, and re-layouts: none -> 1.94 us  [per_device(): jnp.broadcast_to(coarse_init[None], (NO, CB, CB)).reshape(NO * CB, CB)]
    select_n x1 -> x0, other arithmetic: 1.39 us -> none  [per_device(): request = jnp.where(live, coarse >> 11 << 7 | coarse & CB - 1, -1)]
    ppermute x4, waiting for transfers between devices: 1.63 us -> 0.43 us  [exchange_columns(): return (lax.ppermute(first, COL, near), lax.ppermute(second, COL, far))]
    ppermute x4, starting transfers between devices: 4.09 us -> 5.29 us  [exchange_columns(): return (lax.ppermute(first, COL, near), lax.ppermute(second, COL, far))]
    pallas_call x14 -> x13, Pallas kernels: 29.3 us -> 28.6 us  [call(): pl.pallas_call(body, out_shape=outs, in_specs=specs, out_specs=[ANY] * an...]
  transfers between devices with their start and end apart: 12 -> 11, of which waited for: 3 -> 3; matrix products, arithmetic and copies ran while one was open for 1% -> 1% of each run, Pallas kernels for 28% -> 30%
where the time goes in v9:
time: 76.4 us; the launch traced here: 75.9 us
  starting transfers between devices  29.6 us (39%)
  Pallas kernels  28.6 us (37%)
  waiting for transfers between devices  14.1 us (18%)
  local copies, waits for them, and re-layouts  2.01 us (3%)
  between operations  0.8 us (1%)
    pallas_call x13, Pallas kernels, call(): pl.pallas_call(body, out_shape=outs, in_specs=specs, out_specs=[ANY] * an...  28.6 us
    all_to_all x3, starting transfers between devices, spread(): return lax.all_to_all(x, axis, split_axis=0, concat_axis=0, tiled=True)  16 us
    all_to_all x3, waiting for transfers between devices, spread(): return lax.all_to_all(x, axis, split_axis=0, concat_axis=0, tiled=True)  13.7 us
    ppermute x2, starting transfers between devices, exchange_rows(): lax.ppermute(first, ROW, near)  5.63 us
    ppermute x4, starting transfers between devices, exchange_columns(): return (lax.ppermute(first, COL, near), lax.ppermute(second, COL, far))  5.29 us
    ppermute x2, starting transfers between devices, exchange_rows(): lax.ppermute(second, (ROW, COL), far)  2.64 us
    broadcast_in_dim x1, local copies, waits for them, and re-layouts, per_device(): jnp.broadcast_to(coarse_init[None], (NO, CB, CB)).reshape(NO * CB, CB)  1.94 us
  transfers between devices with their start and end apart: 11, of which 3 were waited for; matrix products, arithmetic and copies ran while one was open for 1% of the time, Pallas kernels for 30%

profile of v9, /device:TPU:1, one launch (start us, length us, event | category | flops | bytes accessed | tf_op | source)
XLA Modules:
  0.0 75.9 jit_solution(16500951538135144820)
XLA Ops:
  0.6 1.9 %broadcast_in_dim.27 = f32[16,128,128]{2,1,0:T(8,128)} broadcast(f32[128,128]{1,0:T(8,128)} %volt.1), dimensions={1,2} | broadcast | bytes 1114112 | tf_op jit(solution)/shard_map/broadcast_in_dim | solution.py:601
  2.6 7.6 %all-to-all-start = ((f32[16,128,128]{2,1,0:T(8,128)}), f32[16,128,128]{2,1,0:T(8,128)S(1)}, u32[]{:S(2)}, u32[]{:S(2)}) async-start(f32[16,128,128]{2,1,0:T(8,128)} %broadcast_in_dim.27), calls=%async_computation | async-start | bytes 2097152 | tf_op jit(solution)/shard_map/all_to_all | solution.py:582
  10.1 0.7 fusion.wt
  10.9 3.5 %shard_map.95 = (f32[16,128]{1,0:T(8,128)S(1)}, s32[32,128]{1,0:T(8,128)}, f32[128,128]{1,0:T(8,128)S(1)}, s32[16,128]{1,0:T(8,128)S(1)}, f32[16,128]{1,0:T(8,128)S(1)}, /*index=5*/f32[512,512]{1,0:T(8,128)}) custom-call(f32[128,128]{1,0:T(8,128)} %volt.1, s32[16,128]{1,0:T(8,128)} %bitcast.14, s32[16,128]{1,0:T(8,128)} %bitcast.15, f32[16,128]{1,0:T(8,128)S(1)} %fusion.wt), custom_call_target="tpu_custom_call" | custom-call | flops 20000000000 | tf_op jit(solution)/shard_map/pallas_call | solution.py:552
  14.4 3.1 %shard_map.96 = (f32[512,512]{1,0:T(8,128)S(1)}, f32[512,512]{1,0:T(8,128)S(1)}, f32[16,512]{1,0:T(8,128)S(1)}, f32[16,512]{1,0:T(8,128)S(1)}) custom-call(f32[512,512]{1,0:T(8,128)} %amp.1, s32[512,512]{1,0:T(8,128)} %mask.1, f32[512,512]{1,0:T(8,128)} %leak.1, f32[512,512]{1,0:T(8,128)} %get-tuple-element.38.via), custom_call_target="tpu_custom_call" | custom-call | flops 20000000000 | tf_op jit(solution)/shard_map/pallas_call | solution.py:552
  17.5 8.7 %all-to-all-done = f32[16,128,128]{2,1,0:T(8,128)S(1)} async-done(((f32[16,128,128]{2,1,0:T(8,128)}), f32[16,128,128]{2,1,0:T(8,128)S(1)}, u32[]{:S(2)}, u32[]{:S(2)}) %all-to-all-start) | async-done | bytes 1048608 | tf_op jit(solution)/shard_map/all_to_all | solution.py:582
  26.3 1.6 %shard_map.97 = (bf16[512,2048]{1,0:T(8,128)(2,1)S(1)}, f32[8,640]{1,0:T(8,128)S(1)}, f32[8,640]{1,0:T(8,128)S(1)}, f32[16,128]{1,0:T(8,128)S(1)}) custom-call(s32[8,768]{1,0:T(8,128)S(1)} %iota.11.pos, f32[2048,128]{1,0:T(8,128)S(1)} %bitcast.10, f32[16,128]{1,0:T(8,128)S(1)} %get-tuple-element.37.node, s32[16,128]{1,0:T(8,128)S(1)} %get-tuple-element.36.vf, ...), custom_call_target="tpu_custom_call" | custom-call | tf_op jit(solution)/shard_map/pallas_call | solution.py:552
  28.2 2.7 %collective-permute-start.1 = (f32[8,640]{1,0:T(8,128)S(1)}, f32[8,640]{1,0:T(8,128)S(1)}, u32[]{:S(2)}, u32[]{:S(2)}) collective-permute-start(f32[8,640]{1,0:T(8,128)S(1)} %get-tuple-element.47), channel_id=1, source_target_pairs={{0,15},{1,2},{2,1},{3,4},{4,3},{5,6},{6,5},{7,8},{8,7},{9,10},{10,... | collective-permute-start | bytes 61448 | tf_op jit(solution)/shard_map/ppermute | solution.py:567
  30.9 2.8 %shard_map.98 = (f32[512,512]{1,0:T(8,128)S(1)}, f32[16,512]{1,0:T(8,128)S(1)}) custom-call(s32[16,128]{1,0:T(8,128)S(1)} %get-tuple-element.36.vf, f32[16,128]{1,0:T(8,128)S(1)} %get-tuple-element.41.injected, f32[512,512]{1,0:T(8,128)S(1)} %get-tuple-element.42.zl, f32[512,512]{1,0:T(8,128)S(1)} %get-tuple-element.43.invd, ...), custom_call_target="tpu_custom_call" | custom-call | flops 20000000000 | tf_op jit(solution)/shard_map/pallas_call | solution.py:552
  34.3 3.6 %collective-permute-start.2 = (f32[8,768]{1,0:T(8,128)S(1)}, f32[8,768]{1,0:T(8,128)S(1)}, u32[]{:S(2)}, u32[]{:S(2)}) collective-permute-start(f32[8,768]{1,0:T(8,128)S(1)} %get-tuple-element.52), channel_id=1, source_target_pairs={{0,16},{16,0},{32,48},{48,32},{64,80},{80,64},{96,112},{112,96},{1... | collective-permute-start | bytes 73736 | tf_op jit(solution)/shard_map/ppermute | solution.py:578
  38.0 1.6 %collective-permute-start.3 = (f32[8,768]{1,0:T(8,128)S(1)}, f32[8,768]{1,0:T(8,128)S(1)}, u32[]{:S(2)}, u32[]{:S(2)}) collective-permute-start(f32[8,768]{1,0:T(8,128)S(1)} %get-tuple-element.53), channel_id=1, source_target_pairs={{0,1},{1,0},{2,3},{3,2},{4,5},{5,4},{6,7},{7,6},{8,9},{9,8},{10,11... | collective-permute-start | bytes 73736 | tf_op jit(solution)/shard_map/ppermute | solution.py:578
  39.6 4.4 %shard_map.99 = (f32[4,4,512,128]{3,2,1,0:T(8,128)}, f32[64,128]{1,0:T(8,128)S(1)}) custom-call(s32[8,768]{1,0:T(8,128)S(1)} %iota.11.pos, f32[512,512]{1,0:T(8,128)S(1)} %get-tuple-element.45.z, f32[512,512]{1,0:T(8,128)S(1)} %get-tuple-element.43.invd, f32[8,640]{1,0:T(8,128)S(1)} %collective-permute-done.col_1, f32[8,640]{1,0:T(8,128)S(1)} %collective-permute-done.1.col_2), custom_call_target="tpu_custom_call" | custom-call | flops 20000000000 | tf_op jit(solution)/shard_map/pallas_call | solution.py:552
  44.0 1.1 %shard_map.102 = (f32[48,512]{1,0:T(8,128)S(1)}, f32[8,128]{1,0:T(8,128)}) custom-call(s32[8,768]{1,0:T(8,128)S(1)} %iota.11.pos, f32[512,512]{1,0:T(8,128)S(1)} %get-tuple-element.45.z, f32[512,512]{1,0:T(8,128)S(1)} %get-tuple-element.43.invd, f32[64,128]{1,0:T(8,128)S(1)} %get-tuple-element.56.corners, f32[8,768]{1,0:T(8,128)S(1)} %collective-permute-done.2.row_1, ...), custom_call_target="tpu_custom_call" | custom-call | tf_op jit(solution)/shard_map/pallas_call | solution.py:552
  45.1 5.0 %all-to-all-start.1 = ((f32[8,1,128]{2,1,0:T(1,128)}), f32[8,1,128]{2,1,0:T(1,128)S(1)}, u32[]{:S(2)}, u32[]{:S(2)}) async-start(f32[8,1,128]{2,1,0:T(1,128)} %bitcast.5), calls=%async_computation.1 | async-start | bytes 8192 | tf_op jit(solution)/shard_map/all_to_all | solution.py:582
  50.1 4.6 %shard_map.103.g = f32[128,128]{1,0:T(8,128)S(1)} custom-call(f32[4,4,512,128]{3,2,1,0:T(8,128)} %get-tuple-element.48.hist, s32[32,128]{1,0:T(8,128)} %get-tuple-element.55.table, f32[48,512]{1,0:T(8,128)S(1)} %get-tuple-element.58.rims, f32[16,128]{1,0:T(8,128)S(1)} %fusion.wt), custom_call_target="tpu_custom_call" | custom-call | flops 20000000000 | tf_op jit(solution)/shard_map/pallas_call | solution.py:552
  55.4 3.5 %all-to-all-start.2 = ((f32[16,8,128]{2,1,0:T(8,128)}), f32[16,8,128]{2,1,0:T(8,128)S(1)}, u32[]{:S(2)}, u32[]{:S(2)}) async-start(f32[16,8,128]{2,1,0:T(8,128)} %bitcast.7), calls=%async_computation.2 | async-start | bytes 131072 | tf_op jit(solution)/shard_map/all_to_all | solution.py:582
  58.9 1.5 %shard_map.101 = (f32[128,128]{1,0:T(8,128)S(1)}, f32[1,4,512,128]{3,2,1,0:T(8,128)S(1)}) custom-call(f32[4,4,512,128]{3,2,1,0:T(8,128)} %get-tuple-element.48.hist, s32[8,768]{1,0:T(8,128)S(1)} %iota.11.pos, f32[128,128]{1,0:T(8,128)S(1)} %get-tuple-element.49.volt, f32[8,640]{1,0:T(8,128)S(1)} %collective-permute-done.col_1, ...), custom_call_target="tpu_custom_call" | custom-call | flops 20000000000 | tf_op jit(solution)/shard_map/pallas_call | solution.py:552
  60.4 5.0 %all-to-all-done.2 = f32[16,8,128]{2,1,0:T(8,128)S(1)} async-done(((f32[16,8,128]{2,1,0:T(8,128)}), f32[16,8,128]{2,1,0:T(8,128)S(1)}, u32[]{:S(2)}, u32[]{:S(2)}) %all-to-all-start.2) | async-done | bytes 65568 | tf_op jit(solution)/shard_map/all_to_all | solution.py:582
  65.3 1.6 %shard_map.105 = (f32[8,128]{1,0:T(8,128)S(1)}, f32[128,128]{1,0:T(8,128)S(1)}, f32[128,128]{1,0:T(8,128)S(1)}, f32[128,128]{1,0:T(8,128)S(1)}, f32[128,128]{1,0...) custom-call(s32[8,768]{1,0:T(8,128)S(1)} %iota.11.pos, ...), custom_call_target="tpu_custom_call" | custom-call | tf_op jit(solution)/shard_map/pallas_call | solution.py:552
  67.3 1.9 %collective-permute-start.5 = (f32[8,128]{1,0:T(8,128)S(1)}, f32[8,128]{1,0:T(8,128)S(1)}, u32[]{:S(2)}, u32[]{:S(2)}) collective-permute-start(f32[8,128]{1,0:T(8,128)S(1)} %get-tuple-element.67), channel_id=1, source_target_pairs={{0,15},{1,2},{2,1},{3,4},{4,3},{5,6},{6,5},{7,8},{8,7},{9,10},{10,... | collective-permute-start | bytes 12296 | tf_op jit(solution)/shard_map/ppermute | solution.py:567
  69.1 2.0 %collective-permute-start.6 = (f32[8,128]{1,0:T(8,128)S(1)}, f32[8,128]{1,0:T(8,128)S(1)}, u32[]{:S(2)}, u32[]{:S(2)}) collective-permute-start(f32[8,128]{1,0:T(8,128)S(1)} %get-tuple-element.68), channel_id=1, source_target_pairs={{0,16},{16,0},{32,48},{48,32},{64,80},{80,64},{96,112},{112,96},{1... | collective-permute-start | bytes 12296 | tf_op jit(solution)/shard_map/ppermute | solution.py:578
  71.2 1.0 %collective-permute-start.7 = (f32[8,128]{1,0:T(8,128)S(1)}, f32[8,128]{1,0:T(8,128)S(1)}, u32[]{:S(2)}, u32[]{:S(2)}) collective-permute-start(f32[8,128]{1,0:T(8,128)S(1)} %get-tuple-element.69), channel_id=1, source_target_pairs={{0,1},{1,0},{2,3},{3,2},{4,5},{5,4},{6,7},{7,6},{8,9},{9,8},{10,11... | collective-permute-start | bytes 12296 | tf_op jit(solution)/shard_map/ppermute | solution.py:578
  72.2 2.7 %shard_map.106 = f32[512,512]{1,0:T(8,128)} custom-call(f32[4,4,512,128]{3,2,1,0:T(8,128)} %get-tuple-element.48.hist, f32[1,4,512,128]{3,2,1,0:T(8,128)S(1)} %get-tuple-element.54.ahead, f32[8,128]{1,0:T(8,128)S(1)} %get-tuple-element.61.coef, f32[48,512]{1,0:T(8,128)S(1)} %get-tuple-element.58.rims), custom_call_target="tpu_custom_call" | custom-call | flops 5000000000 | tf_op jit(solution)/shard_map/pallas_call | solution.py:552
  74.9 1.0 %shard_map.107 = f32[128,128]{1,0:T(8,128)} custom-call(s32[8,768]{1,0:T(8,128)S(1)} %iota.11.pos, f32[128,128]{1,0:T(8,128)S(1)} %get-tuple-element.62.u, f32[128,128]{1,0:T(8,128)S(1)} %get-tuple-element.63.src, f32[128,128]{1,0:T(8,128)S(1)} %get-tuple-element.64.cdiag, f32[128,128]{1,0:T(8,128)S(1)} %get-tuple-element.65.scale, ...), custom_call_target="tpu_custom_call" | custom-call | tf_op jit(solution)/shard_map/pallas_call | solution.py:552
  (17 shorter events, 2.1 us)
Async XLA Ops:
  2.6 23.6 %all-to-all-start = ((f32[16,128,128]{2,1,0:T(8,128)}), f32[16,128,128]{2,1,0:T(8,128)S(1)}, u32[]{:S(2)}, u32[]{:S(2)}) async-start(f32[16,128,128]{2,1,0:T(8,128)} %broadcast_in_dim.27), calls=%async_computation | async-start | bytes 2097152 | tf_op jit(solution)/shard_map/all_to_all | solution.py:582
  27.8 5.9 %collective-permute-start = (f32[8,640]{1,0:T(8,128)S(1)}, f32[8,640]{1,0:T(8,128)S(1)}, u32[]{:S(2)}, u32[]{:S(2)}) collective-permute-start(f32[8,640]{1,0:T(8,128)S(1)} %get-tuple-element.46), channel_id=1, source_target_pairs={{0,1},{1,0},{2,3},{3,2},{4,5},{5,4},{6,7},{7,6},{8,9},{9,8},{10,11... | collective-permute-start | bytes 61448 | tf_op jit(solution)/shard_map/ppermute | solution.py:567
  28.2 6.0 %collective-permute-start.1 = (f32[8,640]{1,0:T(8,128)S(1)}, f32[8,640]{1,0:T(8,128)S(1)}, u32[]{:S(2)}, u32[]{:S(2)}) collective-permute-start(f32[8,640]{1,0:T(8,128)S(1)} %get-tuple-element.47), channel_id=1, source_target_pairs={{0,15},{1,2},{2,1},{3,4},{4,3},{5,6},{6,5},{7,8},{8,7},{9,10},{10,... | collective-permute-start | bytes 61448 | tf_op jit(solution)/shard_map/ppermute | solution.py:567
  34.3 9.6 %collective-permute-start.2 = (f32[8,768]{1,0:T(8,128)S(1)}, f32[8,768]{1,0:T(8,128)S(1)}, u32[]{:S(2)}, u32[]{:S(2)}) collective-permute-start(f32[8,768]{1,0:T(8,128)S(1)} %get-tuple-element.52), channel_id=1, source_target_pairs={{0,16},{16,0},{32,48},{48,32},{64,80},{80,64},{96,112},{112,96},{1... | collective-permute-start | bytes 73736 | tf_op jit(solution)/shard_map/ppermute | solution.py:578
  38.0 6.0 %collective-permute-start.3 = (f32[8,768]{1,0:T(8,128)S(1)}, f32[8,768]{1,0:T(8,128)S(1)}, u32[]{:S(2)}, u32[]{:S(2)}) collective-permute-start(f32[8,768]{1,0:T(8,128)S(1)} %get-tuple-element.53), channel_id=1, source_target_pairs={{0,1},{1,0},{2,3},{3,2},{4,5},{5,4},{6,7},{7,6},{8,9},{9,8},{10,11... | collective-permute-start | bytes 73736 | tf_op jit(solution)/shard_map/ppermute | solution.py:578
  45.1 9.6 %all-to-all-start.1 = ((f32[8,1,128]{2,1,0:T(1,128)}), f32[8,1,128]{2,1,0:T(1,128)S(1)}, u32[]{:S(2)}, u32[]{:S(2)}) async-start(f32[8,1,128]{2,1,0:T(1,128)} %bitcast.5), calls=%async_computation.1 | async-start | bytes 8192 | tf_op jit(solution)/shard_map/all_to_all | solution.py:582
  55.4 10.0 %all-to-all-start.2 = ((f32[16,8,128]{2,1,0:T(8,128)}), f32[16,8,128]{2,1,0:T(8,128)S(1)}, u32[]{:S(2)}, u32[]{:S(2)}) async-start(f32[16,8,128]{2,1,0:T(8,128)} %bitcast.7), calls=%async_computation.2 | async-start | bytes 131072 | tf_op jit(solution)/shard_map/all_to_all | solution.py:582
  58.9 6.5 %copy-start = (f32[128,128]{1,0:T(8,128)S(1)}, f32[128,128]{1,0:T(8,128)}, u32[]{:S(2)}) copy-start(f32[128,128]{1,0:T(8,128)} %cleak.1) | copy-start | bytes 196612
  66.9 7.9 %collective-permute-start.4 = (f32[8,128]{1,0:T(8,128)S(1)}, f32[8,128]{1,0:T(8,128)S(1)}, u32[]{:S(2)}, u32[]{:S(2)}) collective-permute-start(f32[8,128]{1,0:T(8,128)S(1)} %get-tuple-element.66), channel_id=1, source_target_pairs={{0,1},{1,0},{2,3},{3,2},{4,5},{5,4},{6,7},{7,6},{8,9},{9,8},{10,11... | collective-permute-start | bytes 12296 | tf_op jit(solution)/shard_map/ppermute | solution.py:567
  67.3 7.6 %collective-permute-start.5 = (f32[8,128]{1,0:T(8,128)S(1)}, f32[8,128]{1,0:T(8,128)S(1)}, u32[]{:S(2)}, u32[]{:S(2)}) collective-permute-start(f32[8,128]{1,0:T(8,128)S(1)} %get-tuple-element.67), channel_id=1, source_target_pairs={{0,15},{1,2},{2,1},{3,4},{4,3},{5,6},{6,5},{7,8},{8,7},{9,10},{10,... | collective-permute-start | bytes 12296 | tf_op jit(solution)/shard_map/ppermute | solution.py:567
  69.1 5.7 %collective-permute-start.6 = (f32[8,128]{1,0:T(8,128)S(1)}, f32[8,128]{1,0:T(8,128)S(1)}, u32[]{:S(2)}, u32[]{:S(2)}) collective-permute-start(f32[8,128]{1,0:T(8,128)S(1)} %get-tuple-element.68), channel_id=1, source_target_pairs={{0,16},{16,0},{32,48},{48,32},{64,80},{80,64},{96,112},{112,96},{1... | collective-permute-start | bytes 12296 | tf_op jit(solution)/shard_map/ppermute | solution.py:578
  71.2 3.7 %collective-permute-start.7 = (f32[8,128]{1,0:T(8,128)S(1)}, f32[8,128]{1,0:T(8,128)S(1)}, u32[]{:S(2)}, u32[]{:S(2)}) collective-permute-start(f32[8,128]{1,0:T(8,128)S(1)} %get-tuple-element.69), channel_id=1, source_target_pairs={{0,1},{1,0},{2,3},{3,2},{4,5},{5,4},{6,7},{7,6},{8,9},{9,8},{10,11... | collective-permute-start | bytes 12296 | tf_op jit(solution)/shard_map/ppermute | solution.py:578
